TPU v7x, 128 devices: a whole 4x4x4 slice. The times are simulated.
128 devices in a mesh: seq: 32 (over x, z, y_lo), doc: 4 (over y_hi, core).
Axes of the slice: x: 4, y: 4 (y_hi: 2, y_lo: 2; y = y_hi * 2 + y_lo), z: 4, core: 2. Of those that a mesh axis runs over, the one named last changes fastest.
Arguments:
- queries: bfloat16 [65536, 4096], P(('doc', 'seq')), parts along dimension 0, may hold values from -24 to 24
- keys: bfloat16 [65536, 4096], P(('doc', 'seq')), parts along dimension 0, may hold values from -24 to 24
- values: bfloat16 [65536, 4096], P(('doc', 'seq')), parts along dimension 0, may hold values from -6 to 6
Outputs:
- attended: bfloat16 [65536, 4096], P(('doc', 'seq')), parts along dimension 0
There are 4 independent parts, one for each index of `doc`. A program takes and returns all parts, laid end to end along the dimension named above; each array names one. Nothing has to cross between parts.
All inputs are finite; a program needn't handle non-finite values. Where the computation divides by a largest or mean magnitude, that divisor is 1e-20 or more.
Results may differ from a plain program's by a relative error of at most 0.04.
Values may be sent and summed in bfloat16 or wider, within the bound.
No kernel may reach another device: no remote copies, remote signals or barrier semaphores. Data moves between devices by JAX's collectives and lax.ppermute only.
A program may use at most 192 MiB of HBM per device.

v0:
```python
import math

import jax
import jax.numpy as jnp
from jax import lax
from jax.sharding import Mesh
from jax.sharding import PartitionSpec as P

H = 32
DH = 128
M = 512
ITERS = 6
D = 4096
SEQ = ("seq_0", "seq_1", "seq_2")
DOC_SEQ = ("doc", "seq_0", "seq_1", "seq_2")


def side_by_side(arrays, axis, dim, along):
    widths = [a.shape[along] for a in arrays]
    both = jnp.concatenate(arrays, axis=along)
    filled = lax.all_gather(both, axis, axis=dim, tiled=True)
    return tuple(jnp.split(filled, [sum(widths[:k]) for k in range(1, len(widths))], axis=along))


def copy_for_each(shard, axis):
    copies = jnp.broadcast_to(shard, (lax.axis_size(axis), *shard.shape))
    return lax.all_to_all(copies, axis, split_axis=0, concat_axis=0, tiled=True)


def of_everyone(shard, axis):
    everything = copy_for_each(shard, axis)
    return jnp.max(everything, axis=0)


def in_one_piece(arrays, axis, dim, along):
    widths = [math.prod(a.shape[along:]) for a in arrays]
    both = jnp.concatenate(
        [a.reshape(*a.shape[:along], w) for a, w in zip(arrays, widths)], axis=along
    )
    filled = lax.psum_scatter(both, axis, scatter_dimension=dim, tiled=True)
    parts = jnp.split(filled, [sum(widths[:k]) for k in range(1, len(widths))], axis=along)
    return tuple(
        (b.reshape(*filled.shape[:along], *a.shape[along:]) for a, b in zip(arrays, parts))
    )


def joined_along(parts, dim):
    parts = jnp.moveaxis(parts, 0, dim)
    dims = parts.shape
    return parts.reshape(*dims[:dim], dims[dim] * dims[dim + 1], *dims[dim + 2 :])


def gather_in_order(shard, axes, sequence):
    parts = shard
    for k in sequence:
        parts = lax.all_gather(parts, axes[k])
    done = sequence[::-1]
    back = [done.index(k) for k in range(len(axes))]
    parts = parts.transpose(*back, *range(len(axes), parts.ndim))
    return parts.reshape(-1, *shard.shape)


def gathered_by_axis(shard, axes, sequence, dim):
    return joined_along(gather_in_order(shard, axes, sequence), dim)


def softmax_last(scores):
    top = jnp.max(scores, -1, keepdims=True)
    exponent_values = jnp.exp(scores - top)
    return exponent_values / jnp.sum(exponent_values, -1, keepdims=True)


def newton_schulz(kernel):
    row_most = jnp.max(jnp.sum(jnp.abs(kernel), 2), 1)
    col_most = jnp.max(jnp.sum(jnp.abs(kernel), 1), 1)
    inverse = jnp.swapaxes(kernel, 1, 2) / (row_most * col_most)[:, None, None]
    identity = jnp.eye(kernel.shape[1], dtype=jnp.float32)[None]
    for sweep in range(ITERS):
        kernel_inv = jnp.einsum("hij,hjk->hik", kernel, inverse)
        inner = jnp.einsum("hij,hjk->hik", kernel_inv, 7.0 * identity - kernel_inv)
        middle = jnp.einsum("hij,hjk->hik", kernel_inv, 15.0 * identity - inner)
        inverse = 0.25 * jnp.einsum("hij,hjk->hik", inverse, 13.0 * identity - middle)
    return inverse


def body(queries, keys, values):
    devices = lax.axis_size(SEQ)
    position = lax.axis_index(SEQ)
    tokens_here = queries.shape[0]
    per_device = M // devices
    segment = tokens_here // per_device
    owned = H // devices
    score_scale = DH ** (-0.5)
    local_q = (
        jnp.sum(queries.reshape(per_device, segment, D), axis=1, dtype=jnp.float32) / segment
    ).astype(jnp.bfloat16)
    local_k = (
        jnp.sum(keys.reshape(per_device, segment, D), axis=1, dtype=jnp.float32) / segment
    ).astype(jnp.bfloat16)
    land_q, land_k = side_by_side((local_q, local_k), SEQ, 0, 1)
    query_landmark_means = land_q.reshape(M, H, DH)
    key_landmark_means = land_k.reshape(M, H, DH)
    query_heads_split = queries.reshape(tokens_here, H, DH)
    key_heads_split = keys.reshape(tokens_here, H, DH)
    value_heads_split = values.reshape(tokens_here, H, DH)
    start = position * owned
    local_query_block = lax.dynamic_slice_in_dim(query_landmark_means, start, owned, 1)
    local_key_block = lax.dynamic_slice_in_dim(key_landmark_means, start, owned, 1)
    kernel = softmax_last(
        jnp.einsum(
            "aft,eft->fae", local_query_block, local_key_block, preferred_element_type=jnp.float32
        )
        * score_scale
    )
    inverse = newton_schulz(kernel).astype(jnp.bfloat16)
    scores = (
        jnp.einsum(
            "luv,xuv->ulx",
            query_landmark_means,
            key_heads_split,
            preferred_element_type=jnp.float32,
        )
        * score_scale
    )
    local_peak = jnp.max(scores, -1)
    peak = of_everyone(local_peak.astype(jnp.bfloat16), SEQ).astype(local_peak.dtype)
    exponent_values = jnp.exp(scores - peak[..., None])
    totals = jnp.sum(exponent_values, -1)
    weighted = jnp.einsum(
        "fta,afr->ftr",
        exponent_values.astype(jnp.bfloat16),
        value_heads_split,
        preferred_element_type=jnp.float32,
    )
    totals, weighted = (totals, weighted)
    totals, weighted = tuple(
        (
            part.astype(jnp.float32)
            for part in in_one_piece(
                (totals.astype(jnp.bfloat16), weighted.astype(jnp.bfloat16)), SEQ, 0, 2
            )
        )
    )
    mine = (weighted / totals[..., None]).astype(jnp.bfloat16)
    own_product = jnp.einsum(
        "yco,yor->ycr", inverse, mine, preferred_element_type=jnp.float32
    ).astype(jnp.bfloat16)
    attention_product = gathered_by_axis(own_product, SEQ, (2, 0, 1), 0)
    near = (
        jnp.einsum(
            "ivb,avb->via",
            query_heads_split,
            key_landmark_means,
            preferred_element_type=jnp.float32,
        )
        * score_scale
    )
    attention_weight = softmax_last(near).astype(jnp.bfloat16)
    result = jnp.einsum(
        "vcn,vnl->cvl", attention_weight, attention_product, preferred_element_type=jnp.float32
    ).astype(jnp.bfloat16)
    return result.reshape(tokens_here, D)


def solution(mesh):
    torus = Mesh(
        mesh.devices.reshape(4, 4, 2, mesh.shape["doc"]), ("seq_0", "seq_1", "seq_2", "doc")
    )
    in_specs = (P(DOC_SEQ, None), P(DOC_SEQ, None), P(DOC_SEQ, None))
    out_specs = P(DOC_SEQ, None)
    return jax.shard_map(body, mesh=torus, in_specs=in_specs, out_specs=out_specs, check_vma=False)
```

profile of v0, /device:TPU:0, one launch (start us, length us, event | category | flops | bytes accessed | tf_op | source)
XLA Modules:
  0.0 583.9 jit_solution(1902278482105150710)
XLA Ops:
  6.5 3.5 convert_reduce_fusion
  10.0 1.1 convert_reduce_fusion.1
  11.2 0.7 pad_maximum_fusion.1
  11.9 191.9 %all-gather.7.cloned.1.call-done = bf16[512,8192]{1,0:T(8,128)(2,1)} async-done(((bf16[16,8192]{1,0:T(8,128)(2,1)}), bf16[512,8192]{1,0:T(8,128)(2,1)}) %all-gather.7.cloned.1.call-update) | async-done | bytes 8388624 | tf_op jit(solution)/shard_map/all_gather | solution.py:21
  203.8 6.1 %fusion.114 = (bf16[512,4096]{1,0:T(8,128)(2,1)}, bf16[512,4096]{1,0:T(8,128)(2,1)}) fusion(bf16[512,8192]{1,0:T(8,128)(2,1)} %all-gather.7.cloned.1.call-done), kind=kLoop, calls=%fused_computation.128 | loop fusion | bytes 16777216 | tf_op jit(solution)/shard_map/split | solution.py:22
  209.9 6.4 %copy.62 = bf16[512,4096]{0,1:T(8,128)(2,1)} copy(bf16[512,4096]{1,0:T(8,128)(2,1)} %get-tuple-element.7) | data formatting | bytes 8388608
  216.3 15.9 %multiply_reduce_fusion = (bf16[32,512]{1,0:T(8,128)(2,1)S(1)}, f32[32,512,512]{1,2,0:T(8,128)}) fusion(bf16[512,32,128]{0,2,1:T(8,128)(2,1)} %bitcast.103, bf16[512,4096]{1,0:T(8,128)(2,1)} %param.4), kind=kOutput, calls=%fused_computation.7 | convolution fusion | flops 2164244480 | bytes 41975808 | tf_op jit(solution)/shard_map/luv,xuv->ulx/dot_general | solution.py:117
  232.2 1.1 broadcast_in_dim.2
  233.3 6.2 %all-to-all-start = ((bf16[32,32,512]{2,1,0:T(8,128)(2,1)}), bf16[32,32,512]{2,1,0:T(8,128)(2,1)S(1)}, u32[]{:S(2)}, u32[]{:S(2)}) async-start(bf16[32,32,512]{2,1,0:T(8,128)(2,1)} %broadcast_in_dim.2), calls=%async_computation | async-start | bytes 2097152 | tf_op jit(solution)/shard_map/all_to_all | solution.py:27
  239.7 6.4 %copy.61 = bf16[512,4096]{0,1:T(8,128)(2,1)} copy(bf16[512,4096]{1,0:T(8,128)(2,1)} %param.5) | data formatting | bytes 8388608 | tf_op jit(solution)/shard_map/reshape | solution.py:105
  246.1 10.2 %all-to-all-done = bf16[32,32,512]{2,1,0:T(8,128)(2,1)S(1)} async-done(((bf16[32,32,512]{2,1,0:T(8,128)(2,1)}), bf16[32,32,512]{2,1,0:T(8,128)(2,1)S(1)}, u32[]{:S(2)}, u32[]{:S(2)}) %all-to-all-start) | async-done | bytes 1048608 | tf_op jit(solution)/shard_map/all_to_all | solution.py:27
  256.5 13.6 %fusion.5 = bf16[32,512]{1,0:T(8,128)(2,1)S(1)} fusion(f32[32,512,512]{1,2,0:T(8,128)} %get-tuple-element.12, f32[32,512]{1,0:T(8,128)S(1)} %convert_element_type.83), kind=kLoop, calls=%fused_computation.10 | loop fusion | flops 25149440 | bytes 33652736 | tf_op jit(solution)/shard_map/reduce_sum | solution.py:128
  270.2 17.3 %fusion.21 = bf16[32,512,128]{1,2,0:T(8,128)(2,1)} fusion(bf16[512,32,128]{0,2,1:T(8,128)(2,1)} %bitcast.100, f32[32,512,512]{1,2,0:T(8,128)} %get-tuple-element.12, f32[32,512]{1,0:T(8,128)S(1)} %convert_element_type.83), kind=kOutput, calls=%fused_computation.44 | convolution fusion | flops 2174746624 | bytes 42008576 | tf_op jit(solution)/shard_map/fta,afr->ftr/dot_general | solution.py:129
  287.5 6.8 %pad_maximum_fusion = bf16[32,512,129]{1,2,0:T(8,128)(2,1)} fusion(bf16[32,512,128]{1,2,0:T(8,128)(2,1)} %fusion.21, bf16[32,512,1]{1,2,0:T(2,128)(2,1)S(1)} %copy.48), kind=kLoop, calls=%fused_computation.18 | loop fusion | flops 8454144 | bytes 8454144 | tf_op jit(solution)/shard_map/concatenate | solution.py:37
  294.4 6.4 %copy.63 = bf16[512,4096]{0,1:T(8,128)(2,1)} copy(bf16[512,4096]{1,0:T(8,128)(2,1)} %get-tuple-element.8) | data formatting | bytes 8388608
  300.8 1.4 fusion.115
  302.4 0.5 fusion.113
  302.9 0.6 reduce_max.55
  303.5 0.7 reduce_max.56
  305.7 1.3 copy.43
  307.0 3.2 online-softmax
  310.2 2.9 select_subtract_fusion.17
  313.1 1.5 convolution_multiply_fusion.5
  314.6 3.3 online-softmax.1
  317.8 2.9 select_subtract_fusion.16
  320.7 1.4 convolution_multiply_fusion.4
  322.2 3.3 online-softmax.2
  325.4 2.9 select_subtract_fusion.15
  328.4 1.4 convolution_multiply_fusion.3
  329.8 3.3 online-softmax.3
  333.1 2.9 select_subtract_fusion.14
  336.0 1.4 convolution_multiply_fusion.2
  337.4 3.3 online-softmax.4
  340.7 2.9 select_subtract_fusion.13
  343.6 1.4 convolution_multiply_fusion.1
  345.0 3.3 online-softmax.5
  348.3 2.9 select_subtract_fusion.12
  351.2 112.1 %reduce-scatter.2.cloned.1.call-done = bf16[1,512,129]{1,2,0:T(8,128)(2,1)} async-done(((bf16[32,512,129]{1,2,0:T(8,128)(2,1)}), bf16[1,512,129]{1,2,0:T(8,128)(2,1)}) %reduce-scatter.2.cloned.1.call-update) | async-done | bytes 132112 | tf_op jit(solution)/shard_map/reduce_scatter | solution.py:40
  463.3 0.7 slice_convert_fusion
  464.0 1.6 fusion.38
  465.6 5.7 all-gather
  471.4 0.3 all-gather.11.cloned.1.call-start
  471.7 19.6 %all-gather.9.cloned.1.call-done = bf16[8,1,512,128]{3,2,1,0:T(8,128)(2,1)} async-done(((bf16[2,1,512,128]{3,2,1,0:T(8,128)(2,1)}), bf16[8,1,512,128]{3,2,1,0:T(8,128)(2,1)}) %all-gather.9.cloned.1.call-update) | async-done | bytes 1048592 | tf_op jit(solution)/shard_map/all_gather | solution.py:56
  491.4 20.1 %fusion.14 = f32[32,512,512]{1,2,0:T(8,128)} fusion(bf16[512,32,128]{0,2,1:T(8,128)(2,1)} %bitcast.102, bf16[512,4096]{1,0:T(8,128)(2,1)} %param.3), kind=kOutput, calls=%fused_computation.19 | convolution fusion | flops 2147483648 | bytes 41943040 | tf_op jit(solution)/shard_map/ivb,avb->via/dot_general | solution.py:150
  511.5 37.1 %fusion.116 = (f32[32,512]{1,0:T(8,128)S(1)}, f32[32,512,512]{2,1,0:T(8,128)}) fusion(f32[32,512,512]{1,2,0:T(8,128)} %fusion.14), kind=kOutput, calls=%fused_computation.130 | output fusion | flops 33554944 | bytes 67174400 | tf_op jit(solution)/shard_map/sub | solution.py:69
  548.6 7.2 %copy.51 = bf16[4,4,2,1,512,128]{4,5,2,1,0,3:T(8,128)(2,1)} copy(bf16[4,4,2,1,512,128]{5,4,2,0,1,3:T(8,128)(2,1)} %bitcast.105) | data formatting | bytes 8388608 | tf_op jit(solution)/shard_map/transpose | solution.py:59
  555.8 15.2 %fusion.20 = bf16[32,128,512]{2,1,0:T(8,128)(2,1)} fusion(bf16[32,512,128]{1,2,0:T(8,128)(2,1)} %bitcast.106, f32[32,512,512]{2,1,0:T(8,128)} %get-tuple-element.14, f32[32,512]{1,0:T(8,128)S(1)} %get-tuple-element.13), kind=kOutput, calls=%fused_computation.43 | convolution fusion | flops 2166358016 | bytes 42008576 | tf_op jit(solution)/shard_map/vcn,vnl->cvl/dot_general | solution.py:159
  571.0 6.3 %copy.55 = bf16[512,4096]{1,0:T(8,128)(2,1)} copy(bf16[512,4096]{0,1:T(8,128)(2,1)} %bitcast.107) | data formatting | bytes 8388608 | tf_op jit(solution)/shard_map/reshape | solution.py:162
  (29 shorter events, 1.2 us)
Async XLA Ops:
  6.5 197.2 %all-gather.7.cloned.1.call-start = ((), (), s32[]{:S(2)}) async-start(), calls=%async_computation.2 | async-start | bytes 8650752 | tf_op jit(solution)/shard_map/all_gather | solution.py:21
  6.5 3.5 copy-start.1
  233.3 23.0 %all-to-all-start = ((bf16[32,32,512]{2,1,0:T(8,128)(2,1)}), bf16[32,32,512]{2,1,0:T(8,128)(2,1)S(1)}, u32[]{:S(2)}, u32[]{:S(2)}) async-start(bf16[32,32,512]{2,1,0:T(8,128)(2,1)} %broadcast_in_dim.2), calls=%async_computation | async-start | bytes 2097152 | tf_op jit(solution)/shard_map/all_to_all | solution.py:27
  239.5 223.8 %reduce-scatter.2.cloned.1.call-start = ((), (), s32[]{:S(2)}) async-start(), calls=%async_computation.3 | async-start | bytes 4595712 | tf_op jit(solution)/shard_map/reduce_scatter | solution.py:40
  294.3 197.0 %all-gather.9.cloned.1.call-start = ((), (), s32[]{:S(2)}) async-start(), calls=%async_computation.4 | async-start | bytes 1310720 | tf_op jit(solution)/shard_map/all_gather | solution.py:56
  302.1 4.9 copy-start
  314.6 6.2 %copy-start.2 = (f32[512,512]{1,0:T(8,128)S(1)}, f32[512,512]{1,0:T(8,128)}, u32[]{:S(2)}) copy-start(f32[512,512]{1,0:T(8,128)} %convolution_multiply_fusion.5) | copy-start | bytes 3145732
  322.2 6.2 %copy-start.3 = (f32[512,512]{1,0:T(8,128)S(1)}, f32[512,512]{1,0:T(8,128)}, u32[]{:S(2)}) copy-start(f32[512,512]{1,0:T(8,128)} %convolution_multiply_fusion.4) | copy-start | bytes 3145732
  329.8 6.2 %copy-start.4 = (f32[512,512]{1,0:T(8,128)S(1)}, f32[512,512]{1,0:T(8,128)}, u32[]{:S(2)}) copy-start(f32[512,512]{1,0:T(8,128)} %convolution_multiply_fusion.3) | copy-start | bytes 3145732
  337.4 6.2 %copy-start.5 = (f32[512,512]{1,0:T(8,128)S(1)}, f32[512,512]{1,0:T(8,128)}, u32[]{:S(2)}) copy-start(f32[512,512]{1,0:T(8,128)} %convolution_multiply_fusion.2) | copy-start | bytes 3145732
  345.0 119.0 %copy-start.6 = (f32[512,512]{1,0:T(8,128)S(1)}, f32[512,512]{1,0:T(8,128)}, u32[]{:S(2)}) copy-start(f32[512,512]{1,0:T(8,128)} %convolution_multiply_fusion.1) | copy-start | bytes 3145732
  471.4 77.2 %all-gather.11.cloned.1.call-start = ((), (), s32[]{:S(2)}) async-start(), calls=%async_computation.5 | async-start | bytes 5242880 | tf_op jit(solution)/shard_map/all_gather | solution.py:56
Sparse Core Ops, SparseCore 0:
  12.0 191.6 all-gather.6
  294.4 168.8 reduce-scatter.1
  471.5 19.7 all-gather.8
  492.8 48.7 all-gather.10
where the time goes:
time: 585 us; the launch traced here: 584 us
  waiting for transfers between devices  334 us (57%)
  matrix products  96.2 us (16%)
  other arithmetic  65.9 us (11%)
  local copies, waits for them, and re-layouts  41.4 us (7%)
  Pallas kernels  19.5 us (3%)
  between operations  14.5 us (2%)
  starting transfers between devices  6.72 us (1%)
    all_gather x1, waiting for transfers between devices, side_by_side(): filled = lax.all_gather(both, axis, axis=dim, tiled=True)  192 us
    reduce_scatter x1, waiting for transfers between devices, in_one_piece(): filled = lax.psum_scatter(both, axis, scatter_dimension=dim, tiled=True)  112 us
    sub x1, other arithmetic, softmax_last(): exponent_values = jnp.exp(scores - top)  37.1 us
    dot_general x1, matrix products, body(): jnp.einsum('ivb,avb->via', query_heads_split, key_landmark_means, preferr...  20.1 us
    all_gather x2, waiting for transfers between devices, gather_in_order(): parts = lax.all_gather(parts, axes[k])  19.6 us
    unnamed x6, Pallas kernels  19.5 us
    dot_general x6, matrix products, newton_schulz(): middle = jnp.einsum('hij,hjk->hik', kernel_inv, 15.0 * identity - inner)  17.4 us
    dot_general x1, matrix products, body(): jnp.einsum('fta,afr->ftr', exponent_values.astype(jnp.bfloat16), value_he...  17.3 us
  transfers between devices with their start and end apart: 5, of which 4 were waited for; matrix products, arithmetic and copies ran while one was open for 17% of the time, Pallas kernels for 3%

commit v1 on v0

v1 whole, which is shorter than its diff:
```python
import math

import jax
import jax.numpy as jnp
from jax import lax
from jax.experimental import pallas as pl
from jax.experimental.pallas import tpu as pltpu
from jax.sharding import Mesh
from jax.sharding import PartitionSpec as P


H = 32
DH = 128
M = 512
ITERS = 6
D = 4096
SEQ = ("x", "z", "y")
DOC_SEQ = ("doc", "x", "z", "y")
C2 = DH ** (-0.5) * math.log2(math.e)
F32 = jnp.float32
BF16 = jnp.bfloat16
EXTRA = 16
ROWS = M // 32
GROUP = 4
LAST = 8
TALL = 128


def shifted(v, axis, by):
    n = lax.axis_size(axis)
    return lax.ppermute(v, axis, [(i, (i + by) % n) for i in range(n)])


def ring(v, axis):
    return [v] + [shifted(v, axis, s) for s in (1, 3, 2)]


def in_slots(parts):
    own, one, three, two = parts
    return [own, one, two, three]


def gather_first(v):
    both = jnp.stack([v, shifted(v, "y", 1)])
    half = both.shape[-1] // 2
    return (in_slots(ring(both[..., :half], "x")), in_slots(ring(both[..., half:], "z")))


def place(pos, slot_x, slot_z, slot_y):
    jx = (pos[0] + 4 - slot_x) % 4
    jz = (pos[1] + 4 - slot_z) % 4
    jy = (pos[2] + slot_y) % 2
    return (jx * 4 + jz) * 2 + jy


def fill_table(pos, table):
    for later in range(4):
        for early in range(4):
            for slot_y in range(2):
                at = (later * 4 + early) * 2 + slot_y
                table[at] = place(pos, early, later, slot_y) * ROWS
                table[32 + at] = place(pos, later, early, slot_y) * ROWS


def spread(table, base, pieces, out):
    for later, piece in enumerate(pieces):
        for early in range(4):
            for slot_y in range(2):
                at = pl.multiple_of(table[base + (later * 4 + early) * 2 + slot_y], ROWS)
                out[pl.ds(at, ROWS), :] = piece[early, slot_y]


def spread_head(table, head, pieces_a, pieces_b, out):
    @pl.when(head < H // 2)
    def _():
        spread(table, 0, pieces_a, out)

    @pl.when(head >= H // 2)
    def _():
        spread(table, 32, pieces_b, out)


def piece_specs(block_of, heads):
    shape = (4, 2, ROWS, heads * DH)
    last = H // 2 // heads
    a = pl.BlockSpec(shape, lambda *g: (0, 0, 0, jnp.minimum(block_of(*g), last - 1)))
    b = pl.BlockSpec(shape, lambda *g: (0, 0, 0, jnp.maximum(block_of(*g) - last, 0)))
    return [a] * 4 + [b] * 4


def nt(a, b):
    return lax.dot_general(a, b, (((1,), (1,)), ((), ())), preferred_element_type=F32)


def parts_kernel(pos, keys, values, *rest):
    pieces, (out, land, table) = rest[:8], rest[8:]
    g = pl.program_id(0)

    @pl.when(g == 0)
    def _():
        fill_table(pos, table)

    spread_head(table, g * GROUP, pieces[:4], pieces[4:], land)

    def scores_of(j):
        return nt(keys[:, j * DH : (j + 1) * DH], land[:, j * DH : (j + 1) * DH])

    def expo_of(scores):
        top = jnp.max(scores, 0, keepdims=True)
        expo = jnp.exp2(scores * C2 - top * C2)
        return top, expo.astype(BF16), jnp.sum(expo, 0, keepdims=True)

    def store(j, top, expo, totals):
        weighted = lax.dot_general(
            values[:, j * DH : (j + 1) * DH],
            expo,
            (((0,), (0,)), ((), ())),
            preferred_element_type=F32,
        )
        part = (weighted * (1.0 / totals)).astype(BF16)
        level = top * C2 + jnp.log2(totals)
        high = level.astype(BF16).astype(F32)
        mid = (level - high).astype(BF16).astype(F32)
        low = level - high - mid
        rows = []
        for k in range(0, M, 128):
            at = slice(k, k + 128)
            out[j, at, :] = part[:, at]
            rows += [high[:, at], mid[:, at], low[:, at]]
        rows.append(jnp.zeros((EXTRA - 12, 128), F32))
        out[j, M : M + EXTRA, :] = jnp.concatenate(rows, 0).astype(BF16)

    scores = scores_of(0)
    ready = None
    for j in range(GROUP):
        following = scores_of(j + 1) if j + 1 < GROUP else None
        current = expo_of(scores)
        if ready is not None:
            store(j - 1, *ready)
        ready, scores = current, following
    store(GROUP - 1, *ready)


def near_kernel(pos, queries, *rest):
    pieces, (out, land, table) = rest[:8], rest[8:]
    g = pl.program_id(0)

    @pl.when(g == 0)
    def _():
        fill_table(pos, table)

    spread_head(table, g * GROUP, pieces[:4], pieces[4:], land)
    for j in range(GROUP):
        cols = slice(j * DH, (j + 1) * DH)
        for t in range(0, queries.shape[0], TALL):
            near = nt(queries[t : t + TALL, cols], land[:, cols])
            top = jnp.max(near, 1, keepdims=True)
            expo = jnp.exp2(near * C2 - top * C2)
            totals = jnp.sum(expo, 1, keepdims=True)
            out[j, t : t + TALL] = (expo * (1.0 / totals)).astype(BF16)


def inverse_kernel(pos, *rest):
    pieces, (out, land_q, land_k, table) = rest[:16], rest[16:]
    fill_table(pos, table)
    head = place(pos, 0, 0, 0)
    spread_head(table, head, pieces[:4], pieces[4:8], land_q)
    spread_head(table, head, pieces[8:12], pieces[12:], land_k)
    scores = nt(land_q[...], land_k[...])
    top = jnp.max(scores, 1, keepdims=True)
    expo = jnp.exp2((scores - top) * C2)
    kernel = expo / jnp.sum(expo, 1, keepdims=True)
    row_most = jnp.max(jnp.sum(jnp.abs(kernel), 1, keepdims=True))
    col_most = jnp.max(jnp.sum(jnp.abs(kernel), 0, keepdims=True))
    low = kernel.astype(BF16)
    inverse = kernel.T / (row_most * col_most)

    def dot(a, b):
        return jnp.dot(a, b, preferred_element_type=F32)

    def sweep(_, inverse):
        inv = inverse.astype(BF16)
        prod = dot(low, inv)
        p = prod.astype(BF16)
        inner = 7.0 * prod - dot(p, p)
        middle = 15.0 * prod - dot(p, inner.astype(BF16))
        return 0.25 * (13.0 * inverse - dot(inv, middle.astype(BF16)))

    out[...] = lax.fori_loop(0, ITERS, sweep, inverse).astype(BF16)


def product_kernel(parts, levels, inverse, out, acc):
    c = pl.program_id(0)
    level = jnp.zeros((32, 128), F32)
    for k in range(4):
        rows = [levels[:, 3 * k + t, :].astype(F32) for t in range(3)]
        level = jnp.where(c == k, rows[0] + rows[1] + rows[2], level)
    weight = jnp.exp2(level - jnp.max(level, 0, keepdims=True))
    weight = weight / jnp.sum(weight, 0, keepdims=True)
    normed = jnp.zeros((128, 128), F32)
    for s in range(32):
        normed = normed + parts[s].astype(F32) * weight[s : s + 1]
    part = nt(inverse[...], normed.astype(BF16))

    @pl.when(c == 0)
    def _():
        acc[...] = part

    @pl.when(c > 0)
    def _():
        acc[...] += part

    @pl.when(c == 3)
    def _():
        out[...] = acc[...].astype(BF16)


def final_kernel(pos, weights, *rest):
    pieces, (out, prod) = rest[:8], rest[8:]
    g = pl.program_id(0)
    half = M // 2

    @pl.when(g == 0)
    def _():
        for slot_x in range(4):
            for slot_z in range(4):
                for slot_y in range(2):
                    at = (slot_x * 4 + slot_z) * 2 + slot_y
                    prod[at, :half] = pieces[slot_z][slot_x, slot_y]
                    prod[at, half:] = pieces[4 + slot_x][slot_z, slot_y]

    for j in range(LAST):
        head = g * LAST + j
        jx, jz, jy = head // 8, (head // 2) % 4, head % 2
        slot_x, slot_z = (pos[0] + 4 - jx) % 4, (pos[1] + 4 - jz) % 4
        at = (slot_x * 4 + slot_z) * 2 + (pos[2] + jy) % 2
        both = jnp.dot(weights[j], prod[at], preferred_element_type=F32)
        out[:, j * DH : (j + 1) * DH] = both.astype(BF16)


def call(kernel, grid, in_specs, out_spec, out_shape, scratch, prefetch=1):
    return pl.pallas_call(
        kernel,
        grid_spec=pltpu.PrefetchScalarGridSpec(
            num_scalar_prefetch=prefetch,
            grid=grid,
            in_specs=in_specs,
            out_specs=out_spec,
            scratch_shapes=scratch,
        ),
        out_shape=out_shape,
        compiler_params=pltpu.CompilerParams(dimension_semantics=("arbitrary",) * len(grid)),
    )


def landmarks(tokens, per_device):
    segment = tokens.shape[0] // per_device
    sums = jnp.sum(tokens.reshape(per_device, segment, D), axis=1, dtype=F32)
    return (sums / segment).astype(BF16)


def steps(queries, keys, values):
    pos = jnp.stack([lax.axis_index(a) for a in SEQ]).astype(jnp.int32)
    here = queries.shape[0]
    per_device = M // 32
    means = jnp.stack([landmarks(queries, per_device), landmarks(keys, per_device)])
    first_a, first_b = gather_first(means)
    q_a = in_slots(ring(jnp.stack([p[:, 0] for p in first_a]), "z"))
    q_b = in_slots(ring(jnp.stack([p[:, 0] for p in first_b]), "x"))
    k_a = in_slots(ring(jnp.stack([p[:, 1] for p in first_a]), "z"))
    k_b = in_slots(ring(jnp.stack([p[:, 1] for p in first_b]), "x"))

    column = pl.BlockSpec((here, GROUP * DH), lambda h, pos: (0, h))
    per_head = piece_specs(lambda h, pos: h, GROUP)
    land = pltpu.VMEM((M, GROUP * DH), BF16)
    table = pltpu.SMEM((64,), jnp.int32)
    parts = call(
        parts_kernel,
        (H // GROUP,),
        [column, column] + per_head,
        pl.BlockSpec((GROUP, M + EXTRA, DH), lambda h, pos: (h, 0, 0)),
        jax.ShapeDtypeStruct((H, M + EXTRA, DH), BF16),
        [land, table],
    )(pos, keys, values, *q_a, *q_b)
    parts = lax.all_to_all(parts, SEQ, split_axis=0, concat_axis=0, tiled=True)

    weights = call(
        near_kernel,
        (H // GROUP,),
        [column] + per_head,
        pl.BlockSpec((GROUP, here, M), lambda h, pos: (h, 0, 0)),
        jax.ShapeDtypeStruct((H, here, M), BF16),
        [land, table],
    )(pos, queries, *k_a, *k_b)

    owned = piece_specs(lambda g, pos: place(pos, 0, 0, 0), 1)
    inverse = call(
        inverse_kernel,
        (1,),
        owned + owned,
        pl.BlockSpec((M, M), lambda g, pos: (0, 0)),
        jax.ShapeDtypeStruct((M, M), BF16),
        [pltpu.VMEM((M, DH), BF16)] * 2 + [table],
    )(pos, *q_a, *q_b, *k_a, *k_b)

    product = call(
        product_kernel,
        (4,),
        [
            pl.BlockSpec((H, DH, 128), lambda c: (0, c, 0)),
            pl.BlockSpec((H, EXTRA, 128), lambda c: (0, M // EXTRA, 0)),
            pl.BlockSpec((M, 128), lambda c: (0, c)),
        ],
        pl.BlockSpec((M, DH), lambda c: (0, 0)),
        jax.ShapeDtypeStruct((M, DH), BF16),
        [pltpu.VMEM((M, DH), F32)],
        prefetch=0,
    )(parts, parts, inverse)

    both = jnp.stack([product, shifted(product, "y", 1)])
    half = M // 2
    p_a = in_slots(ring(jnp.stack(in_slots(ring(both[:, :half], "x"))), "z"))
    p_b = in_slots(ring(jnp.stack(in_slots(ring(both[:, half:], "z"))), "x"))

    whole = pl.BlockSpec((4, 2, half, DH), lambda g, pos: (0, 0, 0, 0))

    return call(
        final_kernel,
        (H // LAST,),
        [pl.BlockSpec((LAST, here, M), lambda g, pos: (g, 0, 0))] + [whole] * 8,
        pl.BlockSpec((here, LAST * DH), lambda g, pos: (0, g)),
        jax.ShapeDtypeStruct((here, D), BF16),
        [pltpu.VMEM((H, M, DH), BF16)],
    )(pos, weights, *p_a, *p_b)


def solution(mesh):
    torus = Mesh(mesh.devices.reshape(4, 4, 2, mesh.shape["doc"]), ("x", "z", "y", "doc"))
    spec = P(DOC_SEQ, None)
    return jax.shard_map(
        steps, mesh=torus, in_specs=(spec, spec, spec), out_specs=spec, check_vma=False
    )
```

time: 585 us -> 266 us (0.45)
  the two profiles are of different devices: /device:TPU:0 before, /device:TPU:60 now
where the time goes in v1:
time: 266 us; the launch traced here: 265 us
  waiting for transfers between devices  132 us (50%)
  Pallas kernels  64.3 us (24%)
  starting transfers between devices  57 us (21%)
  other arithmetic  7.4 us (3%)
  local copies, waits for them, and re-layouts  4.4 us (2%)
    ppermute x32, waiting for transfers between devices, shifted(): return lax.ppermute(v, axis, [(i, (i + by) % n) for i in range(n)])  132 us
    ppermute x32, starting transfers between devices, shifted(): return lax.ppermute(v, axis, [(i, (i + by) % n) for i in range(n)])  45.6 us
    pallas_call x1, Pallas kernels, steps(): call(parts_kernel, (H // GROUP,), [column, column] + per_head, pl.BlockSp...  17.2 us
    pallas_call x1, Pallas kernels, steps(): call(near_kernel, (H // GROUP,), [column] + per_head, pl.BlockSpec((GROUP...  16.3 us
    pallas_call x1, Pallas kernels, steps(): call(inverse_kernel, (1,), owned + owned, pl.BlockSpec((M, M), lambda g,...  13.4 us
    pallas_call x1, Pallas kernels, steps(): call(final_kernel, (H // LAST,), [pl.BlockSpec((LAST, here, M), lambda g,...  12.2 us
    all_to_all x1, starting transfers between devices, steps(): parts = lax.all_to_all(parts, SEQ, split_axis=0, concat_axis=0, tiled=True)  11.4 us
  transfers between devices with their start and end apart: 33, of which 15 were waited for; matrix products, arithmetic and copies ran while one was open for 1% of the time, Pallas kernels for 11%

profile of v1, /device:TPU:60, one launch (start us, length us, event | category | flops | bytes accessed | tf_op | source)
XLA Modules:
  0.0 265.4 jit_solution(870668346844988663)
XLA Ops:
  0.0 3.5 %convert_reduce_fusion.1 = f32[16,4096]{1,0:T(8,128)S(1)} fusion(bf16[512,4096]{1,0:T(8,128)(2,1)} %queries.1), kind=kLoop, calls=%fused_computation.1 | loop fusion | flops 4128768 | bytes 4456448 | tf_op jit(solution)/shard_map/reduce_sum | solution.py:258
  3.5 1.1 convert_reduce_fusion
  4.7 0.8 collective-permute-start
  5.5 7.3 %collective-permute-done = bf16[2,16,4096]{2,1,0:T(8,128)(2,1)S(1)} collective-permute-done((bf16[2,16,4096]{2,1,0:T(8,128)(2,1)S(1)}, bf16[2,16,4096]{2,1,0:T(8,128)(2,1)S(1)}, u32[]{:S(2)}, u32[]{:S(2)}) %collective-permute-start) | collective-permute-done | bytes 262176 | tf_op jit(solution)/shard_map/ppermute | solution.py:31
  13.6 3.3 %collective-permute-start.8 = (bf16[2,2,16,2048]{3,2,0,1:T(8,128)(2,1)S(1)}, bf16[2,2,16,2048]{3,2,0,1:T(8,128)(2,1)S(1)}, u32[]{:S(2)}, u32[]{:S(2)}) collective-permute-start(bf16[2,2,16,2048]{3,2,0,1:T(8,128)(2,1)S(1)} %get-tuple-element.9), channel_id=1, source_target_pairs={{0,16},{8,24},{16,0},{24,8},{1,17},{9,25},{17,1},{25,9},{2,18},{10... | collective-permute-start | bytes 786440 | tf_op jit(solution)/shard_map/ppermute | solution.py:31
  16.8 2.2 collective-permute-start.7
  19.1 2.7 %collective-permute-start.2 = (bf16[2,2,16,2048]{3,2,0,1:T(8,128)(2,1)S(1)}, bf16[2,2,16,2048]{3,2,0,1:T(8,128)(2,1)S(1)}, u32[]{:S(2)}, u32[]{:S(2)}) collective-permute-start(bf16[2,2,16,2048]{3,2,0,1:T(8,128)(2,1)S(1)} %get-tuple-element.10), channel_id=1, source_target_pairs={{0,64},{32,96},{64,0},{96,32},{1,65},{33,97},{65,1},{97,33},{2,66}... | collective-permute-start | bytes 786440 | tf_op jit(solution)/shard_map/ppermute | solution.py:31
  21.8 0.7 fusion.11
  22.6 6.9 %collective-permute-done.2 = bf16[2,2,16,2048]{3,2,0,1:T(8,128)(2,1)S(1)} collective-permute-done((bf16[2,2,16,2048]{3,2,0,1:T(8,128)(2,1)S(1)}, bf16[2,2,16,2048]{3,2,0,1:T(8,128)(2,1)S(1)}, u32[]{:S(2)}, u32[]{:S(2)}) %collective-permute-start.2) | collective-permute-done | bytes 262176 | tf_op jit(solution)/shard_map/ppermute | solution.py:31
  29.5 2.8 %collective-permute-done.1 = bf16[2,2,16,2048]{3,2,0,1:T(8,128)(2,1)S(1)} collective-permute-done((bf16[2,2,16,2048]{3,2,0,1:T(8,128)(2,1)S(1)}, bf16[2,2,16,2048]{3,2,0,1:T(8,128)(2,1)S(1)}, u32[]{:S(2)}, u32[]{:S(2)}) %collective-permute-start.1) | collective-permute-done | bytes 262176 | tf_op jit(solution)/shard_map/ppermute | solution.py:31
  32.5 3.1 %collective-permute-start.14 = (bf16[4,2,16,2048]{3,2,1,0:T(8,128)(2,1)S(1)}, bf16[4,2,16,2048]{3,2,1,0:T(8,128)(2,1)S(1)}, u32[]{:S(2)}, u32[]{:S(2)}) collective-permute-start(bf16[4,2,16,2048]{3,2,1,0:T(8,128)(2,1)S(1)} %pad_maximum_fusion.2.rest_0_), channel_id=1, source_target_pairs={{0,16},{8,24},{16,0},{24,8},{1,17},{9,25},{17,1},{25,9},{2,18},{10... | collective-permute-start | bytes 1572872 | tf_op jit(solution)/shard_map/ppermute | solution.py:31
  35.6 2.2 collective-permute-start.13
  38.5 0.7 slice_bitcast_fusion.1
  39.2 0.7 slice_bitcast_fusion.2
  40.0 4.5 %collective-permute-start.17 = (bf16[4,2,16,2048]{3,2,1,0:T(8,128)(2,1)S(1)}, bf16[4,2,16,2048]{3,2,1,0:T(8,128)(2,1)}, u32[]{:S(2)}, u32[]{:S(2)}) collective-permute-start(bf16[4,2,16,2048]{3,2,1,0:T(8,128)(2,1)S(1)} %pad_maximum_fusion.3.rest_4_), channel_id=1, source_target_pairs={{0,64},{32,96},{64,0},{96,32},{1,65},{33,97},{65,1},{97,33},{2,66}... | collective-permute-start | bytes 1572872 | tf_op jit(solution)/shard_map/ppermute | solution.py:31
  44.5 11.8 %collective-permute-done.15.rest_3_ = bf16[4,2,16,2048]{3,2,1,0:T(8,128)(2,1)S(1)} collective-permute-done((bf16[4,2,16,2048]{3,2,1,0:T(8,128)(2,1)S(1)}, bf16[4,2,16,2048]{3,2,1,0:T(8,128)(2,1)S(1)}, u32[]{:S(2)}, u32[]{:S(2)}) %collective-permute-start.15) | collective-permute-done | bytes 524320 | tf_op jit(solution)/shard_map/ppermute | solution.py:31
  56.9 0.7 pad_add_fusion.pos
  58.2 7.4 %collective-permute-done.16.rest_5_ = bf16[4,2,16,2048]{3,2,1,0:T(8,128)(2,1)} collective-permute-done((bf16[4,2,16,2048]{3,2,1,0:T(8,128)(2,1)S(1)}, bf16[4,2,16,2048]{3,2,1,0:T(8,128)(2,1)}, u32[]{:S(2)}, u32[]{:S(2)}) %collective-permute-start.16) | collective-permute-done | bytes 524320 | tf_op jit(solution)/shard_map/ppermute | solution.py:31
  65.7 17.2 %shard_map.38 = bf16[32,528,128]{2,1,0:T(8,128)(2,1)} custom-call(s32[3]{0:T(128)} %pad_add_fusion.pos, bf16[512,4096]{1,0:T(8,128)(2,1)} %keys.1, bf16[512,4096]{1,0:T(8,128)(2,1)} %values.1, bf16[4,2,16,2048]{3,2,1,0:T(8,128)(2,1)} %copy-done.2, bf16[4,2,16,2048]{3,2,1,0:T(8,128)(2,1)} %copy-done.10, bf16[4,2,16,2048]{3,2,1,0:T(8,128)(2,1)} %copy-done.8, ...), custom_call_target="tpu_custom_call" | custom-call | tf_op jit(solution)/shard_map/pallas_call | solution.py:277
  82.9 11.4 %all-to-all-start = ((bf16[32,528,128]{2,1,0:T(8,128)(2,1)}), bf16[32,528,128]{2,1,0:T(8,128)(2,1)}, u32[]{:S(2)}, u32[]{:S(2)}) async-start(bf16[32,528,128]{2,1,0:T(8,128)(2,1)} %shard_map.38), calls=%async_computation | async-start | bytes 8650752 | tf_op jit(solution)/shard_map/all_to_all | solution.py:285
  95.0 2.4 collective-permute-start.5
  97.4 1.8 collective-permute-start.4
  99.9 2.8 %collective-permute-start.11 = (bf16[4,2,16,2048]{3,2,1,0:T(8,128)(2,1)S(1)}, bf16[4,2,16,2048]{3,2,1,0:T(8,128)(2,1)S(1)}, u32[]{:S(2)}, u32[]{:S(2)}) collective-permute-start(bf16[4,2,16,2048]{3,2,1,0:T(8,128)(2,1)S(1)} %pad_maximum_fusion.1.rest_4_.rest_12_), channel_id=1, source_target_pairs={{0,64},{32,96},{64,0},{96,32},{1,65},{33,97},{65,1},{97,33},{2,66}... | collective-permute-start | bytes 1572872 | tf_op jit(solution)/shard_map/ppermute | solution.py:31
  102.6 48.6 %collective-permute-done.6.rest_3_.rest_11_ = bf16[4,2,16,2048]{3,2,1,0:T(8,128)(2,1)S(1)} collective-permute-done((bf16[4,2,16,2048]{3,2,1,0:T(8,128)(2,1)S(1)}, bf16[4,2,16,2048]{3,2,1,0:T(8,128)(2,1)S(1)}, u32[]{:S(2)}, u32[]{:S(2)}) %collective-permute-start.6) | collective-permute-done | bytes 524320 | tf_op jit(solution)/shard_map/ppermute | solution.py:31
  151.2 1.2 collective-permute-start.10
  152.5 11.4 %collective-permute-done.5.rest_2_.rest_10_ = bf16[4,2,16,2048]{3,2,1,0:T(8,128)(2,1)S(1)} collective-permute-done((bf16[4,2,16,2048]{3,2,1,0:T(8,128)(2,1)S(1)}, bf16[4,2,16,2048]{3,2,1,0:T(8,128)(2,1)S(1)}, u32[]{:S(2)}, u32[]{:S(2)}) %collective-permute-start.5) | collective-permute-done | bytes 524320 | tf_op jit(solution)/shard_map/ppermute | solution.py:31
  163.9 3.4 %collective-permute-done.4.rest_1_.rest_9_ = bf16[4,2,16,2048]{3,2,1,0:T(8,128)(2,1)S(1)} collective-permute-done((bf16[4,2,16,2048]{3,2,1,0:T(8,128)(2,1)S(1)}, bf16[4,2,16,2048]{3,2,1,0:T(8,128)(2,1)S(1)}, u32[]{:S(2)}, u32[]{:S(2)}) %collective-permute-start.4) | collective-permute-done | bytes 524320 | tf_op jit(solution)/shard_map/ppermute | solution.py:31
  167.3 0.8 copy-done.12
  168.5 13.4 %shard_map.39.inverse = bf16[512,512]{1,0:T(8,128)(2,1)} custom-call(s32[3]{0:T(128)} %pad_add_fusion.pos, bf16[4,2,16,2048]{3,2,1,0:T(8,128)(2,1)} %copy-done.2, bf16[4,2,16,2048]{3,2,1,0:T(8,128)(2,1)} %copy-done.10, bf16[4,2,16,2048]{3,2,1,0:T(8,128)(2,1)} %copy-done.8, bf16[4,2,16,2048]{3,2,1,0:T(8,128)(2,1)} %copy-done.6, ...), custom_call_target="tpu_custom_call" | custom-call | tf_op jit(solution)/shard_map/pallas_call | solution.py:297
  181.9 5.2 %shard_map.40 = bf16[512,128]{1,0:T(8,128)(2,1)} custom-call(bf16[32,528,128]{2,1,0:T(8,128)(2,1)} %all-to-all-done.parts.levels, bf16[32,528,128]{2,1,0:T(8,128)(2,1)} %all-to-all-done.parts.levels, bf16[512,512]{1,0:T(8,128)(2,1)} %shard_map.39.inverse), custom_call_target="tpu_custom_call" | custom-call | tf_op jit(solution)/shard_map/pallas_call | solution.py:306
  187.1 5.7 %collective-permute-done.19 = bf16[512,128]{1,0:T(8,128)(2,1)S(1)} collective-permute-done((bf16[512,128]{1,0:T(8,128)(2,1)}, bf16[512,128]{1,0:T(8,128)(2,1)S(1)}, u32[]{:S(2)}, u32[]{:S(2)}) %collective-permute-start.19) | collective-permute-done | bytes 131104 | tf_op jit(solution)/shard_map/ppermute | solution.py:31
  192.8 0.9 pad_maximum_fusion.7
  193.7 2.7 %collective-permute-start.22 = (bf16[2,256,128]{2,1,0:T(8,128)(2,1)S(1)}, bf16[2,256,128]{2,1,0:T(8,128)(2,1)S(1)}, u32[]{:S(2)}, u32[]{:S(2)}) collective-permute-start(bf16[2,256,128]{2,1,0:T(8,128)(2,1)S(1)} %get-tuple-element.12), channel_id=1, source_target_pairs={{0,96},{32,0},{64,32},{96,64},{1,97},{33,1},{65,33},{97,65},{2,98}... | collective-permute-start | bytes 393224 | tf_op jit(solution)/shard_map/ppermute | solution.py:31
  196.4 1.9 collective-permute-start.21
  198.6 1.3 collective-permute-done.22
  199.9 3.1 %collective-permute-done.21 = bf16[2,256,128]{2,1,0:T(8,128)(2,1)S(1)} collective-permute-done((bf16[2,256,128]{2,1,0:T(8,128)(2,1)S(1)}, bf16[2,256,128]{2,1,0:T(8,128)(2,1)S(1)}, u32[]{:S(2)}, u32[]{:S(2)}) %collective-permute-start.21) | collective-permute-done | bytes 131104 | tf_op jit(solution)/shard_map/ppermute | solution.py:31
  203.0 1.3 collective-permute-done.20
  204.6 1.9 collective-permute-start.26
  206.5 2.1 collective-permute-start.28
  208.6 2.1 collective-permute-start.24
  210.6 9.0 %collective-permute-done.27 = bf16[2,256,128]{2,1,0:T(8,128)(2,1)S(1)} collective-permute-done((bf16[2,256,128]{2,1,0:T(8,128)(2,1)S(1)}, bf16[2,256,128]{2,1,0:T(8,128)(2,1)S(1)}, u32[]{:S(2)}, u32[]{:S(2)}) %collective-permute-start.27) | collective-permute-done | bytes 131104 | tf_op jit(solution)/shard_map/ppermute | solution.py:31
  219.6 11.2 %collective-permute-done.28 = bf16[2,256,128]{2,1,0:T(8,128)(2,1)S(1)} collective-permute-done((bf16[2,256,128]{2,1,0:T(8,128)(2,1)S(1)}, bf16[2,256,128]{2,1,0:T(8,128)(2,1)S(1)}, u32[]{:S(2)}, u32[]{:S(2)}) %collective-permute-start.28) | collective-permute-done | bytes 131104 | tf_op jit(solution)/shard_map/ppermute | solution.py:31
  230.9 0.8 collective-permute-start.31
  231.7 1.4 collective-permute-start.30
  233.2 2.5 collective-permute-start.29
  235.7 16.3 %shard_map.37.weights = bf16[32,512,512]{2,1,0:T(8,128)(2,1)} custom-call(s32[3]{0:T(128)} %pad_add_fusion.pos, bf16[512,4096]{1,0:T(8,128)(2,1)} %queries.1, bf16[4,2,16,2048]{3,2,1,0:T(8,128)(2,1)} %copy-done.1, bf16[4,2,16,2048]{3,2,1,0:T(8,128)(2,1)} %copy-done.9, bf16[4,2,16,2048]{3,2,1,0:T(8,128)(2,1)} %copy-done.7, ...), custom_call_target="tpu_custom_call" | custom-call | tf_op jit(solution)/shard_map/pallas_call | solution.py:287
  252.1 0.8 copy-done.17
  253.2 12.2 %shard_map.41 = bf16[512,4096]{1,0:T(8,128)(2,1)} custom-call(s32[3]{0:T(128)} %pad_add_fusion.pos, bf16[32,512,512]{2,1,0:T(8,128)(2,1)} %shard_map.37.weights, bf16[4,2,256,128]{3,2,1,0:T(8,128)(2,1)} %copy-done.14, bf16[4,2,256,128]{3,2,1,0:T(8,128)(2,1)} %copy-done.18, bf16[4,2,256,128]{3,2,1,0:T(8,128)(2,1)} %copy-done.17, ...), custom_call_target="tpu_custom_call" | custom-call | tf_op jit(solution)/shard_map/pallas_call | solution.py:327
  (93 shorter events, 5.7 us)
Async XLA Ops:
  4.7 8.1 %collective-permute-start = (bf16[2,16,4096]{2,1,0:T(8,128)(2,1)S(1)}, bf16[2,16,4096]{2,1,0:T(8,128)(2,1)S(1)}, u32[]{:S(2)}, u32[]{:S(2)}) collective-permute-start(bf16[2,16,4096]{2,1,0:T(8,128)(2,1)S(1)} %get-tuple-element.25), channel_id=1, source_target_pairs={{0,4},{4,0},{1,5},{5,1},{2,6},{6,2},{3,7},{7,3},{8,12},{12,8},{9,1... | collective-permute-start | bytes 786440 | tf_op jit(solution)/shard_map/ppermute | solution.py:31
  12.9 9.7 %collective-permute-start.3 = (bf16[2,2,16,2048]{3,2,0,1:T(8,128)(2,1)S(1)}, bf16[2,2,16,2048]{3,2,0,1:T(8,128)(2,1)S(1)}, u32[]{:S(2)}, u32[]{:S(2)}) collective-permute-start(bf16[2,2,16,2048]{3,2,0,1:T(8,128)(2,1)S(1)} %get-tuple-element.10), channel_id=1, source_target_pairs={{0,96},{32,0},{64,32},{96,64},{1,97},{33,1},{65,33},{97,65},{2,98}... | collective-permute-start | bytes 786440 | tf_op jit(solution)/shard_map/ppermute | solution.py:31
  13.5 22.1 %collective-permute-start.9 = (bf16[2,2,16,2048]{3,2,0,1:T(8,128)(2,1)S(1)}, bf16[2,2,16,2048]{3,2,0,1:T(8,128)(2,1)S(1)}, u32[]{:S(2)}, u32[]{:S(2)}) collective-permute-start(bf16[2,2,16,2048]{3,2,0,1:T(8,128)(2,1)S(1)} %get-tuple-element.9), channel_id=1, source_target_pairs={{0,24},{8,0},{16,8},{24,16},{1,25},{9,1},{17,9},{25,17},{2,26},{10... | collective-permute-start | bytes 786440 | tf_op jit(solution)/shard_map/ppermute | solution.py:31
  13.6 24.9 %collective-permute-start.8 = (bf16[2,2,16,2048]{3,2,0,1:T(8,128)(2,1)S(1)}, bf16[2,2,16,2048]{3,2,0,1:T(8,128)(2,1)S(1)}, u32[]{:S(2)}, u32[]{:S(2)}) collective-permute-start(bf16[2,2,16,2048]{3,2,0,1:T(8,128)(2,1)S(1)} %get-tuple-element.9), channel_id=1, source_target_pairs={{0,16},{8,24},{16,0},{24,8},{1,17},{9,25},{17,1},{25,9},{2,18},{10... | collective-permute-start | bytes 786440 | tf_op jit(solution)/shard_map/ppermute | solution.py:31
  16.8 22.3 %collective-permute-start.7 = (bf16[2,2,16,2048]{3,2,0,1:T(8,128)(2,1)S(1)}, bf16[2,2,16,2048]{3,2,0,1:T(8,128)(2,1)S(1)}, u32[]{:S(2)}, u32[]{:S(2)}) collective-permute-start(bf16[2,2,16,2048]{3,2,0,1:T(8,128)(2,1)S(1)} %get-tuple-element.9), channel_id=1, source_target_pairs={{0,8},{8,16},{16,24},{24,0},{1,9},{9,17},{17,25},{25,1},{2,10},{10... | collective-permute-start | bytes 786440 | tf_op jit(solution)/shard_map/ppermute | solution.py:31
  19.1 10.4 %collective-permute-start.2 = (bf16[2,2,16,2048]{3,2,0,1:T(8,128)(2,1)S(1)}, bf16[2,2,16,2048]{3,2,0,1:T(8,128)(2,1)S(1)}, u32[]{:S(2)}, u32[]{:S(2)}) collective-permute-start(bf16[2,2,16,2048]{3,2,0,1:T(8,128)(2,1)S(1)} %get-tuple-element.10), channel_id=1, source_target_pairs={{0,64},{32,96},{64,0},{96,32},{1,65},{33,97},{65,1},{97,33},{2,66}... | collective-permute-start | bytes 786440 | tf_op jit(solution)/shard_map/ppermute | solution.py:31
  22.5 9.7 %collective-permute-start.1 = (bf16[2,2,16,2048]{3,2,0,1:T(8,128)(2,1)S(1)}, bf16[2,2,16,2048]{3,2,0,1:T(8,128)(2,1)S(1)}, u32[]{:S(2)}, u32[]{:S(2)}) collective-permute-start(bf16[2,2,16,2048]{3,2,0,1:T(8,128)(2,1)S(1)} %get-tuple-element.10), channel_id=1, source_target_pairs={{0,32},{32,64},{64,96},{96,0},{1,33},{33,65},{65,97},{97,1},{2,34}... | collective-permute-start | bytes 786440 | tf_op jit(solution)/shard_map/ppermute | solution.py:31
  32.4 33.3 %copy-start.2 = (bf16[4,2,16,2048]{3,2,1,0:T(8,128)(2,1)}, bf16[4,2,16,2048]{3,2,1,0:T(8,128)(2,1)S(1)}, u32[]{:S(2)}) copy-start(bf16[4,2,16,2048]{3,2,1,0:T(8,128)(2,1)S(1)} %pad_maximum_fusion.2.rest_0_) | copy-start | bytes 1572868
  32.4 24.0 %collective-permute-start.15 = (bf16[4,2,16,2048]{3,2,1,0:T(8,128)(2,1)S(1)}, bf16[4,2,16,2048]{3,2,1,0:T(8,128)(2,1)S(1)}, u32[]{:S(2)}, u32[]{:S(2)}) collective-permute-start(bf16[4,2,16,2048]{3,2,1,0:T(8,128)(2,1)S(1)} %pad_maximum_fusion.2.rest_0_), channel_id=1, source_target_pairs={{0,24},{8,0},{16,8},{24,16},{1,25},{9,1},{17,9},{25,17},{2,26},{10... | collective-permute-start | bytes 1572872 | tf_op jit(solution)/shard_map/ppermute | solution.py:31
  32.5 25.1 %collective-permute-start.14 = (bf16[4,2,16,2048]{3,2,1,0:T(8,128)(2,1)S(1)}, bf16[4,2,16,2048]{3,2,1,0:T(8,128)(2,1)S(1)}, u32[]{:S(2)}, u32[]{:S(2)}) collective-permute-start(bf16[4,2,16,2048]{3,2,1,0:T(8,128)(2,1)S(1)} %pad_maximum_fusion.2.rest_0_), channel_id=1, source_target_pairs={{0,16},{8,24},{16,0},{24,8},{1,17},{9,25},{17,1},{25,9},{2,18},{10... | collective-permute-start | bytes 1572872 | tf_op jit(solution)/shard_map/ppermute | solution.py:31
  35.6 22.6 %collective-permute-start.13 = (bf16[4,2,16,2048]{3,2,1,0:T(8,128)(2,1)S(1)}, bf16[4,2,16,2048]{3,2,1,0:T(8,128)(2,1)S(1)}, u32[]{:S(2)}, u32[]{:S(2)}) collective-permute-start(bf16[4,2,16,2048]{3,2,1,0:T(8,128)(2,1)S(1)} %pad_maximum_fusion.2.rest_0_), channel_id=1, source_target_pairs={{0,8},{8,16},{16,24},{24,0},{1,9},{9,17},{17,25},{25,1},{2,10},{10... | collective-permute-start | bytes 1572872 | tf_op jit(solution)/shard_map/ppermute | solution.py:31
  39.9 25.7 %copy-start.4 = (bf16[4,2,16,2048]{3,2,1,0:T(8,128)(2,1)}, bf16[4,2,16,2048]{3,2,1,0:T(8,128)(2,1)S(1)}, u32[]{:S(2)}) copy-start(bf16[4,2,16,2048]{3,2,1,0:T(8,128)(2,1)S(1)} %pad_maximum_fusion.3.rest_4_) | copy-start | bytes 1572868
  39.9 18.3 %collective-permute-start.18 = (bf16[4,2,16,2048]{3,2,1,0:T(8,128)(2,1)S(1)}, bf16[4,2,16,2048]{3,2,1,0:T(8,128)(2,1)S(1)}, u32[]{:S(2)}, u32[]{:S(2)}) collective-permute-start(bf16[4,2,16,2048]{3,2,1,0:T(8,128)(2,1)S(1)} %pad_maximum_fusion.3.rest_4_), channel_id=1, source_target_pairs={{0,96},{32,0},{64,32},{96,64},{1,97},{33,1},{65,33},{97,65},{2,98}... | collective-permute-start | bytes 1572872 | tf_op jit(solution)/shard_map/ppermute | solution.py:31
  40.0 18.2 %collective-permute-start.17 = (bf16[4,2,16,2048]{3,2,1,0:T(8,128)(2,1)S(1)}, bf16[4,2,16,2048]{3,2,1,0:T(8,128)(2,1)}, u32[]{:S(2)}, u32[]{:S(2)}) collective-permute-start(bf16[4,2,16,2048]{3,2,1,0:T(8,128)(2,1)S(1)} %pad_maximum_fusion.3.rest_4_), channel_id=1, source_target_pairs={{0,64},{32,96},{64,0},{96,32},{1,65},{33,97},{65,1},{97,33},{2,66}... | collective-permute-start | bytes 1572872 | tf_op jit(solution)/shard_map/ppermute | solution.py:31
  56.3 9.3 %copy-start.6 = (bf16[4,2,16,2048]{3,2,1,0:T(8,128)(2,1)}, bf16[4,2,16,2048]{3,2,1,0:T(8,128)(2,1)S(1)}, u32[]{:S(2)}) copy-start(bf16[4,2,16,2048]{3,2,1,0:T(8,128)(2,1)S(1)} %collective-permute-done.15.rest_3_) | copy-start | bytes 1572868
  56.3 9.3 %collective-permute-start.16 = (bf16[4,2,16,2048]{3,2,1,0:T(8,128)(2,1)S(1)}, bf16[4,2,16,2048]{3,2,1,0:T(8,128)(2,1)}, u32[]{:S(2)}, u32[]{:S(2)}) collective-permute-start(bf16[4,2,16,2048]{3,2,1,0:T(8,128)(2,1)S(1)} %pad_maximum_fusion.3.rest_4_), channel_id=1, source_target_pairs={{0,32},{32,64},{64,96},{96,0},{1,33},{33,65},{65,97},{97,1},{2,34}... | collective-permute-start | bytes 1572872 | tf_op jit(solution)/shard_map/ppermute | solution.py:31
  57.6 8.1 %copy-start.8 = (bf16[4,2,16,2048]{3,2,1,0:T(8,128)(2,1)}, bf16[4,2,16,2048]{3,2,1,0:T(8,128)(2,1)S(1)}, u32[]{:S(2)}) copy-start(bf16[4,2,16,2048]{3,2,1,0:T(8,128)(2,1)S(1)} %collective-permute-done.14.rest_2_) | copy-start | bytes 1572868
  82.8 11.4 %copy-start.24 = (bf16[1,2,16,2048]{3,2,1,0:T(8,128)(2,1)S(1)}, bf16[1,2,16,2048]{3,2,1,0:T(8,128)(2,1)}, u32[]{:S(2)}) copy-start(bf16[1,2,16,2048]{3,2,1,0:T(8,128)(2,1)} %get-tuple-element.6) | copy-start | bytes 393220
  82.8 16.3 %copy-start.20 = (bf16[1,2,16,2048]{3,2,1,0:T(8,128)(2,1)S(1)}, bf16[1,2,16,2048]{3,2,1,0:T(8,128)(2,1)}, u32[]{:S(2)}) copy-start(bf16[1,2,16,2048]{3,2,1,0:T(8,128)(2,1)} %get-tuple-element.18) | copy-start | bytes 393220
  82.9 16.3 %copy-start.21 = (bf16[1,2,16,2048]{3,2,1,0:T(8,128)(2,1)S(1)}, bf16[1,2,16,2048]{3,2,1,0:T(8,128)(2,1)}, u32[]{:S(2)}) copy-start(bf16[1,2,16,2048]{3,2,1,0:T(8,128)(2,1)} %get-tuple-element.16) | copy-start | bytes 393220
  82.9 16.3 %copy-start.22 = (bf16[1,2,16,2048]{3,2,1,0:T(8,128)(2,1)S(1)}, bf16[1,2,16,2048]{3,2,1,0:T(8,128)(2,1)}, u32[]{:S(2)}) copy-start(bf16[1,2,16,2048]{3,2,1,0:T(8,128)(2,1)} %get-tuple-element.14) | copy-start | bytes 393220
  82.9 16.3 %copy-start.23 = (bf16[1,2,16,2048]{3,2,1,0:T(8,128)(2,1)S(1)}, bf16[1,2,16,2048]{3,2,1,0:T(8,128)(2,1)}, u32[]{:S(2)}) copy-start(bf16[1,2,16,2048]{3,2,1,0:T(8,128)(2,1)} %get-tuple-element.7) | copy-start | bytes 393220
  82.9 99.0 %all-to-all-start = ((bf16[32,528,128]{2,1,0:T(8,128)(2,1)}), bf16[32,528,128]{2,1,0:T(8,128)(2,1)}, u32[]{:S(2)}, u32[]{:S(2)}) async-start(bf16[32,528,128]{2,1,0:T(8,128)(2,1)} %shard_map.38), calls=%async_computation | async-start | bytes 8650752 | tf_op jit(solution)/shard_map/all_to_all | solution.py:285
  94.4 73.8 %copy-start.1 = (bf16[4,2,16,2048]{3,2,1,0:T(8,128)(2,1)}, bf16[4,2,16,2048]{3,2,1,0:T(8,128)(2,1)S(1)}, u32[]{:S(2)}) copy-start(bf16[4,2,16,2048]{3,2,1,0:T(8,128)(2,1)S(1)} %pad_maximum_fusion.rest_0_.rest_8_) | copy-start | bytes 1572868
  94.4 56.9 %collective-permute-start.6 = (bf16[4,2,16,2048]{3,2,1,0:T(8,128)(2,1)S(1)}, bf16[4,2,16,2048]{3,2,1,0:T(8,128)(2,1)S(1)}, u32[]{:S(2)}, u32[]{:S(2)}) collective-permute-start(bf16[4,2,16,2048]{3,2,1,0:T(8,128)(2,1)S(1)} %pad_maximum_fusion.rest_0_.rest_8_), channel_id=1, source_target_pairs={{0,24},{8,0},{16,8},{24,16},{1,25},{9,1},{17,9},{25,17},{2,26},{10... | collective-permute-start | bytes 1572872 | tf_op jit(solution)/shard_map/ppermute | solution.py:31
  95.0 68.9 %collective-permute-start.5 = (bf16[4,2,16,2048]{3,2,1,0:T(8,128)(2,1)S(1)}, bf16[4,2,16,2048]{3,2,1,0:T(8,128)(2,1)S(1)}, u32[]{:S(2)}, u32[]{:S(2)}) collective-permute-start(bf16[4,2,16,2048]{3,2,1,0:T(8,128)(2,1)S(1)} %pad_maximum_fusion.rest_0_.rest_8_), channel_id=1, source_target_pairs={{0,16},{8,24},{16,0},{24,8},{1,17},{9,25},{17,1},{25,9},{2,18},{10... | collective-permute-start | bytes 1572872 | tf_op jit(solution)/shard_map/ppermute | solution.py:31
  97.4 69.9 %collective-permute-start.4 = (bf16[4,2,16,2048]{3,2,1,0:T(8,128)(2,1)S(1)}, bf16[4,2,16,2048]{3,2,1,0:T(8,128)(2,1)S(1)}, u32[]{:S(2)}, u32[]{:S(2)}) collective-permute-start(bf16[4,2,16,2048]{3,2,1,0:T(8,128)(2,1)S(1)} %pad_maximum_fusion.rest_0_.rest_8_), channel_id=1, source_target_pairs={{0,8},{8,16},{16,24},{24,0},{1,9},{9,17},{17,25},{25,1},{2,10},{10... | collective-permute-start | bytes 1572872 | tf_op jit(solution)/shard_map/ppermute | solution.py:31
  99.3 68.9 %copy-start.3 = (bf16[4,2,16,2048]{3,2,1,0:T(8,128)(2,1)}, bf16[4,2,16,2048]{3,2,1,0:T(8,128)(2,1)S(1)}, u32[]{:S(2)}) copy-start(bf16[4,2,16,2048]{3,2,1,0:T(8,128)(2,1)S(1)} %pad_maximum_fusion.1.rest_4_.rest_12_) | copy-start | bytes 1572868
  99.3 68.0 %collective-permute-start.12 = (bf16[4,2,16,2048]{3,2,1,0:T(8,128)(2,1)S(1)}, bf16[4,2,16,2048]{3,2,1,0:T(8,128)(2,1)S(1)}, u32[]{:S(2)}, u32[]{:S(2)}) collective-permute-start(bf16[4,2,16,2048]{3,2,1,0:T(8,128)(2,1)S(1)} %pad_maximum_fusion.1.rest_4_.rest_12_), channel_id=1, source_target_pairs={{0,96},{32,0},{64,32},{96,64},{1,97},{33,1},{65,33},{97,65},{2,98}... | collective-permute-start | bytes 1572872 | tf_op jit(solution)/shard_map/ppermute | solution.py:31
  99.9 67.4 %collective-permute-start.11 = (bf16[4,2,16,2048]{3,2,1,0:T(8,128)(2,1)S(1)}, bf16[4,2,16,2048]{3,2,1,0:T(8,128)(2,1)S(1)}, u32[]{:S(2)}, u32[]{:S(2)}) collective-permute-start(bf16[4,2,16,2048]{3,2,1,0:T(8,128)(2,1)S(1)} %pad_maximum_fusion.1.rest_4_.rest_12_), channel_id=1, source_target_pairs={{0,64},{32,96},{64,0},{96,32},{1,65},{33,97},{65,1},{97,33},{2,66}... | collective-permute-start | bytes 1572872 | tf_op jit(solution)/shard_map/ppermute | solution.py:31
  151.2 16.9 %copy-start.5 = (bf16[4,2,16,2048]{3,2,1,0:T(8,128)(2,1)}, bf16[4,2,16,2048]{3,2,1,0:T(8,128)(2,1)S(1)}, u32[]{:S(2)}) copy-start(bf16[4,2,16,2048]{3,2,1,0:T(8,128)(2,1)S(1)} %collective-permute-done.6.rest_3_.rest_11_) | copy-start | bytes 1572868
  151.2 16.9 %collective-permute-start.10 = (bf16[4,2,16,2048]{3,2,1,0:T(8,128)(2,1)S(1)}, bf16[4,2,16,2048]{3,2,1,0:T(8,128)(2,1)}, u32[]{:S(2)}, u32[]{:S(2)}) collective-permute-start(bf16[4,2,16,2048]{3,2,1,0:T(8,128)(2,1)S(1)} %pad_maximum_fusion.1.rest_4_.rest_12_), channel_id=1, source_target_pairs={{0,32},{32,64},{64,96},{96,0},{1,33},{33,65},{65,97},{97,1},{2,34}... | collective-permute-start | bytes 1572872 | tf_op jit(solution)/shard_map/ppermute | solution.py:31
  187.1 5.7 %collective-permute-start.19 = (bf16[512,128]{1,0:T(8,128)(2,1)}, bf16[512,128]{1,0:T(8,128)(2,1)S(1)}, u32[]{:S(2)}, u32[]{:S(2)}) collective-permute-start(bf16[512,128]{1,0:T(8,128)(2,1)} %shard_map.40), channel_id=1, source_target_pairs={{0,4},{4,0},{1,5},{5,1},{2,6},{6,2},{3,7},{7,3},{8,12},{12,8},{9,1... | collective-permute-start | bytes 393224 | tf_op jit(solution)/shard_map/ppermute | solution.py:31
  193.7 6.1 %collective-permute-start.22 = (bf16[2,256,128]{2,1,0:T(8,128)(2,1)S(1)}, bf16[2,256,128]{2,1,0:T(8,128)(2,1)S(1)}, u32[]{:S(2)}, u32[]{:S(2)}) collective-permute-start(bf16[2,256,128]{2,1,0:T(8,128)(2,1)S(1)} %get-tuple-element.12), channel_id=1, source_target_pairs={{0,96},{32,0},{64,32},{96,64},{1,97},{33,1},{65,33},{97,65},{2,98}... | collective-permute-start | bytes 393224 | tf_op jit(solution)/shard_map/ppermute | solution.py:31
  196.4 6.6 %collective-permute-start.21 = (bf16[2,256,128]{2,1,0:T(8,128)(2,1)S(1)}, bf16[2,256,128]{2,1,0:T(8,128)(2,1)S(1)}, u32[]{:S(2)}, u32[]{:S(2)}) collective-permute-start(bf16[2,256,128]{2,1,0:T(8,128)(2,1)S(1)} %get-tuple-element.12), channel_id=1, source_target_pairs={{0,64},{32,96},{64,0},{96,32},{1,65},{33,97},{65,1},{97,33},{2,66}... | collective-permute-start | bytes 393224 | tf_op jit(solution)/shard_map/ppermute | solution.py:31
  198.4 5.9 %collective-permute-start.20 = (bf16[2,256,128]{2,1,0:T(8,128)(2,1)S(1)}, bf16[2,256,128]{2,1,0:T(8,128)(2,1)S(1)}, u32[]{:S(2)}, u32[]{:S(2)}) collective-permute-start(bf16[2,256,128]{2,1,0:T(8,128)(2,1)S(1)} %get-tuple-element.12), channel_id=1, source_target_pairs={{0,32},{32,64},{64,96},{96,0},{1,33},{33,65},{65,97},{97,1},{2,34}... | collective-permute-start | bytes 393224 | tf_op jit(solution)/shard_map/ppermute | solution.py:31
  204.4 47.6 %copy-start.14 = (bf16[4,2,256,128]{3,2,1,0:T(8,128)(2,1)}, bf16[4,2,256,128]{3,2,1,0:T(8,128)(2,1)S(1)}, u32[]{:S(2)}) copy-start(bf16[4,2,256,128]{3,2,1,0:T(8,128)(2,1)S(1)} %pad_maximum_fusion.4.rest_0_) | copy-start | bytes 1572868
  204.4 28.8 %collective-permute-start.25 = (bf16[4,2,256,128]{3,2,1,0:T(8,128)(2,1)S(1)}, bf16[4,2,256,128]{3,2,1,0:T(8,128)(2,1)S(1)}, u32[]{:S(2)}, u32[]{:S(2)}) collective-permute-start(bf16[4,2,256,128]{3,2,1,0:T(8,128)(2,1)S(1)} %pad_maximum_fusion.4.rest_0_), channel_id=1, source_target_pairs={{0,24},{8,0},{16,8},{24,16},{1,25},{9,1},{17,9},{25,17},{2,26},{10... | collective-permute-start | bytes 1572872 | tf_op jit(solution)/shard_map/ppermute | solution.py:31
  204.5 15.2 %collective-permute-start.27 = (bf16[2,256,128]{2,1,0:T(8,128)(2,1)S(1)}, bf16[2,256,128]{2,1,0:T(8,128)(2,1)S(1)}, u32[]{:S(2)}, u32[]{:S(2)}) collective-permute-start(bf16[2,256,128]{2,1,0:T(8,128)(2,1)S(1)} %get-tuple-element.11), channel_id=1, source_target_pairs={{0,16},{8,24},{16,0},{24,8},{1,17},{9,25},{17,1},{25,9},{2,18},{10... | collective-permute-start | bytes 393224 | tf_op jit(solution)/shard_map/ppermute | solution.py:31
  204.6 15.1 %collective-permute-start.26 = (bf16[2,256,128]{2,1,0:T(8,128)(2,1)S(1)}, bf16[2,256,128]{2,1,0:T(8,128)(2,1)S(1)}, u32[]{:S(2)}, u32[]{:S(2)}) collective-permute-start(bf16[2,256,128]{2,1,0:T(8,128)(2,1)S(1)} %get-tuple-element.11), channel_id=1, source_target_pairs={{0,8},{8,16},{16,24},{24,0},{1,9},{9,17},{17,25},{25,1},{2,10},{10... | collective-permute-start | bytes 393224 | tf_op jit(solution)/shard_map/ppermute | solution.py:31
  206.5 24.3 %collective-permute-start.28 = (bf16[2,256,128]{2,1,0:T(8,128)(2,1)S(1)}, bf16[2,256,128]{2,1,0:T(8,128)(2,1)S(1)}, u32[]{:S(2)}, u32[]{:S(2)}) collective-permute-start(bf16[2,256,128]{2,1,0:T(8,128)(2,1)S(1)} %get-tuple-element.11), channel_id=1, source_target_pairs={{0,24},{8,0},{16,8},{24,16},{1,25},{9,1},{17,9},{25,17},{2,26},{10... | collective-permute-start | bytes 393224 | tf_op jit(solution)/shard_map/ppermute | solution.py:31
  208.6 43.4 %collective-permute-start.24 = (bf16[4,2,256,128]{3,2,1,0:T(8,128)(2,1)S(1)}, bf16[4,2,256,128]{3,2,1,0:T(8,128)(2,1)S(1)}, u32[]{:S(2)}, u32[]{:S(2)}) collective-permute-start(bf16[4,2,256,128]{3,2,1,0:T(8,128)(2,1)S(1)} %pad_maximum_fusion.4.rest_0_), channel_id=1, source_target_pairs={{0,16},{8,24},{16,0},{24,8},{1,17},{9,25},{17,1},{25,9},{2,18},{10... | collective-permute-start | bytes 1572872 | tf_op jit(solution)/shard_map/ppermute | solution.py:31
  219.6 32.4 %collective-permute-start.23 = (bf16[4,2,256,128]{3,2,1,0:T(8,128)(2,1)S(1)}, bf16[4,2,256,128]{3,2,1,0:T(8,128)(2,1)S(1)}, u32[]{:S(2)}, u32[]{:S(2)}) collective-permute-start(bf16[4,2,256,128]{3,2,1,0:T(8,128)(2,1)S(1)} %pad_maximum_fusion.4.rest_0_), channel_id=1, source_target_pairs={{0,8},{8,16},{16,24},{24,0},{1,9},{9,17},{17,25},{25,1},{2,10},{10... | collective-permute-start | bytes 1572872 | tf_op jit(solution)/shard_map/ppermute | solution.py:31
  230.9 21.1 %copy-start.15 = (bf16[4,2,256,128]{3,2,1,0:T(8,128)(2,1)}, bf16[4,2,256,128]{3,2,1,0:T(8,128)(2,1)S(1)}, u32[]{:S(2)}) copy-start(bf16[4,2,256,128]{3,2,1,0:T(8,128)(2,1)S(1)} %pad_maximum_fusion.5.rest_4_) | copy-start | bytes 1572868
  230.9 21.1 %collective-permute-start.31 = (bf16[4,2,256,128]{3,2,1,0:T(8,128)(2,1)S(1)}, bf16[4,2,256,128]{3,2,1,0:T(8,128)(2,1)S(1)}, u32[]{:S(2)}, u32[]{:S(2)}) collective-permute-start(bf16[4,2,256,128]{3,2,1,0:T(8,128)(2,1)S(1)} %pad_maximum_fusion.5.rest_4_), channel_id=1, source_target_pairs={{0,96},{32,0},{64,32},{96,64},{1,97},{33,1},{65,33},{97,65},{2,98}... | collective-permute-start | bytes 1572872 | tf_op jit(solution)/shard_map/ppermute | solution.py:31
  231.7 20.3 %collective-permute-start.30 = (bf16[4,2,256,128]{3,2,1,0:T(8,128)(2,1)S(1)}, bf16[4,2,256,128]{3,2,1,0:T(8,128)(2,1)}, u32[]{:S(2)}, u32[]{:S(2)}) collective-permute-start(bf16[4,2,256,128]{3,2,1,0:T(8,128)(2,1)S(1)} %pad_maximum_fusion.5.rest_4_), channel_id=1, source_target_pairs={{0,64},{32,96},{64,0},{96,32},{1,65},{33,97},{65,1},{97,33},{2,66}... | collective-permute-start | bytes 1572872 | tf_op jit(solution)/shard_map/ppermute | solution.py:31
  233.2 18.8 %copy-start.16 = (bf16[4,2,256,128]{3,2,1,0:T(8,128)(2,1)}, bf16[4,2,256,128]{3,2,1,0:T(8,128)(2,1)S(1)}, u32[]{:S(2)}) copy-start(bf16[4,2,256,128]{3,2,1,0:T(8,128)(2,1)S(1)} %collective-permute-done.25.rest_3_) | copy-start | bytes 1572868
  233.2 18.9 %collective-permute-start.29 = (bf16[4,2,256,128]{3,2,1,0:T(8,128)(2,1)S(1)}, bf16[4,2,256,128]{3,2,1,0:T(8,128)(2,1)}, u32[]{:S(2)}, u32[]{:S(2)}) collective-permute-start(bf16[4,2,256,128]{3,2,1,0:T(8,128)(2,1)S(1)} %pad_maximum_fusion.5.rest_4_), channel_id=1, source_target_pairs={{0,32},{32,64},{64,96},{96,0},{1,33},{33,65},{65,97},{97,1},{2,34}... | collective-permute-start | bytes 1572872 | tf_op jit(solution)/shard_map/ppermute | solution.py:31
  (10 other events, 28.7 us)

commit v2 on v1

--- a/solution.py
+++ b/solution.py
@@ -1,3 +1,4 @@
+import functools
 import math
 
 import jax
@@ -40,10 +41,12 @@
     return [own, one, two, three]
 
 
-def gather_first(v):
+def gather_rows(v):
     both = jnp.stack([v, shifted(v, "y", 1)])
     half = both.shape[-1] // 2
-    return (in_slots(ring(both[..., :half], "x")), in_slots(ring(both[..., half:], "z")))
+    a = jnp.stack(in_slots(ring(both[..., :half], "x")))
+    b = jnp.stack(in_slots(ring(both[..., half:], "z")))
+    return in_slots(ring(a, "z")), in_slots(ring(b, "x"))
 
 
 def place(pos, slot_x, slot_z, slot_y):
@@ -215,27 +218,69 @@
         out[...] = acc[...].astype(BF16)
 
 
-def final_kernel(pos, weights, *rest):
-    pieces, (out, prod) = rest[:8], rest[8:]
-    g = pl.program_id(0)
-    half = M // 2
-
-    @pl.when(g == 0)
-    def _():
-        for slot_x in range(4):
-            for slot_z in range(4):
-                for slot_y in range(2):
-                    at = (slot_x * 4 + slot_z) * 2 + slot_y
-                    prod[at, :half] = pieces[slot_z][slot_x, slot_y]
-                    prod[at, half:] = pieces[4 + slot_x][slot_z, slot_y]
-
-    for j in range(LAST):
-        head = g * LAST + j
-        jx, jz, jy = head // 8, (head // 2) % 4, head % 2
-        slot_x, slot_z = (pos[0] + 4 - jx) % 4, (pos[1] + 4 - jz) % 4
-        at = (slot_x * 4 + slot_z) * 2 + (pos[2] + jy) % 2
-        both = jnp.dot(weights[j], prod[at], preferred_element_type=F32)
-        out[:, j * DH : (j + 1) * DH] = both.astype(BF16)
+def final_kernel(shifts, pos, weights, *rest):
+    n = LAST * len(shifts)
+    given = rest[: 2 * len(shifts)]
+    out, tiles, results, prods, sems_in, sems_out, sems_prod = rest[-7:]
+    heads = []
+    for shift in shifts:
+        x, z = (pos[0] + 4 - shift) % 4, (pos[1] + 4 - shift) % 4
+        heads += [(((pos[0] + 4 - early) % 4) * 4 + z) * 2 for early in range(4)]
+        heads += [(x * 4 + (pos[1] + 4 - early) % 4) * 2 + 1 for early in range(4)]
+    pieces = [
+        pltpu.make_async_copy(piece, prods.at[i], sems_prod.at[i]) for i, piece in enumerate(given)
+    ]
+    into = [
+        pltpu.make_async_copy(weights.at[h], tiles.at[i], sems_in.at[i]) for i, h in enumerate(heads)
+    ]
+    back = [
+        pltpu.make_async_copy(
+            results.at[i],
+            out.at[:, pl.ds(pl.multiple_of(h * DH, DH), DH)],
+            sems_out.at[i],
+        )
+        for i, h in enumerate(heads)
+    ]
+    for copy in pieces + into:
+        copy.start()
+    for copy in pieces:
+        copy.wait()
+    for first in range(0, n, 4):
+        for i in range(first, first + 4):
+            into[i].wait()
+        held = None
+        for i in range(first, first + 4):
+            both = jnp.dot(tiles[i], prods[i // 4, i % 4], preferred_element_type=F32)
+            if held is not None:
+                results[i - 1] = held.astype(BF16)
+            held = both
+        results[first + 3] = held.astype(BF16)
+        for i in range(first, first + 4):
+            back[i].start()
+    for copy in back:
+        copy.wait()
+
+
+def final(shifts, pos, weights, pieces, *out):
+    anywhere = pl.BlockSpec(memory_space=pl.ANY)
+    here = weights.shape[1]
+    n = LAST * len(shifts)
+    return pl.pallas_call(
+        functools.partial(final_kernel, shifts),
+        in_specs=[pl.BlockSpec(memory_space=pltpu.SMEM)]
+        + [anywhere] * (1 + len(pieces) + len(out)),
+        out_specs=anywhere,
+        out_shape=jax.ShapeDtypeStruct((here, D), BF16),
+        scratch_shapes=[
+            pltpu.VMEM((n, here, M), BF16),
+            pltpu.VMEM((n, here, DH), BF16),
+            pltpu.VMEM((len(pieces), 4, M, DH), BF16),
+            pltpu.SemaphoreType.DMA((n,)),
+            pltpu.SemaphoreType.DMA((n,)),
+            pltpu.SemaphoreType.DMA((len(pieces),)),
+        ],
+        input_output_aliases={2 + len(pieces): 0} if out else {},
+    )(pos, weights, *pieces, *out)
 
 
 def call(kernel, grid, in_specs, out_spec, out_shape, scratch, prefetch=1):
@@ -263,12 +308,8 @@
     pos = jnp.stack([lax.axis_index(a) for a in SEQ]).astype(jnp.int32)
     here = queries.shape[0]
     per_device = M // 32
-    means = jnp.stack([landmarks(queries, per_device), landmarks(keys, per_device)])
-    first_a, first_b = gather_first(means)
-    q_a = in_slots(ring(jnp.stack([p[:, 0] for p in first_a]), "z"))
-    q_b = in_slots(ring(jnp.stack([p[:, 0] for p in first_b]), "x"))
-    k_a = in_slots(ring(jnp.stack([p[:, 1] for p in first_a]), "z"))
-    k_b = in_slots(ring(jnp.stack([p[:, 1] for p in first_b]), "x"))
+    q_a, q_b = gather_rows(landmarks(queries, per_device))
+    k_a, k_b = gather_rows(landmarks(keys, per_device))
 
     column = pl.BlockSpec((here, GROUP * DH), lambda h, pos: (0, h))
     per_head = piece_specs(lambda h, pos: h, GROUP)
@@ -317,21 +358,18 @@
         prefetch=0,
     )(parts, parts, inverse)
 
-    both = jnp.stack([product, shifted(product, "y", 1)])
-    half = M // 2
-    p_a = in_slots(ring(jnp.stack(in_slots(ring(both[:, :half], "x"))), "z"))
-    p_b = in_slots(ring(jnp.stack(in_slots(ring(both[:, half:], "z"))), "x"))
-
-    whole = pl.BlockSpec((4, 2, half, DH), lambda g, pos: (0, 0, 0, 0))
-
-    return call(
-        final_kernel,
-        (H // LAST,),
-        [pl.BlockSpec((LAST, here, M), lambda g, pos: (g, 0, 0))] + [whole] * 8,
-        pl.BlockSpec((here, LAST * DH), lambda g, pos: (0, g)),
-        jax.ShapeDtypeStruct((here, D), BF16),
-        [pltpu.VMEM((H, M, DH), BF16)],
-    )(pos, weights, *p_a, *p_b)
+    other = shifted(product, "y", 1)
+    lower = pos[2] == 0
+    a = jnp.where(lower, product, other)
+    b = jnp.where(lower, other, product)
+    a = jnp.stack(in_slots(ring(a, "x")))
+    b = jnp.stack(in_slots(ring(b, "z")))
+    out = final((0,), pos, weights, [a, b])
+    pieces = {}
+    for s in (1, 3, 2):
+        pieces[s] = [shifted(a, "z", s), shifted(b, "x", s)]
+    out = final((1,), pos, weights, pieces[1], out)
+    return final((3, 2), pos, weights, pieces[3] + pieces[2], out)
 
 
 def solution(mesh):

time: 266 us -> 294 us (1.11)
  the two profiles are of different devices: /device:TPU:60 before, /device:TPU:0 now
where the time goes in v2:
time: 294 us; the launch traced here: 292 us
  waiting for transfers between devices  134 us (46%)
  starting transfers between devices  75.8 us (26%)
  Pallas kernels  71.3 us (24%)
  other arithmetic  8.64 us (3%)
    ppermute x39, waiting for transfers between devices, shifted(): return lax.ppermute(v, axis, [(i, (i + by) % n) for i in range(n)])  134 us
    ppermute x39, starting transfers between devices, shifted(): return lax.ppermute(v, axis, [(i, (i + by) % n) for i in range(n)])  66.1 us
    pallas_call x3, Pallas kernels, final(): pl.pallas_call(functools.partial(final_kernel, shifts), in_specs=[pl.Bloc...  19.2 us
    pallas_call x1, Pallas kernels, steps(): call(parts_kernel, (H // GROUP,), [column, column] + per_head, pl.BlockSp...  17.2 us
    pallas_call x1, Pallas kernels, steps(): call(near_kernel, (H // GROUP,), [column] + per_head, pl.BlockSpec((GROUP...  16.3 us
    pallas_call x1, Pallas kernels, steps(): call(inverse_kernel, (1,), owned + owned, pl.BlockSpec((M, M), lambda g,...  13.4 us
    all_to_all x1, starting transfers between devices, steps(): parts = lax.all_to_all(parts, SEQ, split_axis=0, concat_axis=0, tiled=True)  9.69 us
    reduce_sum x2, other arithmetic, landmarks(): sums = jnp.sum(tokens.reshape(per_device, segment, D), axis=1, dtype=F32)  6.61 us
  transfers between devices with their start and end apart: 40, of which 25 were waited for; matrix products, arithmetic and copies ran while one was open for 1% of the time, Pallas kernels for 14%

profile of v2, /device:TPU:0, one launch (start us, length us, event | category | flops | bytes accessed | tf_op | source)
XLA Modules:
  0.0 292.0 jit_solution(12726938011363630645)
XLA Ops:
  0.0 3.3 %convert_reduce_fusion = f32[16,4096]{1,0:T(8,128)S(1)} fusion(bf16[512,4096]{1,0:T(8,128)(2,1)} %queries.1), kind=kLoop, calls=%fused_computation | loop fusion | flops 4128768 | bytes 4456448 | tf_op jit(solution)/shard_map/reduce_sum | solution.py:303
  3.3 1.8 collective-permute-start.13
  5.1 3.5 %collective-permute-done.13 = bf16[16,4096]{1,0:T(8,128)(2,1)S(1)} collective-permute-done((bf16[16,4096]{1,0:T(8,128)(2,1)S(1)}, bf16[16,4096]{1,0:T(8,128)(2,1)S(1)}, u32[]{:S(2)}, u32[]{:S(2)}) %collective-permute-start.13) | collective-permute-done | bytes 131104 | tf_op jit(solution)/shard_map/ppermute | solution.py:32
  10.3 2.7 collective-permute-start.15
  16.3 2.0 collective-permute-done.15
  18.4 2.0 collective-permute-start.17
  20.4 1.9 collective-permute-start.20
  24.0 2.5 collective-permute-start.22
  26.6 10.6 %collective-permute-done.20 = bf16[2,16,2048]{2,1,0:T(8,128)(2,1)S(1)} collective-permute-done((bf16[2,16,2048]{2,1,0:T(8,128)(2,1)S(1)}, bf16[2,16,2048]{2,1,0:T(8,128)(2,1)S(1)}, u32[]{:S(2)}, u32[]{:S(2)}) %collective-permute-start.20) | collective-permute-done | bytes 131104 | tf_op jit(solution)/shard_map/ppermute | solution.py:32
  37.2 2.9 collective-permute-start.19
  40.1 2.2 collective-permute-done.21
  43.8 2.9 collective-permute-start.24
  48.3 2.5 collective-permute-done.18.rest_2_
  50.9 5.1 %collective-permute-done.19.rest_3_ = bf16[4,2,16,2048]{3,2,1,0:T(8,128)(2,1)S(1)} collective-permute-done((bf16[4,2,16,2048]{3,2,1,0:T(8,128)(2,1)S(1)}, bf16[4,2,16,2048]{3,2,1,0:T(8,128)(2,1)S(1)}, u32[]{:S(2)}, u32[]{:S(2)}) %collective-permute-start.19) | collective-permute-done | bytes 524320 | tf_op jit(solution)/shard_map/ppermute | solution.py:32
  55.9 2.5 collective-permute-done.23.rest_5_
  58.4 5.7 %collective-permute-done.24.rest_6_ = bf16[4,2,16,2048]{3,2,1,0:T(8,128)(2,1)} collective-permute-done((bf16[4,2,16,2048]{3,2,1,0:T(8,128)(2,1)S(1)}, bf16[4,2,16,2048]{3,2,1,0:T(8,128)(2,1)}, u32[]{:S(2)}, u32[]{:S(2)}) %collective-permute-start.24) | collective-permute-done | bytes 524320 | tf_op jit(solution)/shard_map/ppermute | solution.py:32
  64.2 17.2 %shard_map.38 = bf16[32,528,128]{2,1,0:T(8,128)(2,1)} custom-call(s32[3]{0:T(128)} %pad_add_fusion.pos, bf16[512,4096]{1,0:T(8,128)(2,1)} %keys.1, bf16[512,4096]{1,0:T(8,128)(2,1)} %values.1, bf16[4,2,16,2048]{3,2,1,0:T(8,128)(2,1)} %copy-done, bf16[4,2,16,2048]{3,2,1,0:T(8,128)(2,1)} %copy-done.4, bf16[4,2,16,2048]{3,2,1,0:T(8,128)(2,1)} %copy-done.5, ...), custom_call_target="tpu_custom_call" | custom-call | tf_op jit(solution)/shard_map/pallas_call | solution.py:318
  81.4 9.7 %all-to-all-start = ((bf16[32,528,128]{2,1,0:T(8,128)(2,1)}), bf16[32,528,128]{2,1,0:T(8,128)(2,1)}, u32[]{:S(2)}, u32[]{:S(2)}) async-start(bf16[32,528,128]{2,1,0:T(8,128)(2,1)} %shard_map.38), calls=%async_computation | async-start | bytes 8650752 | tf_op jit(solution)/shard_map/all_to_all | solution.py:326
  91.1 3.3 %convert_reduce_fusion.1 = f32[16,4096]{1,0:T(8,128)S(1)} fusion(bf16[512,4096]{1,0:T(8,128)(2,1)} %keys.1), kind=kLoop, calls=%fused_computation.1 | loop fusion | flops 4128768 | bytes 4456448 | tf_op jit(solution)/shard_map/reduce_sum | solution.py:303
  94.4 1.8 collective-permute-start
  96.3 43.6 %collective-permute-done = bf16[16,4096]{1,0:T(8,128)(2,1)S(1)} collective-permute-done((bf16[16,4096]{1,0:T(8,128)(2,1)S(1)}, bf16[16,4096]{1,0:T(8,128)(2,1)S(1)}, u32[]{:S(2)}, u32[]{:S(2)}) %collective-permute-start) | collective-permute-done | bytes 131104 | tf_op jit(solution)/shard_map/ppermute | solution.py:32
  139.9 4.7 %collective-permute-start.8 = (bf16[2,16,2048]{2,1,0:T(8,128)(2,1)S(1)}, bf16[2,16,2048]{2,1,0:T(8,128)(2,1)S(1)}, u32[]{:S(2)}, u32[]{:S(2)}) collective-permute-start(bf16[2,16,2048]{2,1,0:T(8,128)(2,1)S(1)} %get-tuple-element.9), channel_id=1, source_target_pairs={{0,16},{8,24},{16,0},{24,8},{1,17},{9,25},{17,1},{25,9},{2,18},{10... | collective-permute-start | bytes 393224 | tf_op jit(solution)/shard_map/ppermute | solution.py:32
  144.7 2.4 collective-permute-done.7
  147.1 1.9 collective-permute-done.8
  149.7 3.7 %collective-permute-start.10 = (bf16[4,2,16,2048]{3,2,1,0:T(8,128)(2,1)S(1)}, bf16[4,2,16,2048]{3,2,1,0:T(8,128)(2,1)S(1)}, u32[]{:S(2)}, u32[]{:S(2)}) collective-permute-start(bf16[4,2,16,2048]{3,2,1,0:T(8,128)(2,1)S(1)} %pad_maximum_fusion.1.rest_4_.rest_12_), channel_id=1, source_target_pairs={{0,32},{32,64},{64,96},{96,0},{1,33},{33,65},{65,97},{97,1},{2,34}... | collective-permute-start | bytes 1572872 | tf_op jit(solution)/shard_map/ppermute | solution.py:32
  154.5 2.2 collective-permute-start.3
  156.7 2.9 %collective-permute-start.11 = (bf16[4,2,16,2048]{3,2,1,0:T(8,128)(2,1)S(1)}, bf16[4,2,16,2048]{3,2,1,0:T(8,128)(2,1)S(1)}, u32[]{:S(2)}, u32[]{:S(2)}) collective-permute-start(bf16[4,2,16,2048]{3,2,1,0:T(8,128)(2,1)S(1)} %pad_maximum_fusion.1.rest_4_.rest_12_), channel_id=1, source_target_pairs={{0,64},{32,96},{64,0},{96,32},{1,65},{33,97},{65,1},{97,33},{2,66}... | collective-permute-start | bytes 1572872 | tf_op jit(solution)/shard_map/ppermute | solution.py:32
  159.6 9.0 %collective-permute-done.1 = bf16[2,16,2048]{2,1,0:T(8,128)(2,1)S(1)} collective-permute-done((bf16[2,16,2048]{2,1,0:T(8,128)(2,1)S(1)}, bf16[2,16,2048]{2,1,0:T(8,128)(2,1)S(1)}, u32[]{:S(2)}, u32[]{:S(2)}) %collective-permute-start.1) | collective-permute-done | bytes 131104 | tf_op jit(solution)/shard_map/ppermute | solution.py:32
  170.0 2.2 collective-permute-done.2
  172.4 2.2 collective-permute-start.4
  174.6 2.6 collective-permute-start.5
  178.3 3.0 %collective-permute-done.11.rest_6_.rest_14_ = bf16[4,2,16,2048]{3,2,1,0:T(8,128)(2,1)S(1)} collective-permute-done((bf16[4,2,16,2048]{3,2,1,0:T(8,128)(2,1)S(1)}, bf16[4,2,16,2048]{3,2,1,0:T(8,128)(2,1)S(1)}, u32[]{:S(2)}, u32[]{:S(2)}) %collective-permute-start.11) | collective-permute-done | bytes 524320 | tf_op jit(solution)/shard_map/ppermute | solution.py:32
  182.9 4.7 %collective-permute-done.4.rest_1_.rest_9_ = bf16[4,2,16,2048]{3,2,1,0:T(8,128)(2,1)S(1)} collective-permute-done((bf16[4,2,16,2048]{3,2,1,0:T(8,128)(2,1)S(1)}, bf16[4,2,16,2048]{3,2,1,0:T(8,128)(2,1)S(1)}, u32[]{:S(2)}, u32[]{:S(2)}) %collective-permute-start.4) | collective-permute-done | bytes 524320 | tf_op jit(solution)/shard_map/ppermute | solution.py:32
  187.6 9.2 %collective-permute-done.5.rest_2_.rest_10_ = bf16[4,2,16,2048]{3,2,1,0:T(8,128)(2,1)S(1)} collective-permute-done((bf16[4,2,16,2048]{3,2,1,0:T(8,128)(2,1)S(1)}, bf16[4,2,16,2048]{3,2,1,0:T(8,128)(2,1)S(1)}, u32[]{:S(2)}, u32[]{:S(2)}) %collective-permute-start.5) | collective-permute-done | bytes 524320 | tf_op jit(solution)/shard_map/ppermute | solution.py:32
  197.7 13.4 %shard_map.39.inverse = bf16[512,512]{1,0:T(8,128)(2,1)} custom-call(s32[3]{0:T(128)} %pad_add_fusion.pos, bf16[4,2,16,2048]{3,2,1,0:T(8,128)(2,1)} %copy-done, bf16[4,2,16,2048]{3,2,1,0:T(8,128)(2,1)} %copy-done.4, bf16[4,2,16,2048]{3,2,1,0:T(8,128)(2,1)} %copy-done.5, bf16[4,2,16,2048]{3,2,1,0:T(8,128)(2,1)} %copy-done.6, ...), custom_call_target="tpu_custom_call" | custom-call | tf_op jit(solution)/shard_map/pallas_call | solution.py:338
  211.1 5.2 %shard_map.40 = bf16[512,128]{1,0:T(8,128)(2,1)} custom-call(bf16[32,528,128]{2,1,0:T(8,128)(2,1)} %all-to-all-done.parts.levels, bf16[32,528,128]{2,1,0:T(8,128)(2,1)} %all-to-all-done.parts.levels, bf16[512,512]{1,0:T(8,128)(2,1)} %shard_map.39.inverse), custom_call_target="tpu_custom_call" | custom-call | tf_op jit(solution)/shard_map/pallas_call | solution.py:347
  217.5 4.0 %collective-permute-done.26 = bf16[512,128]{1,0:T(8,128)(2,1)S(1)} collective-permute-done((bf16[512,128]{1,0:T(8,128)(2,1)}, bf16[512,128]{1,0:T(8,128)(2,1)S(1)}, u32[]{:S(2)}, u32[]{:S(2)}) %collective-permute-start.26) | collective-permute-done | bytes 131104 | tf_op jit(solution)/shard_map/ppermute | solution.py:32
  223.3 2.6 collective-permute-start.32
  226.9 2.8 collective-permute-done.31
  231.6 2.5 collective-permute-start.27
  234.0 2.1 collective-permute-start.28
  236.2 2.5 collective-permute-start.29
  238.7 11.3 %collective-permute-done.27 = bf16[512,128]{1,0:T(8,128)(2,1)S(1)} collective-permute-done((bf16[512,128]{1,0:T(8,128)(2,1)S(1)}, bf16[512,128]{1,0:T(8,128)(2,1)S(1)}, u32[]{:S(2)}, u32[]{:S(2)}) %collective-permute-start.27) | collective-permute-done | bytes 131104 | tf_op jit(solution)/shard_map/ppermute | solution.py:32
  250.9 3.1 %collective-permute-start.30 = (bf16[4,512,128]{2,1,0:T(8,128)(2,1)S(1)}, bf16[4,512,128]{2,1,0:T(8,128)(2,1)S(1)}, u32[]{:S(2)}, u32[]{:S(2)}) collective-permute-start(bf16[4,512,128]{2,1,0:T(8,128)(2,1)S(1)} %pad_maximum_fusion.4.rest_0_), channel_id=1, source_target_pairs={{0,24},{8,0},{16,8},{24,16},{1,25},{9,1},{17,9},{25,17},{2,26},{10... | collective-permute-start | bytes 1572872 | tf_op jit(solution)/shard_map/ppermute | solution.py:32
  255.1 16.3 %shard_map.37.weights = bf16[32,512,512]{2,1,0:T(8,128)(2,1)} custom-call(s32[3]{0:T(128)} %pad_add_fusion.pos, bf16[512,4096]{1,0:T(8,128)(2,1)} %queries.1, bf16[4,2,16,2048]{3,2,1,0:T(8,128)(2,1)} %copy-done.3, bf16[4,2,16,2048]{3,2,1,0:T(8,128)(2,1)} %copy-done.11, bf16[4,2,16,2048]{3,2,1,0:T(8,128)(2,1)} %copy-done.12, ...), custom_call_target="tpu_custom_call" | custom-call | tf_op jit(solution)/shard_map/pallas_call | solution.py:328
  271.4 5.4 %shard_map.41.rest_2_ = bf16[512,4096]{1,0:T(8,128)(2,1)} custom-call(s32[3]{0:T(128)} %pad_add_fusion.pos, bf16[32,512,512]{2,1,0:T(8,128)(2,1)} %shard_map.37.weights, bf16[4,512,128]{2,1,0:T(8,128)(2,1)} %copy-done.14, bf16[4,512,128]{2,1,0:T(8,128)(2,1)} %copy-done.13), custom_call_target="tpu_custom_call" | custom-call | tf_op jit(solution)/shard_map/pallas_call | solution.py:268
  276.8 5.4 %shard_map.42.rest_4_ = bf16[512,4096]{1,0:T(8,128)(2,1)} custom-call(s32[3]{0:T(128)} %pad_add_fusion.pos, bf16[32,512,512]{2,1,0:T(8,128)(2,1)} %shard_map.37.weights, bf16[4,512,128]{2,1,0:T(8,128)(2,1)} %collective-permute-done.37.rest_0_, bf16[4,512,128]{2,1,0:T(8,128)(2,1)} %copy-done.15, ...), custom_call_target="tpu_custom_call", output_to_operand_aliasing={{}: (4, {})} | custom-call | tf_op jit(solution)/shard_map/pallas_call | solution.py:268
  283.3 8.5 %shard_map.43 = bf16[512,4096]{1,0:T(8,128)(2,1)} custom-call(s32[3]{0:T(128)} %pad_add_fusion.pos, bf16[32,512,512]{2,1,0:T(8,128)(2,1)} %shard_map.37.weights, bf16[4,512,128]{2,1,0:T(8,128)(2,1)} %copy-done.18, bf16[4,512,128]{2,1,0:T(8,128)(2,1)} %copy-done.16, ...), custom_call_target="tpu_custom_call", output_to_operand_aliasing={{}: (6, {})} | custom-call | tf_op jit(solution)/shard_map/pallas_call | solution.py:268
  (93 shorter events, 26.0 us)
Async XLA Ops:
  3.3 5.3 %collective-permute-start.13 = (bf16[16,4096]{1,0:T(8,128)(2,1)S(1)}, bf16[16,4096]{1,0:T(8,128)(2,1)S(1)}, u32[]{:S(2)}, u32[]{:S(2)}) collective-permute-start(bf16[16,4096]{1,0:T(8,128)(2,1)S(1)} %multiply_convert_fusion), channel_id=1, source_target_pairs={{0,4},{4,0},{1,5},{5,1},{2,6},{6,2},{3,7},{7,3},{8,12},{12,8},{9,1... | collective-permute-start | bytes 393224 | tf_op jit(solution)/shard_map/ppermute | solution.py:32
  8.6 7.7 %collective-permute-start.14 = (bf16[2,16,2048]{2,1,0:T(8,128)(2,1)S(1)}, bf16[2,16,2048]{2,1,0:T(8,128)(2,1)S(1)}, u32[]{:S(2)}, u32[]{:S(2)}) collective-permute-start(bf16[2,16,2048]{2,1,0:T(8,128)(2,1)S(1)} %get-tuple-element.8), channel_id=1, source_target_pairs={{0,32},{32,64},{64,96},{96,0},{1,33},{33,65},{65,97},{97,1},{2,34}... | collective-permute-start | bytes 393224 | tf_op jit(solution)/shard_map/ppermute | solution.py:32
  10.3 7.9 %collective-permute-start.15 = (bf16[2,16,2048]{2,1,0:T(8,128)(2,1)S(1)}, bf16[2,16,2048]{2,1,0:T(8,128)(2,1)S(1)}, u32[]{:S(2)}, u32[]{:S(2)}) collective-permute-start(bf16[2,16,2048]{2,1,0:T(8,128)(2,1)S(1)} %get-tuple-element.8), channel_id=1, source_target_pairs={{0,64},{32,96},{64,0},{96,32},{1,65},{33,97},{65,1},{97,33},{2,66}... | collective-permute-start | bytes 393224 | tf_op jit(solution)/shard_map/ppermute | solution.py:32
  13.1 5.2 %collective-permute-start.16 = (bf16[2,16,2048]{2,1,0:T(8,128)(2,1)S(1)}, bf16[2,16,2048]{2,1,0:T(8,128)(2,1)S(1)}, u32[]{:S(2)}, u32[]{:S(2)}) collective-permute-start(bf16[2,16,2048]{2,1,0:T(8,128)(2,1)S(1)} %get-tuple-element.8), channel_id=1, source_target_pairs={{0,96},{32,0},{64,32},{96,64},{1,97},{33,1},{65,33},{97,65},{2,98}... | collective-permute-start | bytes 393224 | tf_op jit(solution)/shard_map/ppermute | solution.py:32
  18.4 45.8 %copy-start = (bf16[4,2,16,2048]{3,2,1,0:T(8,128)(2,1)}, bf16[4,2,16,2048]{3,2,1,0:T(8,128)(2,1)S(1)}, u32[]{:S(2)}) copy-start(bf16[4,2,16,2048]{3,2,1,0:T(8,128)(2,1)S(1)} %pad_maximum_fusion.2.rest_0_) | copy-start | bytes 1572868
  18.4 28.2 %collective-permute-start.17 = (bf16[4,2,16,2048]{3,2,1,0:T(8,128)(2,1)S(1)}, bf16[4,2,16,2048]{3,2,1,0:T(8,128)(2,1)S(1)}, u32[]{:S(2)}, u32[]{:S(2)}) collective-permute-start(bf16[4,2,16,2048]{3,2,1,0:T(8,128)(2,1)S(1)} %pad_maximum_fusion.2.rest_0_), channel_id=1, source_target_pairs={{0,8},{8,16},{16,24},{24,0},{1,9},{9,17},{17,25},{25,1},{2,10},{10... | collective-permute-start | bytes 1572872 | tf_op jit(solution)/shard_map/ppermute | solution.py:32
  20.4 16.8 %collective-permute-start.20 = (bf16[2,16,2048]{2,1,0:T(8,128)(2,1)S(1)}, bf16[2,16,2048]{2,1,0:T(8,128)(2,1)S(1)}, u32[]{:S(2)}, u32[]{:S(2)}) collective-permute-start(bf16[2,16,2048]{2,1,0:T(8,128)(2,1)S(1)} %get-tuple-element.7), channel_id=1, source_target_pairs={{0,8},{8,16},{16,24},{24,0},{1,9},{9,17},{17,25},{25,1},{2,10},{10... | collective-permute-start | bytes 393224 | tf_op jit(solution)/shard_map/ppermute | solution.py:32
  22.3 20.0 %collective-permute-start.21 = (bf16[2,16,2048]{2,1,0:T(8,128)(2,1)S(1)}, bf16[2,16,2048]{2,1,0:T(8,128)(2,1)S(1)}, u32[]{:S(2)}, u32[]{:S(2)}) collective-permute-start(bf16[2,16,2048]{2,1,0:T(8,128)(2,1)S(1)} %get-tuple-element.7), channel_id=1, source_target_pairs={{0,16},{8,24},{16,0},{24,8},{1,17},{9,25},{17,1},{25,9},{2,18},{10... | collective-permute-start | bytes 393224 | tf_op jit(solution)/shard_map/ppermute | solution.py:32
  24.0 18.3 %collective-permute-start.22 = (bf16[2,16,2048]{2,1,0:T(8,128)(2,1)S(1)}, bf16[2,16,2048]{2,1,0:T(8,128)(2,1)S(1)}, u32[]{:S(2)}, u32[]{:S(2)}) collective-permute-start(bf16[2,16,2048]{2,1,0:T(8,128)(2,1)S(1)} %get-tuple-element.7), channel_id=1, source_target_pairs={{0,24},{8,0},{16,8},{24,16},{1,25},{9,1},{17,9},{25,17},{2,26},{10... | collective-permute-start | bytes 393224 | tf_op jit(solution)/shard_map/ppermute | solution.py:32
  26.6 24.3 %collective-permute-start.18 = (bf16[4,2,16,2048]{3,2,1,0:T(8,128)(2,1)S(1)}, bf16[4,2,16,2048]{3,2,1,0:T(8,128)(2,1)S(1)}, u32[]{:S(2)}, u32[]{:S(2)}) collective-permute-start(bf16[4,2,16,2048]{3,2,1,0:T(8,128)(2,1)S(1)} %pad_maximum_fusion.2.rest_0_), channel_id=1, source_target_pairs={{0,16},{8,24},{16,0},{24,8},{1,17},{9,25},{17,1},{25,9},{2,18},{10... | collective-permute-start | bytes 1572872 | tf_op jit(solution)/shard_map/ppermute | solution.py:32
  37.2 18.8 %collective-permute-start.19 = (bf16[4,2,16,2048]{3,2,1,0:T(8,128)(2,1)S(1)}, bf16[4,2,16,2048]{3,2,1,0:T(8,128)(2,1)S(1)}, u32[]{:S(2)}, u32[]{:S(2)}) collective-permute-start(bf16[4,2,16,2048]{3,2,1,0:T(8,128)(2,1)S(1)} %pad_maximum_fusion.2.rest_0_), channel_id=1, source_target_pairs={{0,24},{8,0},{16,8},{24,16},{1,25},{9,1},{17,9},{25,17},{2,26},{10... | collective-permute-start | bytes 1572872 | tf_op jit(solution)/shard_map/ppermute | solution.py:32
  42.4 21.8 %copy-start.2 = (bf16[4,2,16,2048]{3,2,1,0:T(8,128)(2,1)}, bf16[4,2,16,2048]{3,2,1,0:T(8,128)(2,1)S(1)}, u32[]{:S(2)}) copy-start(bf16[4,2,16,2048]{3,2,1,0:T(8,128)(2,1)S(1)} %pad_maximum_fusion.3.rest_4_) | copy-start | bytes 1572868
  42.4 16.0 %collective-permute-start.23 = (bf16[4,2,16,2048]{3,2,1,0:T(8,128)(2,1)S(1)}, bf16[4,2,16,2048]{3,2,1,0:T(8,128)(2,1)S(1)}, u32[]{:S(2)}, u32[]{:S(2)}) collective-permute-start(bf16[4,2,16,2048]{3,2,1,0:T(8,128)(2,1)S(1)} %pad_maximum_fusion.3.rest_4_), channel_id=1, source_target_pairs={{0,32},{32,64},{64,96},{96,0},{1,33},{33,65},{65,97},{97,1},{2,34}... | collective-permute-start | bytes 1572872 | tf_op jit(solution)/shard_map/ppermute | solution.py:32
  43.8 20.4 %collective-permute-start.24 = (bf16[4,2,16,2048]{3,2,1,0:T(8,128)(2,1)S(1)}, bf16[4,2,16,2048]{3,2,1,0:T(8,128)(2,1)}, u32[]{:S(2)}, u32[]{:S(2)}) collective-permute-start(bf16[4,2,16,2048]{3,2,1,0:T(8,128)(2,1)S(1)} %pad_maximum_fusion.3.rest_4_), channel_id=1, source_target_pairs={{0,64},{32,96},{64,0},{96,32},{1,65},{33,97},{65,1},{97,33},{2,66}... | collective-permute-start | bytes 1572872 | tf_op jit(solution)/shard_map/ppermute | solution.py:32
  46.6 17.5 %copy-start.4 = (bf16[4,2,16,2048]{3,2,1,0:T(8,128)(2,1)}, bf16[4,2,16,2048]{3,2,1,0:T(8,128)(2,1)S(1)}, u32[]{:S(2)}) copy-start(bf16[4,2,16,2048]{3,2,1,0:T(8,128)(2,1)S(1)} %collective-permute-done.17.rest_1_) | copy-start | bytes 1572868
  46.6 17.5 %collective-permute-start.25 = (bf16[4,2,16,2048]{3,2,1,0:T(8,128)(2,1)S(1)}, bf16[4,2,16,2048]{3,2,1,0:T(8,128)(2,1)}, u32[]{:S(2)}, u32[]{:S(2)}) collective-permute-start(bf16[4,2,16,2048]{3,2,1,0:T(8,128)(2,1)S(1)} %pad_maximum_fusion.3.rest_4_), channel_id=1, source_target_pairs={{0,96},{32,0},{64,32},{96,64},{1,97},{33,1},{65,33},{97,65},{2,98}... | collective-permute-start | bytes 1572872 | tf_op jit(solution)/shard_map/ppermute | solution.py:32
  81.4 129.6 %all-to-all-start = ((bf16[32,528,128]{2,1,0:T(8,128)(2,1)}), bf16[32,528,128]{2,1,0:T(8,128)(2,1)}, u32[]{:S(2)}, u32[]{:S(2)}) async-start(bf16[32,528,128]{2,1,0:T(8,128)(2,1)} %shard_map.38), calls=%async_computation | async-start | bytes 8650752 | tf_op jit(solution)/shard_map/all_to_all | solution.py:326
  94.4 45.4 %collective-permute-start = (bf16[16,4096]{1,0:T(8,128)(2,1)S(1)}, bf16[16,4096]{1,0:T(8,128)(2,1)S(1)}, u32[]{:S(2)}, u32[]{:S(2)}) collective-permute-start(bf16[16,4096]{1,0:T(8,128)(2,1)S(1)} %multiply_convert_fusion.1), channel_id=1, source_target_pairs={{0,4},{4,0},{1,5},{5,1},{2,6},{6,2},{3,7},{7,3},{8,12},{12,8},{9,1... | collective-permute-start | bytes 393224 | tf_op jit(solution)/shard_map/ppermute | solution.py:32
  139.9 7.2 %collective-permute-start.7 = (bf16[2,16,2048]{2,1,0:T(8,128)(2,1)S(1)}, bf16[2,16,2048]{2,1,0:T(8,128)(2,1)S(1)}, u32[]{:S(2)}, u32[]{:S(2)}) collective-permute-start(bf16[2,16,2048]{2,1,0:T(8,128)(2,1)S(1)} %get-tuple-element.9), channel_id=1, source_target_pairs={{0,8},{8,16},{16,24},{24,0},{1,9},{9,17},{17,25},{25,1},{2,10},{10... | collective-permute-start | bytes 393224 | tf_op jit(solution)/shard_map/ppermute | solution.py:32
  139.9 9.0 %collective-permute-start.8 = (bf16[2,16,2048]{2,1,0:T(8,128)(2,1)S(1)}, bf16[2,16,2048]{2,1,0:T(8,128)(2,1)S(1)}, u32[]{:S(2)}, u32[]{:S(2)}) collective-permute-start(bf16[2,16,2048]{2,1,0:T(8,128)(2,1)S(1)} %get-tuple-element.9), channel_id=1, source_target_pairs={{0,16},{8,24},{16,0},{24,8},{1,17},{9,25},{17,1},{25,9},{2,18},{10... | collective-permute-start | bytes 393224 | tf_op jit(solution)/shard_map/ppermute | solution.py:32
  144.6 5.0 %collective-permute-start.9 = (bf16[2,16,2048]{2,1,0:T(8,128)(2,1)S(1)}, bf16[2,16,2048]{2,1,0:T(8,128)(2,1)S(1)}, u32[]{:S(2)}, u32[]{:S(2)}) collective-permute-start(bf16[2,16,2048]{2,1,0:T(8,128)(2,1)S(1)} %get-tuple-element.9), channel_id=1, source_target_pairs={{0,24},{8,0},{16,8},{24,16},{1,25},{9,1},{17,9},{25,17},{2,26},{10... | collective-permute-start | bytes 393224 | tf_op jit(solution)/shard_map/ppermute | solution.py:32
  149.7 47.9 %copy-start.1 = (bf16[4,2,16,2048]{3,2,1,0:T(8,128)(2,1)}, bf16[4,2,16,2048]{3,2,1,0:T(8,128)(2,1)S(1)}, u32[]{:S(2)}) copy-start(bf16[4,2,16,2048]{3,2,1,0:T(8,128)(2,1)S(1)} %pad_maximum_fusion.1.rest_4_.rest_12_) | copy-start | bytes 1572868
  149.7 27.5 %collective-permute-start.10 = (bf16[4,2,16,2048]{3,2,1,0:T(8,128)(2,1)S(1)}, bf16[4,2,16,2048]{3,2,1,0:T(8,128)(2,1)S(1)}, u32[]{:S(2)}, u32[]{:S(2)}) collective-permute-start(bf16[4,2,16,2048]{3,2,1,0:T(8,128)(2,1)S(1)} %pad_maximum_fusion.1.rest_4_.rest_12_), channel_id=1, source_target_pairs={{0,32},{32,64},{64,96},{96,0},{1,33},{33,65},{65,97},{97,1},{2,34}... | collective-permute-start | bytes 1572872 | tf_op jit(solution)/shard_map/ppermute | solution.py:32
  153.4 15.1 %collective-permute-start.1 = (bf16[2,16,2048]{2,1,0:T(8,128)(2,1)S(1)}, bf16[2,16,2048]{2,1,0:T(8,128)(2,1)S(1)}, u32[]{:S(2)}, u32[]{:S(2)}) collective-permute-start(bf16[2,16,2048]{2,1,0:T(8,128)(2,1)S(1)} %get-tuple-element.10), channel_id=1, source_target_pairs={{0,32},{32,64},{64,96},{96,0},{1,33},{33,65},{65,97},{97,1},{2,34}... | collective-permute-start | bytes 393224 | tf_op jit(solution)/shard_map/ppermute | solution.py:32
  153.5 18.8 %collective-permute-start.2 = (bf16[2,16,2048]{2,1,0:T(8,128)(2,1)S(1)}, bf16[2,16,2048]{2,1,0:T(8,128)(2,1)S(1)}, u32[]{:S(2)}, u32[]{:S(2)}) collective-permute-start(bf16[2,16,2048]{2,1,0:T(8,128)(2,1)S(1)} %get-tuple-element.10), channel_id=1, source_target_pairs={{0,64},{32,96},{64,0},{96,32},{1,65},{33,97},{65,1},{97,33},{2,66}... | collective-permute-start | bytes 393224 | tf_op jit(solution)/shard_map/ppermute | solution.py:32
  154.5 17.8 %collective-permute-start.3 = (bf16[2,16,2048]{2,1,0:T(8,128)(2,1)S(1)}, bf16[2,16,2048]{2,1,0:T(8,128)(2,1)S(1)}, u32[]{:S(2)}, u32[]{:S(2)}) collective-permute-start(bf16[2,16,2048]{2,1,0:T(8,128)(2,1)S(1)} %get-tuple-element.10), channel_id=1, source_target_pairs={{0,96},{32,0},{64,32},{96,64},{1,97},{33,1},{65,33},{97,65},{2,98}... | collective-permute-start | bytes 393224 | tf_op jit(solution)/shard_map/ppermute | solution.py:32
  156.7 24.7 %collective-permute-start.11 = (bf16[4,2,16,2048]{3,2,1,0:T(8,128)(2,1)S(1)}, bf16[4,2,16,2048]{3,2,1,0:T(8,128)(2,1)S(1)}, u32[]{:S(2)}, u32[]{:S(2)}) collective-permute-start(bf16[4,2,16,2048]{3,2,1,0:T(8,128)(2,1)S(1)} %pad_maximum_fusion.1.rest_4_.rest_12_), channel_id=1, source_target_pairs={{0,64},{32,96},{64,0},{96,32},{1,65},{33,97},{65,1},{97,33},{2,66}... | collective-permute-start | bytes 1572872 | tf_op jit(solution)/shard_map/ppermute | solution.py:32
  168.6 14.4 %collective-permute-start.12 = (bf16[4,2,16,2048]{3,2,1,0:T(8,128)(2,1)S(1)}, bf16[4,2,16,2048]{3,2,1,0:T(8,128)(2,1)S(1)}, u32[]{:S(2)}, u32[]{:S(2)}) collective-permute-start(bf16[4,2,16,2048]{3,2,1,0:T(8,128)(2,1)S(1)} %pad_maximum_fusion.1.rest_4_.rest_12_), channel_id=1, source_target_pairs={{0,96},{32,0},{64,32},{96,64},{1,97},{33,1},{65,33},{97,65},{2,98}... | collective-permute-start | bytes 1572872 | tf_op jit(solution)/shard_map/ppermute | solution.py:32
  172.4 25.2 %copy-start.3 = (bf16[4,2,16,2048]{3,2,1,0:T(8,128)(2,1)}, bf16[4,2,16,2048]{3,2,1,0:T(8,128)(2,1)S(1)}, u32[]{:S(2)}) copy-start(bf16[4,2,16,2048]{3,2,1,0:T(8,128)(2,1)S(1)} %pad_maximum_fusion.rest_0_.rest_8_) | copy-start | bytes 1572868
  172.4 15.2 %collective-permute-start.4 = (bf16[4,2,16,2048]{3,2,1,0:T(8,128)(2,1)S(1)}, bf16[4,2,16,2048]{3,2,1,0:T(8,128)(2,1)S(1)}, u32[]{:S(2)}, u32[]{:S(2)}) collective-permute-start(bf16[4,2,16,2048]{3,2,1,0:T(8,128)(2,1)S(1)} %pad_maximum_fusion.rest_0_.rest_8_), channel_id=1, source_target_pairs={{0,8},{8,16},{16,24},{24,0},{1,9},{9,17},{17,25},{25,1},{2,10},{10... | collective-permute-start | bytes 1572872 | tf_op jit(solution)/shard_map/ppermute | solution.py:32
  174.6 22.2 %collective-permute-start.5 = (bf16[4,2,16,2048]{3,2,1,0:T(8,128)(2,1)S(1)}, bf16[4,2,16,2048]{3,2,1,0:T(8,128)(2,1)S(1)}, u32[]{:S(2)}, u32[]{:S(2)}) collective-permute-start(bf16[4,2,16,2048]{3,2,1,0:T(8,128)(2,1)S(1)} %pad_maximum_fusion.rest_0_.rest_8_), channel_id=1, source_target_pairs={{0,16},{8,24},{16,0},{24,8},{1,17},{9,25},{17,1},{25,9},{2,18},{10... | collective-permute-start | bytes 1572872 | tf_op jit(solution)/shard_map/ppermute | solution.py:32
  177.2 20.4 %copy-start.7 = (bf16[4,2,16,2048]{3,2,1,0:T(8,128)(2,1)}, bf16[4,2,16,2048]{3,2,1,0:T(8,128)(2,1)S(1)}, u32[]{:S(2)}) copy-start(bf16[4,2,16,2048]{3,2,1,0:T(8,128)(2,1)S(1)} %collective-permute-done.10.rest_5_.rest_13_) | copy-start | bytes 1572868
  177.2 20.4 %collective-permute-start.6 = (bf16[4,2,16,2048]{3,2,1,0:T(8,128)(2,1)S(1)}, bf16[4,2,16,2048]{3,2,1,0:T(8,128)(2,1)}, u32[]{:S(2)}, u32[]{:S(2)}) collective-permute-start(bf16[4,2,16,2048]{3,2,1,0:T(8,128)(2,1)S(1)} %pad_maximum_fusion.rest_0_.rest_8_), channel_id=1, source_target_pairs={{0,24},{8,0},{16,8},{24,16},{1,25},{9,1},{17,9},{25,17},{2,26},{10... | collective-permute-start | bytes 1572872 | tf_op jit(solution)/shard_map/ppermute | solution.py:32
  216.3 5.2 %collective-permute-start.26 = (bf16[512,128]{1,0:T(8,128)(2,1)}, bf16[512,128]{1,0:T(8,128)(2,1)S(1)}, u32[]{:S(2)}, u32[]{:S(2)}) collective-permute-start(bf16[512,128]{1,0:T(8,128)(2,1)} %shard_map.40), channel_id=1, source_target_pairs={{0,4},{4,0},{1,5},{5,1},{2,6},{6,2},{3,7},{7,3},{8,12},{12,8},{9,1... | collective-permute-start | bytes 393224 | tf_op jit(solution)/shard_map/ppermute | solution.py:32
  222.4 7.4 %collective-permute-start.31 = (bf16[512,128]{1,0:T(8,128)(2,1)S(1)}, bf16[512,128]{1,0:T(8,128)(2,1)S(1)}, u32[]{:S(2)}, u32[]{:S(2)}) collective-permute-start(bf16[512,128]{1,0:T(8,128)(2,1)S(1)} %get-tuple-element.5), channel_id=1, source_target_pairs={{0,8},{8,16},{16,24},{24,0},{1,9},{9,17},{17,25},{25,1},{2,10},{10... | collective-permute-start | bytes 393224 | tf_op jit(solution)/shard_map/ppermute | solution.py:32
  223.3 7.9 %collective-permute-start.32 = (bf16[512,128]{1,0:T(8,128)(2,1)S(1)}, bf16[512,128]{1,0:T(8,128)(2,1)S(1)}, u32[]{:S(2)}, u32[]{:S(2)}) collective-permute-start(bf16[512,128]{1,0:T(8,128)(2,1)S(1)} %get-tuple-element.5), channel_id=1, source_target_pairs={{0,16},{8,24},{16,0},{24,8},{1,17},{9,25},{17,1},{25,9},{2,18},{10... | collective-permute-start | bytes 393224 | tf_op jit(solution)/shard_map/ppermute | solution.py:32
  225.8 5.4 %collective-permute-start.33 = (bf16[512,128]{1,0:T(8,128)(2,1)S(1)}, bf16[512,128]{1,0:T(8,128)(2,1)S(1)}, u32[]{:S(2)}, u32[]{:S(2)}) collective-permute-start(bf16[512,128]{1,0:T(8,128)(2,1)S(1)} %get-tuple-element.5), channel_id=1, source_target_pairs={{0,24},{8,0},{16,8},{24,16},{1,25},{9,1},{17,9},{25,17},{2,26},{10... | collective-permute-start | bytes 393224 | tf_op jit(solution)/shard_map/ppermute | solution.py:32
  231.3 40.1 %copy-start.13 = (bf16[4,512,128]{2,1,0:T(8,128)(2,1)}, bf16[4,512,128]{2,1,0:T(8,128)(2,1)S(1)}, u32[]{:S(2)}) copy-start(bf16[4,512,128]{2,1,0:T(8,128)(2,1)S(1)} %pad_maximum_fusion.5.rest_1_) | copy-start | bytes 1572868
  231.3 22.7 %collective-permute-start.38 = (bf16[4,512,128]{2,1,0:T(8,128)(2,1)S(1)}, bf16[4,512,128]{2,1,0:T(8,128)(2,1)S(1)}, u32[]{:S(2)}, u32[]{:S(2)}) collective-permute-start(bf16[4,512,128]{2,1,0:T(8,128)(2,1)S(1)} %pad_maximum_fusion.5.rest_1_), channel_id=1, source_target_pairs={{0,32},{32,64},{64,96},{96,0},{1,33},{33,65},{65,97},{97,1},{2,34}... | collective-permute-start | bytes 1572872 | tf_op jit(solution)/shard_map/ppermute | solution.py:32
  231.6 18.4 %collective-permute-start.27 = (bf16[512,128]{1,0:T(8,128)(2,1)S(1)}, bf16[512,128]{1,0:T(8,128)(2,1)S(1)}, u32[]{:S(2)}, u32[]{:S(2)}) collective-permute-start(bf16[512,128]{1,0:T(8,128)(2,1)S(1)} %get-tuple-element.6), channel_id=1, source_target_pairs={{0,32},{32,64},{64,96},{96,0},{1,33},{33,65},{65,97},{97,1},{2,34}... | collective-permute-start | bytes 393224 | tf_op jit(solution)/shard_map/ppermute | solution.py:32
  234.0 15.9 %collective-permute-start.28 = (bf16[512,128]{1,0:T(8,128)(2,1)S(1)}, bf16[512,128]{1,0:T(8,128)(2,1)S(1)}, u32[]{:S(2)}, u32[]{:S(2)}) collective-permute-start(bf16[512,128]{1,0:T(8,128)(2,1)S(1)} %get-tuple-element.6), channel_id=1, source_target_pairs={{0,64},{32,96},{64,0},{96,32},{1,65},{33,97},{65,1},{97,33},{2,66}... | collective-permute-start | bytes 393224 | tf_op jit(solution)/shard_map/ppermute | solution.py:32
  236.2 13.8 %collective-permute-start.29 = (bf16[512,128]{1,0:T(8,128)(2,1)S(1)}, bf16[512,128]{1,0:T(8,128)(2,1)S(1)}, u32[]{:S(2)}, u32[]{:S(2)}) collective-permute-start(bf16[512,128]{1,0:T(8,128)(2,1)S(1)} %get-tuple-element.6), channel_id=1, source_target_pairs={{0,96},{32,0},{64,32},{96,64},{1,97},{33,1},{65,33},{97,65},{2,98}... | collective-permute-start | bytes 393224 | tf_op jit(solution)/shard_map/ppermute | solution.py:32
  250.1 21.3 %copy-start.14 = (bf16[4,512,128]{2,1,0:T(8,128)(2,1)}, bf16[4,512,128]{2,1,0:T(8,128)(2,1)S(1)}, u32[]{:S(2)}) copy-start(bf16[4,512,128]{2,1,0:T(8,128)(2,1)S(1)} %pad_maximum_fusion.4.rest_0_) | copy-start | bytes 1572868
  250.1 26.7 %collective-permute-start.37 = (bf16[4,512,128]{2,1,0:T(8,128)(2,1)S(1)}, bf16[4,512,128]{2,1,0:T(8,128)(2,1)}, u32[]{:S(2)}, u32[]{:S(2)}) collective-permute-start(bf16[4,512,128]{2,1,0:T(8,128)(2,1)S(1)} %pad_maximum_fusion.4.rest_0_), channel_id=1, source_target_pairs={{0,8},{8,16},{16,24},{24,0},{1,9},{9,17},{17,25},{25,1},{2,10},{10... | collective-permute-start | bytes 1572872 | tf_op jit(solution)/shard_map/ppermute | solution.py:32
  250.2 32.0 %collective-permute-start.34 = (bf16[4,512,128]{2,1,0:T(8,128)(2,1)S(1)}, bf16[4,512,128]{2,1,0:T(8,128)(2,1)S(1)}, u32[]{:S(2)}, u32[]{:S(2)}) collective-permute-start(bf16[4,512,128]{2,1,0:T(8,128)(2,1)S(1)} %pad_maximum_fusion.5.rest_1_), channel_id=1, source_target_pairs={{0,96},{32,0},{64,32},{96,64},{1,97},{33,1},{65,33},{97,65},{2,98}... | collective-permute-start | bytes 1572872 | tf_op jit(solution)/shard_map/ppermute | solution.py:32
  250.2 31.9 %collective-permute-start.36 = (bf16[4,512,128]{2,1,0:T(8,128)(2,1)S(1)}, bf16[4,512,128]{2,1,0:T(8,128)(2,1)S(1)}, u32[]{:S(2)}, u32[]{:S(2)}) collective-permute-start(bf16[4,512,128]{2,1,0:T(8,128)(2,1)S(1)} %pad_maximum_fusion.5.rest_1_), channel_id=1, source_target_pairs={{0,64},{32,96},{64,0},{96,32},{1,65},{33,97},{65,1},{97,33},{2,66}... | collective-permute-start | bytes 1572872 | tf_op jit(solution)/shard_map/ppermute | solution.py:32
  250.9 31.3 %collective-permute-start.30 = (bf16[4,512,128]{2,1,0:T(8,128)(2,1)S(1)}, bf16[4,512,128]{2,1,0:T(8,128)(2,1)S(1)}, u32[]{:S(2)}, u32[]{:S(2)}) collective-permute-start(bf16[4,512,128]{2,1,0:T(8,128)(2,1)S(1)} %pad_maximum_fusion.4.rest_0_), channel_id=1, source_target_pairs={{0,24},{8,0},{16,8},{24,16},{1,25},{9,1},{17,9},{25,17},{2,26},{10... | collective-permute-start | bytes 1572872 | tf_op jit(solution)/shard_map/ppermute | solution.py:32
  254.0 28.2 %collective-permute-start.35 = (bf16[4,512,128]{2,1,0:T(8,128)(2,1)S(1)}, bf16[4,512,128]{2,1,0:T(8,128)(2,1)}, u32[]{:S(2)}, u32[]{:S(2)}) collective-permute-start(bf16[4,512,128]{2,1,0:T(8,128)(2,1)S(1)} %pad_maximum_fusion.4.rest_0_), channel_id=1, source_target_pairs={{0,16},{8,24},{16,0},{24,8},{1,17},{9,25},{17,1},{25,9},{2,18},{10... | collective-permute-start | bytes 1572872 | tf_op jit(solution)/shard_map/ppermute | solution.py:32
  (11 other events, 89.4 us)

commit v3 on v2

--- a/solution.py
+++ b/solution.py
@@ -32,21 +32,38 @@
     return lax.ppermute(v, axis, [(i, (i + by) % n) for i in range(n)])
 
 
+def near_ring(v, axis):
+    return shifted(v, axis, 1), shifted(v, axis, 3)
+
+
 def ring(v, axis):
-    return [v] + [shifted(v, axis, s) for s in (1, 3, 2)]
-
-
-def in_slots(parts):
-    own, one, three, two = parts
-    return [own, one, two, three]
-
-
-def gather_rows(v):
+    one, three = near_ring(v, axis)
+    return [v, one, shifted(v, axis, 2), three]
+
+
+def forward(one, three, axis):
+    half = one.shape[0] // 2
+    return shifted(one[:half], axis, 1), shifted(three[half:], axis, 3)
+
+
+def relayed_ring(v, axis):
+    one, three = near_ring(v, axis)
+    return [v, one, *forward(one, three, axis), three]
+
+
+def gather_rows(v, second):
     both = jnp.stack([v, shifted(v, "y", 1)])
     half = both.shape[-1] // 2
-    a = jnp.stack(in_slots(ring(both[..., :half], "x")))
-    b = jnp.stack(in_slots(ring(both[..., half:], "z")))
-    return in_slots(ring(a, "z")), in_slots(ring(b, "x"))
+    a = jnp.stack(ring(both[..., :half], "x"))
+    b = jnp.stack(ring(both[..., half:], "z"))
+    return second(a, "z"), second(b, "x")
+
+
+def blocks(pieces):
+    at = 0
+    for piece in pieces:
+        yield at // 4, at % 4, piece
+        at += piece.shape[0]
 
 
 def place(pos, slot_x, slot_z, slot_y):
@@ -66,29 +83,37 @@
 
 
 def spread(table, base, pieces, out):
-    for later, piece in enumerate(pieces):
-        for early in range(4):
+    for later, first, piece in blocks(pieces):
+        for early in range(piece.shape[0]):
             for slot_y in range(2):
-                at = pl.multiple_of(table[base + (later * 4 + early) * 2 + slot_y], ROWS)
+                slot = (later * 4 + first + early) * 2 + slot_y
+                at = pl.multiple_of(table[base + slot], ROWS)
                 out[pl.ds(at, ROWS), :] = piece[early, slot_y]
 
 
-def spread_head(table, head, pieces_a, pieces_b, out):
+def spread_head(table, head, pieces, out):
+    half = len(pieces) // 2
+
     @pl.when(head < H // 2)
     def _():
-        spread(table, 0, pieces_a, out)
+        spread(table, 0, pieces[:half], out)
 
     @pl.when(head >= H // 2)
     def _():
-        spread(table, 32, pieces_b, out)
-
-
-def piece_specs(block_of, heads):
-    shape = (4, 2, ROWS, heads * DH)
+        spread(table, 32, pieces[half:], out)
+
+
+def piece_specs(pieces, block_of, heads):
     last = H // 2 // heads
-    a = pl.BlockSpec(shape, lambda *g: (0, 0, 0, jnp.minimum(block_of(*g), last - 1)))
-    b = pl.BlockSpec(shape, lambda *g: (0, 0, 0, jnp.maximum(block_of(*g) - last, 0)))
-    return [a] * 4 + [b] * 4
+    specs = []
+    for i, piece in enumerate(pieces):
+        shape = (piece.shape[0], 2, ROWS, heads * DH)
+        if i < len(pieces) // 2:
+            column = lambda *g: jnp.minimum(block_of(*g), last - 1)
+        else:
+            column = lambda *g: jnp.maximum(block_of(*g) - last, 0)
+        specs.append(pl.BlockSpec(shape, lambda *g, column=column: (0, 0, 0, column(*g))))
+    return specs
 
 
 def nt(a, b):
@@ -96,14 +121,14 @@
 
 
 def parts_kernel(pos, keys, values, *rest):
-    pieces, (out, land, table) = rest[:8], rest[8:]
+    pieces, (out, land, table) = rest[:-3], rest[-3:]
     g = pl.program_id(0)
 
     @pl.when(g == 0)
     def _():
         fill_table(pos, table)
 
-    spread_head(table, g * GROUP, pieces[:4], pieces[4:], land)
+    spread_head(table, g * GROUP, pieces, land)
 
     def scores_of(j):
         return nt(keys[:, j * DH : (j + 1) * DH], land[:, j * DH : (j + 1) * DH])
@@ -145,14 +170,14 @@
 
 
 def near_kernel(pos, queries, *rest):
-    pieces, (out, land, table) = rest[:8], rest[8:]
+    pieces, (out, land, table) = rest[:-3], rest[-3:]
     g = pl.program_id(0)
 
     @pl.when(g == 0)
     def _():
         fill_table(pos, table)
 
-    spread_head(table, g * GROUP, pieces[:4], pieces[4:], land)
+    spread_head(table, g * GROUP, pieces, land)
     for j in range(GROUP):
         cols = slice(j * DH, (j + 1) * DH)
         for t in range(0, queries.shape[0], TALL):
@@ -163,12 +188,12 @@
             out[j, t : t + TALL] = (expo * (1.0 / totals)).astype(BF16)
 
 
-def inverse_kernel(pos, *rest):
-    pieces, (out, land_q, land_k, table) = rest[:16], rest[16:]
+def inverse_kernel(n_q, pos, *rest):
+    pieces, (out, land_q, land_k, table) = rest[:-4], rest[-4:]
     fill_table(pos, table)
     head = place(pos, 0, 0, 0)
-    spread_head(table, head, pieces[:4], pieces[4:8], land_q)
-    spread_head(table, head, pieces[8:12], pieces[12:], land_k)
+    spread_head(table, head, pieces[:n_q], land_q)
+    spread_head(table, head, pieces[n_q:], land_k)
     scores = nt(land_q[...], land_k[...])
     top = jnp.max(scores, 1, keepdims=True)
     expo = jnp.exp2((scores - top) * C2)
@@ -192,14 +217,18 @@
     out[...] = lax.fori_loop(0, ITERS, sweep, inverse).astype(BF16)
 
 
-def product_kernel(parts, levels, inverse, out, acc):
+def product_kernel(parts, levels, inverse, out, acc, shares):
     c = pl.program_id(0)
-    level = jnp.zeros((32, 128), F32)
-    for k in range(4):
-        rows = [levels[:, 3 * k + t, :].astype(F32) for t in range(3)]
-        level = jnp.where(c == k, rows[0] + rows[1] + rows[2], level)
-    weight = jnp.exp2(level - jnp.max(level, 0, keepdims=True))
-    weight = weight / jnp.sum(weight, 0, keepdims=True)
+
+    @pl.when(c == 0)
+    def _():
+        for k in range(4):
+            high, mid, low = (levels[:, 3 * k + t, :].astype(F32) for t in range(3))
+            level = high + mid + low
+            weight = jnp.exp2(level - jnp.max(level, 0, keepdims=True))
+            shares[k] = weight / jnp.sum(weight, 0, keepdims=True)
+
+    weight = shares[c]
     normed = jnp.zeros((128, 128), F32)
     for s in range(32):
         normed = normed + parts[s].astype(F32) * weight[s : s + 1]
@@ -218,9 +247,9 @@
         out[...] = acc[...].astype(BF16)
 
 
-def final_kernel(shifts, pos, weights, *rest):
+def final_kernel(shifts, n_given, pos, weights, *rest):
     n = LAST * len(shifts)
-    given = rest[: 2 * len(shifts)]
+    given = rest[:n_given]
     out, tiles, results, prods, sems_in, sems_out, sems_prod = rest[-7:]
     heads = []
     for shift in shifts:
@@ -228,7 +257,10 @@
         heads += [(((pos[0] + 4 - early) % 4) * 4 + z) * 2 for early in range(4)]
         heads += [(x * 4 + (pos[1] + 4 - early) % 4) * 2 + 1 for early in range(4)]
     pieces = [
-        pltpu.make_async_copy(piece, prods.at[i], sems_prod.at[i]) for i, piece in enumerate(given)
+        pltpu.make_async_copy(
+            piece, prods.at[later, pl.ds(early, piece.shape[0])], sems_prod.at[i]
+        )
+        for i, (later, early, piece) in enumerate(blocks(given))
     ]
     into = [
         pltpu.make_async_copy(weights.at[h], tiles.at[i], sems_in.at[i]) for i, h in enumerate(heads)
@@ -266,7 +298,7 @@
     here = weights.shape[1]
     n = LAST * len(shifts)
     return pl.pallas_call(
-        functools.partial(final_kernel, shifts),
+        functools.partial(final_kernel, shifts, len(pieces)),
         in_specs=[pl.BlockSpec(memory_space=pltpu.SMEM)]
         + [anywhere] * (1 + len(pieces) + len(out)),
         out_specs=anywhere,
@@ -274,7 +306,7 @@
         scratch_shapes=[
             pltpu.VMEM((n, here, M), BF16),
             pltpu.VMEM((n, here, DH), BF16),
-            pltpu.VMEM((len(pieces), 4, M, DH), BF16),
+            pltpu.VMEM((2 * len(shifts), 4, M, DH), BF16),
             pltpu.SemaphoreType.DMA((n,)),
             pltpu.SemaphoreType.DMA((n,)),
             pltpu.SemaphoreType.DMA((len(pieces),)),
@@ -308,41 +340,48 @@
     pos = jnp.stack([lax.axis_index(a) for a in SEQ]).astype(jnp.int32)
     here = queries.shape[0]
     per_device = M // 32
-    q_a, q_b = gather_rows(landmarks(queries, per_device))
-    k_a, k_b = gather_rows(landmarks(keys, per_device))
+    q_a, q_b = gather_rows(landmarks(queries, per_device), relayed_ring)
+    k_a, k_b = gather_rows(landmarks(keys, per_device), ring)
+    land_q, land_k = q_a + q_b, k_a + k_b
 
     column = pl.BlockSpec((here, GROUP * DH), lambda h, pos: (0, h))
-    per_head = piece_specs(lambda h, pos: h, GROUP)
+
+    def per_head(pieces):
+        return piece_specs(pieces, lambda h, pos: h, GROUP)
+
     land = pltpu.VMEM((M, GROUP * DH), BF16)
     table = pltpu.SMEM((64,), jnp.int32)
     parts = call(
         parts_kernel,
         (H // GROUP,),
-        [column, column] + per_head,
+        [column, column] + per_head(land_q),
         pl.BlockSpec((GROUP, M + EXTRA, DH), lambda h, pos: (h, 0, 0)),
         jax.ShapeDtypeStruct((H, M + EXTRA, DH), BF16),
         [land, table],
-    )(pos, keys, values, *q_a, *q_b)
+    )(pos, keys, values, *land_q)
     parts = lax.all_to_all(parts, SEQ, split_axis=0, concat_axis=0, tiled=True)
 
     weights = call(
         near_kernel,
         (H // GROUP,),
-        [column] + per_head,
+        [column] + per_head(land_k),
         pl.BlockSpec((GROUP, here, M), lambda h, pos: (h, 0, 0)),
         jax.ShapeDtypeStruct((H, here, M), BF16),
         [land, table],
-    )(pos, queries, *k_a, *k_b)
-
-    owned = piece_specs(lambda g, pos: place(pos, 0, 0, 0), 1)
+    )(pos, queries, *land_k)
+
+
+    def owned(pieces):
+        return piece_specs(pieces, lambda g, pos: place(pos, 0, 0, 0), 1)
+
     inverse = call(
-        inverse_kernel,
+        functools.partial(inverse_kernel, len(land_q)),
         (1,),
-        owned + owned,
+        owned(land_q) + owned(land_k),
         pl.BlockSpec((M, M), lambda g, pos: (0, 0)),
         jax.ShapeDtypeStruct((M, M), BF16),
         [pltpu.VMEM((M, DH), BF16)] * 2 + [table],
-    )(pos, *q_a, *q_b, *k_a, *k_b)
+    )(pos, *land_q, *land_k)
 
     product = call(
         product_kernel,
@@ -354,7 +393,7 @@
         ],
         pl.BlockSpec((M, DH), lambda c: (0, 0)),
         jax.ShapeDtypeStruct((M, DH), BF16),
-        [pltpu.VMEM((M, DH), F32)],
+        [pltpu.VMEM((M, DH), F32), pltpu.VMEM((4, 32, 128), F32)],
         prefetch=0,
     )(parts, parts, inverse)
 
@@ -362,14 +401,14 @@
     lower = pos[2] == 0
     a = jnp.where(lower, product, other)
     b = jnp.where(lower, other, product)
-    a = jnp.stack(in_slots(ring(a, "x")))
-    b = jnp.stack(in_slots(ring(b, "z")))
+    a = jnp.stack(ring(a, "x"))
+    b = jnp.stack(ring(b, "z"))
     out = final((0,), pos, weights, [a, b])
-    pieces = {}
-    for s in (1, 3, 2):
-        pieces[s] = [shifted(a, "z", s), shifted(b, "x", s)]
-    out = final((1,), pos, weights, pieces[1], out)
-    return final((3, 2), pos, weights, pieces[3] + pieces[2], out)
+    a_one, a_three = near_ring(a, "z")
+    b_one, b_three = near_ring(b, "x")
+    far = [*forward(a_one, a_three, "z"), *forward(b_one, b_three, "x")]
+    out = final((1, 3), pos, weights, [a_one, b_one, a_three, b_three], out)
+    return final((2,), pos, weights, far, out)
 
 
 def solution(mesh):

time: 294 us -> 284 us (0.966)
  waiting for transfers between devices: 134 us -> 112 us
  starting transfers between devices: 75.8 us -> 83.1 us
  local copies, waits for them, and re-layouts: 1.97 us -> 7.77 us
    ppermute x39 -> x43, waiting for transfers between devices: 134 us -> 112 us  [shifted(): return lax.ppermute(v, axis, [(i, (i + by) % n) for i in range(n)])]
    ppermute x39 -> x43, starting transfers between devices: 66.1 us -> 76.2 us  [shifted(): return lax.ppermute(v, axis, [(i, (i + by) % n) for i in range(n)])]
    slice x0 -> x8, local copies, waits for them, and re-layouts: none -> 6.21 us  [forward(): return (shifted(one[:half], axis, 1), shifted(three[half:], axis, 3))]
  transfers between devices with their start and end apart: 40 -> 44, of which waited for: 25 -> 21; matrix products, arithmetic and copies ran while one was open for 1% -> 4% of each run, Pallas kernels for 14% -> 15%
where the time goes in v3:
time: 284 us; the launch traced here: 283 us
  waiting for transfers between devices  112 us (39%)
  starting transfers between devices  83.1 us (29%)
  Pallas kernels  70.9 us (25%)
  other arithmetic  8.69 us (3%)
  local copies, waits for them, and re-layouts  7.77 us (3%)
    ppermute x43, waiting for transfers between devices, shifted(): return lax.ppermute(v, axis, [(i, (i + by) % n) for i in range(n)])  112 us
    ppermute x43, starting transfers between devices, shifted(): return lax.ppermute(v, axis, [(i, (i + by) % n) for i in range(n)])  76.2 us
    pallas_call x3, Pallas kernels, final(): pl.pallas_call(functools.partial(final_kernel, shifts, len(pieces)), in_s...  19.2 us
    pallas_call x1, Pallas kernels, steps(): call(parts_kernel, (H // GROUP,), [column, column] + per_head(land_q), pl...  17.1 us
    pallas_call x1, Pallas kernels, steps(): call(near_kernel, (H // GROUP,), [column] + per_head(land_k), pl.BlockSpe...  16.3 us
    pallas_call x1, Pallas kernels, steps(): call(functools.partial(inverse_kernel, len(land_q)), (1,), owned(land_q)...  13.5 us
    all_to_all x1, starting transfers between devices, steps(): parts = lax.all_to_all(parts, SEQ, split_axis=0, concat_axis=0, tiled=True)  6.91 us
    reduce_sum x2, other arithmetic, landmarks(): sums = jnp.sum(tokens.reshape(per_device, segment, D), axis=1, dtype=F32)  6.61 us
  transfers between devices with their start and end apart: 44, of which 21 were waited for; matrix products, arithmetic and copies ran while one was open for 4% of the time, Pallas kernels for 15%

profile of v3, /device:TPU:0, one launch (start us, length us, event | category | flops | bytes accessed | tf_op | source)
XLA Modules:
  0.0 283.0 jit_solution(13059587344822305476)
XLA Ops:
  0.0 3.3 %convert_reduce_fusion = f32[16,4096]{1,0:T(8,128)S(1)} fusion(bf16[512,4096]{1,0:T(8,128)(2,1)} %queries.1), kind=kLoop, calls=%fused_computation | loop fusion | flops 4128768 | bytes 4456448 | tf_op jit(solution)/shard_map/reduce_sum | solution.py:335
  3.3 1.8 collective-permute-start.13
  5.1 3.5 %collective-permute-done.13 = bf16[16,4096]{1,0:T(8,128)(2,1)S(1)} collective-permute-done((bf16[16,4096]{1,0:T(8,128)(2,1)S(1)}, bf16[16,4096]{1,0:T(8,128)(2,1)S(1)}, u32[]{:S(2)}, u32[]{:S(2)}) %collective-permute-start.13) | collective-permute-done | bytes 131104 | tf_op jit(solution)/shard_map/ppermute | solution.py:32
  8.6 1.7 collective-permute-start.14
  10.3 2.7 collective-permute-start.15
  14.5 1.9 collective-permute-start.21
  16.4 3.6 %collective-permute-start.22 = (bf16[2,16,2048]{2,1,0:T(8,128)(2,1)S(1)}, bf16[2,16,2048]{2,1,0:T(8,128)(2,1)S(1)}, u32[]{:S(2)}, u32[]{:S(2)}) collective-permute-start(bf16[2,16,2048]{2,1,0:T(8,128)(2,1)S(1)} %get-tuple-element.7), channel_id=1, source_target_pairs={{0,16},{8,24},{16,0},{24,8},{1,17},{9,25},{17,1},{25,9},{2,18},{10... | collective-permute-start | bytes 393224 | tf_op jit(solution)/shard_map/ppermute | solution.py:32
  22.2 2.2 collective-permute-start.19
  27.3 2.6 collective-permute-start.26
  30.0 5.6 %collective-permute-done.17.rest_1_ = bf16[4,2,16,2048]{3,2,1,0:T(8,128)(2,1)S(1)} collective-permute-done((bf16[4,2,16,2048]{3,2,1,0:T(8,128)(2,1)S(1)}, bf16[4,2,16,2048]{3,2,1,0:T(8,128)(2,1)S(1)}, u32[]{:S(2)}, u32[]{:S(2)}) %collective-permute-start.17) | collective-permute-done | bytes 524320 | tf_op jit(solution)/shard_map/ppermute | solution.py:32
  37.1 3.2 %collective-permute-start.20 = (bf16[2,2,16,2048]{3,2,1,0:T(8,128)(2,1)}, bf16[2,2,16,2048]{3,2,1,0:T(8,128)(2,1)}, u32[]{:S(2)}, u32[]{:S(2)}) collective-permute-start(bf16[2,2,16,2048]{3,2,1,0:T(8,128)(2,1)} %slice.53), channel_id=1, source_target_pairs={{0,24},{8,0},{16,8},{24,16},{1,25},{9,1},{17,9},{25,17},{2,26},{10... | collective-permute-start | bytes 786440 | tf_op jit(solution)/shard_map/ppermute | solution.py:32
  42.5 2.6 collective-permute-start.27
  45.8 3.2 %collective-permute-done.25.rest_7_ = bf16[2,2,16,2048]{3,2,1,0:T(8,128)(2,1)} collective-permute-done((bf16[2,2,16,2048]{3,2,1,0:T(8,128)(2,1)}, bf16[2,2,16,2048]{3,2,1,0:T(8,128)(2,1)}, u32[]{:S(2)}, u32[]{:S(2)}) %collective-permute-start.25) | collective-permute-done | bytes 262176 | tf_op jit(solution)/shard_map/ppermute | solution.py:32
  49.4 17.1 %shard_map.38 = bf16[32,528,128]{2,1,0:T(8,128)(2,1)} custom-call(s32[3]{0:T(128)} %pad_add_fusion.pos, bf16[512,4096]{1,0:T(8,128)(2,1)} %keys.1, bf16[512,4096]{1,0:T(8,128)(2,1)} %values.1, bf16[4,2,16,2048]{3,2,1,0:T(8,128)(2,1)} %copy-done, bf16[4,2,16,2048]{3,2,1,0:T(8,128)(2,1)} %copy-done.4, bf16[2,2,16,2048]{3,2,1,0:T(8,128)(2,1)} %copy-done.19, ...), custom_call_target="tpu_custom_call" | custom-call | tf_op jit(solution)/shard_map/pallas_call | solution.py:354
  66.5 6.9 %all-to-all-start = ((bf16[32,528,128]{2,1,0:T(8,128)(2,1)}), bf16[32,528,128]{2,1,0:T(8,128)(2,1)}, u32[]{:S(2)}, u32[]{:S(2)}) async-start(bf16[32,528,128]{2,1,0:T(8,128)(2,1)} %shard_map.38), calls=%async_computation | async-start | bytes 8650752 | tf_op jit(solution)/shard_map/all_to_all | solution.py:362
  73.5 3.3 %convert_reduce_fusion.1 = f32[16,4096]{1,0:T(8,128)S(1)} fusion(bf16[512,4096]{1,0:T(8,128)(2,1)} %keys.1), kind=kLoop, calls=%fused_computation.1 | loop fusion | flops 4128768 | bytes 4456448 | tf_op jit(solution)/shard_map/reduce_sum | solution.py:335
  76.8 1.8 collective-permute-start
  78.6 44.7 %collective-permute-done = bf16[16,4096]{1,0:T(8,128)(2,1)S(1)} collective-permute-done((bf16[16,4096]{1,0:T(8,128)(2,1)S(1)}, bf16[16,4096]{1,0:T(8,128)(2,1)S(1)}, u32[]{:S(2)}, u32[]{:S(2)}) %collective-permute-start) | collective-permute-done | bytes 131104 | tf_op jit(solution)/shard_map/ppermute | solution.py:32
  123.4 5.9 %collective-permute-start.7 = (bf16[2,16,2048]{2,1,0:T(8,128)(2,1)S(1)}, bf16[2,16,2048]{2,1,0:T(8,128)(2,1)S(1)}, u32[]{:S(2)}, u32[]{:S(2)}) collective-permute-start(bf16[2,16,2048]{2,1,0:T(8,128)(2,1)S(1)} %get-tuple-element.9), channel_id=1, source_target_pairs={{0,8},{8,16},{16,24},{24,0},{1,9},{9,17},{17,25},{25,1},{2,10},{10... | collective-permute-start | bytes 393224 | tf_op jit(solution)/shard_map/ppermute | solution.py:32
  129.7 2.3 collective-permute-start.9
  132.3 3.4 %collective-permute-done.8 = bf16[2,16,2048]{2,1,0:T(8,128)(2,1)S(1)} collective-permute-done((bf16[2,16,2048]{2,1,0:T(8,128)(2,1)S(1)}, bf16[2,16,2048]{2,1,0:T(8,128)(2,1)S(1)}, u32[]{:S(2)}, u32[]{:S(2)}) %collective-permute-start.8) | collective-permute-done | bytes 131104 | tf_op jit(solution)/shard_map/ppermute | solution.py:32
  135.8 5.3 %collective-permute-start.10 = (bf16[4,2,16,2048]{3,2,1,0:T(8,128)(2,1)S(1)}, bf16[4,2,16,2048]{3,2,1,0:T(8,128)(2,1)S(1)}, u32[]{:S(2)}, u32[]{:S(2)}) collective-permute-start(bf16[4,2,16,2048]{3,2,1,0:T(8,128)(2,1)S(1)} %pad_maximum_fusion.1.rest_4_.rest_14_), channel_id=1, source_target_pairs={{0,32},{32,64},{64,96},{96,0},{1,33},{33,65},{65,97},{97,1},{2,34}... | collective-permute-start | bytes 1572872 | tf_op jit(solution)/shard_map/ppermute | solution.py:32
  141.2 3.0 %collective-permute-start.2 = (bf16[2,16,2048]{2,1,0:T(8,128)(2,1)S(1)}, bf16[2,16,2048]{2,1,0:T(8,128)(2,1)S(1)}, u32[]{:S(2)}, u32[]{:S(2)}) collective-permute-start(bf16[2,16,2048]{2,1,0:T(8,128)(2,1)S(1)} %get-tuple-element.10), channel_id=1, source_target_pairs={{0,64},{32,96},{64,0},{96,32},{1,65},{33,97},{65,1},{97,33},{2,66}... | collective-permute-start | bytes 393224 | tf_op jit(solution)/shard_map/ppermute | solution.py:32
  144.2 2.5 collective-permute-start.3
  147.3 10.1 %collective-permute-done.1 = bf16[2,16,2048]{2,1,0:T(8,128)(2,1)S(1)} collective-permute-done((bf16[2,16,2048]{2,1,0:T(8,128)(2,1)S(1)}, bf16[2,16,2048]{2,1,0:T(8,128)(2,1)S(1)}, u32[]{:S(2)}, u32[]{:S(2)}) %collective-permute-start.1) | collective-permute-done | bytes 131104 | tf_op jit(solution)/shard_map/ppermute | solution.py:32
  157.4 2.9 %collective-permute-start.12 = (bf16[4,2,16,2048]{3,2,1,0:T(8,128)(2,1)S(1)}, bf16[4,2,16,2048]{3,2,1,0:T(8,128)(2,1)S(1)}, u32[]{:S(2)}, u32[]{:S(2)}) collective-permute-start(bf16[4,2,16,2048]{3,2,1,0:T(8,128)(2,1)S(1)} %pad_maximum_fusion.1.rest_4_.rest_14_), channel_id=1, source_target_pairs={{0,96},{32,0},{64,32},{96,64},{1,97},{33,1},{65,33},{97,65},{2,98}... | collective-permute-start | bytes 1572872 | tf_op jit(solution)/shard_map/ppermute | solution.py:32
  160.3 2.2 collective-permute-done.2
  164.0 2.8 collective-permute-start.5
  167.3 4.4 %collective-permute-done.11.rest_6_.rest_16_ = bf16[4,2,16,2048]{3,2,1,0:T(8,128)(2,1)S(1)} collective-permute-done((bf16[4,2,16,2048]{3,2,1,0:T(8,128)(2,1)S(1)}, bf16[4,2,16,2048]{3,2,1,0:T(8,128)(2,1)S(1)}, u32[]{:S(2)}, u32[]{:S(2)}) %collective-permute-start.11) | collective-permute-done | bytes 524320 | tf_op jit(solution)/shard_map/ppermute | solution.py:32
  172.0 5.2 %collective-permute-done.4.rest_1_.rest_11_ = bf16[4,2,16,2048]{3,2,1,0:T(8,128)(2,1)S(1)} collective-permute-done((bf16[4,2,16,2048]{3,2,1,0:T(8,128)(2,1)S(1)}, bf16[4,2,16,2048]{3,2,1,0:T(8,128)(2,1)S(1)}, u32[]{:S(2)}, u32[]{:S(2)}) %collective-permute-start.4) | collective-permute-done | bytes 524320 | tf_op jit(solution)/shard_map/ppermute | solution.py:32
  177.3 10.6 %collective-permute-done.5.rest_2_.rest_12_ = bf16[4,2,16,2048]{3,2,1,0:T(8,128)(2,1)S(1)} collective-permute-done((bf16[4,2,16,2048]{3,2,1,0:T(8,128)(2,1)S(1)}, bf16[4,2,16,2048]{3,2,1,0:T(8,128)(2,1)S(1)}, u32[]{:S(2)}, u32[]{:S(2)}) %collective-permute-start.5) | collective-permute-done | bytes 524320 | tf_op jit(solution)/shard_map/ppermute | solution.py:32
  188.8 13.5 %shard_map.39.inverse = bf16[512,512]{1,0:T(8,128)(2,1)} custom-call(s32[3]{0:T(128)} %pad_add_fusion.pos, bf16[4,2,16,2048]{3,2,1,0:T(8,128)(2,1)} %copy-done, bf16[4,2,16,2048]{3,2,1,0:T(8,128)(2,1)} %copy-done.4, bf16[2,2,16,2048]{3,2,1,0:T(8,128)(2,1)} %copy-done.19, bf16[2,2,16,2048]{3,2,1,0:T(8,128)(2,1)} %collective-permute-done.20.rest_3_, ...), custom_call_target="tpu_custom_call" | custom-call | tf_op jit(solution)/shard_map/pallas_call | solution.py:377
  202.3 4.7 %shard_map.40 = bf16[512,128]{1,0:T(8,128)(2,1)} custom-call(bf16[32,528,128]{2,1,0:T(8,128)(2,1)} %all-to-all-done.parts.levels, bf16[32,528,128]{2,1,0:T(8,128)(2,1)} %all-to-all-done.parts.levels, bf16[512,512]{1,0:T(8,128)(2,1)} %shard_map.39.inverse), custom_call_target="tpu_custom_call" | custom-call | tf_op jit(solution)/shard_map/pallas_call | solution.py:386
  207.0 2.5 collective-permute-start.28
  209.5 3.2 %collective-permute-done.28 = bf16[512,128]{1,0:T(8,128)(2,1)S(1)} collective-permute-done((bf16[512,128]{1,0:T(8,128)(2,1)}, bf16[512,128]{1,0:T(8,128)(2,1)S(1)}, u32[]{:S(2)}, u32[]{:S(2)}) %collective-permute-start.28) | collective-permute-done | bytes 131104 | tf_op jit(solution)/shard_map/ppermute | solution.py:32
  214.7 2.6 collective-permute-start.37
  217.5 3.6 %collective-permute-done.36 = bf16[512,128]{1,0:T(8,128)(2,1)S(1)} collective-permute-done((bf16[512,128]{1,0:T(8,128)(2,1)S(1)}, bf16[512,128]{1,0:T(8,128)(2,1)S(1)}, u32[]{:S(2)}, u32[]{:S(2)}) %collective-permute-start.36) | collective-permute-done | bytes 131104 | tf_op jit(solution)/shard_map/ppermute | solution.py:32
  221.1 1.8 collective-permute-done.37
  223.3 3.1 %collective-permute-start.41 = (bf16[4,512,128]{2,1,0:T(8,128)(2,1)S(1)}, bf16[4,512,128]{2,1,0:T(8,128)(2,1)S(1)}, u32[]{:S(2)}, u32[]{:S(2)}) collective-permute-start(bf16[4,512,128]{2,1,0:T(8,128)(2,1)S(1)} %pad_maximum_fusion.5.rest_1_), channel_id=1, source_target_pairs={{0,96},{32,0},{64,32},{96,64},{1,97},{33,1},{65,33},{97,65},{2,98}... | collective-permute-start | bytes 1572872 | tf_op jit(solution)/shard_map/ppermute | solution.py:32
  226.4 2.3 collective-permute-done.31
  230.0 2.1 collective-permute-start.34
  232.1 4.9 %collective-permute-done.39.rest_1_ = bf16[4,512,128]{2,1,0:T(8,128)(2,1)S(1)} collective-permute-done((bf16[4,512,128]{2,1,0:T(8,128)(2,1)S(1)}, bf16[4,512,128]{2,1,0:T(8,128)(2,1)S(1)}, u32[]{:S(2)}, u32[]{:S(2)}) %collective-permute-start.39) | collective-permute-done | bytes 524320 | tf_op jit(solution)/shard_map/ppermute | solution.py:32
  238.5 3.2 %collective-permute-start.42 = (bf16[2,512,128]{2,1,0:T(8,128)(2,1)}, bf16[2,512,128]{2,1,0:T(8,128)(2,1)}, u32[]{:S(2)}, u32[]{:S(2)}) collective-permute-start(bf16[2,512,128]{2,1,0:T(8,128)(2,1)} %slice.59), channel_id=1, source_target_pairs={{0,96},{32,0},{64,32},{96,64},{1,97},{33,1},{65,33},{97,65},{2,98}... | collective-permute-start | bytes 786440 | tf_op jit(solution)/shard_map/ppermute | solution.py:32
  244.9 1.7 collective-permute-start.35
  246.6 16.3 %shard_map.37.weights = bf16[32,512,512]{2,1,0:T(8,128)(2,1)} custom-call(s32[3]{0:T(128)} %pad_add_fusion.pos, bf16[512,4096]{1,0:T(8,128)(2,1)} %queries.1, bf16[4,2,16,2048]{3,2,1,0:T(8,128)(2,1)} %copy-done.3, bf16[4,2,16,2048]{3,2,1,0:T(8,128)(2,1)} %copy-done.11, bf16[4,2,16,2048]{3,2,1,0:T(8,128)(2,1)} %copy-done.12, ...), custom_call_target="tpu_custom_call" | custom-call | tf_op jit(solution)/shard_map/pallas_call | solution.py:364
  262.9 5.4 %shard_map.41.rest_4_ = bf16[512,4096]{1,0:T(8,128)(2,1)} custom-call(s32[3]{0:T(128)} %pad_add_fusion.pos, bf16[32,512,512]{2,1,0:T(8,128)(2,1)} %shard_map.37.weights, bf16[4,512,128]{2,1,0:T(8,128)(2,1)} %copy-done.14, bf16[4,512,128]{2,1,0:T(8,128)(2,1)} %copy-done.13), custom_call_target="tpu_custom_call" | custom-call | tf_op jit(solution)/shard_map/pallas_call | solution.py:300
  268.3 8.5 %shard_map.42.rest_4_ = bf16[512,4096]{1,0:T(8,128)(2,1)} custom-call(s32[3]{0:T(128)} %pad_add_fusion.pos, bf16[32,512,512]{2,1,0:T(8,128)(2,1)} %shard_map.37.weights, bf16[4,512,128]{2,1,0:T(8,128)(2,1)} %copy-done.17, bf16[4,512,128]{2,1,0:T(8,128)(2,1)} %copy-done.15, bf16[4,512,128]{2,1,0:T(8,128)(2,1)} %copy-done.18, ...), custom_call_target="tpu_custom_call", output_to_operand_aliasing={{}: (6, {})} | custom-call | tf_op jit(solution)/shard_map/pallas_call | solution.py:300
  277.5 5.4 %shard_map.43 = bf16[512,4096]{1,0:T(8,128)(2,1)} custom-call(s32[3]{0:T(128)} %pad_add_fusion.pos, bf16[32,512,512]{2,1,0:T(8,128)(2,1)} %shard_map.37.weights, bf16[2,512,128]{2,1,0:T(8,128)(2,1)} %collective-permute-done.33.rest_0_, bf16[2,512,128]{2,1,0:T(8,128)(2,1)} %collective-permute-done.35.rest_1_, ...), custom_call_target="tpu_custom_call", output_to_operand_aliasing={{}: (6, {})} | custom-call | tf_op jit(solution)/shard_map/pallas_call | solution.py:300
  (113 shorter events, 25.1 us)
Async XLA Ops:
  3.3 5.3 %collective-permute-start.13 = (bf16[16,4096]{1,0:T(8,128)(2,1)S(1)}, bf16[16,4096]{1,0:T(8,128)(2,1)S(1)}, u32[]{:S(2)}, u32[]{:S(2)}) collective-permute-start(bf16[16,4096]{1,0:T(8,128)(2,1)S(1)} %multiply_convert_fusion), channel_id=1, source_target_pairs={{0,4},{4,0},{1,5},{5,1},{2,6},{6,2},{3,7},{7,3},{8,12},{12,8},{9,1... | collective-permute-start | bytes 393224 | tf_op jit(solution)/shard_map/ppermute | solution.py:32
  8.6 11.4 %collective-permute-start.14 = (bf16[2,16,2048]{2,1,0:T(8,128)(2,1)S(1)}, bf16[2,16,2048]{2,1,0:T(8,128)(2,1)S(1)}, u32[]{:S(2)}, u32[]{:S(2)}) collective-permute-start(bf16[2,16,2048]{2,1,0:T(8,128)(2,1)S(1)} %get-tuple-element.8), channel_id=1, source_target_pairs={{0,32},{32,64},{64,96},{96,0},{1,33},{33,65},{65,97},{97,1},{2,34}... | collective-permute-start | bytes 393224 | tf_op jit(solution)/shard_map/ppermute | solution.py:32
  10.3 10.7 %collective-permute-start.15 = (bf16[2,16,2048]{2,1,0:T(8,128)(2,1)S(1)}, bf16[2,16,2048]{2,1,0:T(8,128)(2,1)S(1)}, u32[]{:S(2)}, u32[]{:S(2)}) collective-permute-start(bf16[2,16,2048]{2,1,0:T(8,128)(2,1)S(1)} %get-tuple-element.8), channel_id=1, source_target_pairs={{0,64},{32,96},{64,0},{96,32},{1,65},{33,97},{65,1},{97,33},{2,66}... | collective-permute-start | bytes 393224 | tf_op jit(solution)/shard_map/ppermute | solution.py:32
  13.1 8.0 %collective-permute-start.16 = (bf16[2,16,2048]{2,1,0:T(8,128)(2,1)S(1)}, bf16[2,16,2048]{2,1,0:T(8,128)(2,1)S(1)}, u32[]{:S(2)}, u32[]{:S(2)}) collective-permute-start(bf16[2,16,2048]{2,1,0:T(8,128)(2,1)S(1)} %get-tuple-element.8), channel_id=1, source_target_pairs={{0,96},{32,0},{64,32},{96,64},{1,97},{33,1},{65,33},{97,65},{2,98}... | collective-permute-start | bytes 393224 | tf_op jit(solution)/shard_map/ppermute | solution.py:32
  14.5 9.9 %collective-permute-start.21 = (bf16[2,16,2048]{2,1,0:T(8,128)(2,1)S(1)}, bf16[2,16,2048]{2,1,0:T(8,128)(2,1)S(1)}, u32[]{:S(2)}, u32[]{:S(2)}) collective-permute-start(bf16[2,16,2048]{2,1,0:T(8,128)(2,1)S(1)} %get-tuple-element.7), channel_id=1, source_target_pairs={{0,8},{8,16},{16,24},{24,0},{1,9},{9,17},{17,25},{25,1},{2,10},{10... | collective-permute-start | bytes 393224 | tf_op jit(solution)/shard_map/ppermute | solution.py:32
  16.4 9.6 %collective-permute-start.22 = (bf16[2,16,2048]{2,1,0:T(8,128)(2,1)S(1)}, bf16[2,16,2048]{2,1,0:T(8,128)(2,1)S(1)}, u32[]{:S(2)}, u32[]{:S(2)}) collective-permute-start(bf16[2,16,2048]{2,1,0:T(8,128)(2,1)S(1)} %get-tuple-element.7), channel_id=1, source_target_pairs={{0,16},{8,24},{16,0},{24,8},{1,17},{9,25},{17,1},{25,9},{2,18},{10... | collective-permute-start | bytes 393224 | tf_op jit(solution)/shard_map/ppermute | solution.py:32
  20.0 6.5 %collective-permute-start.23 = (bf16[2,16,2048]{2,1,0:T(8,128)(2,1)S(1)}, bf16[2,16,2048]{2,1,0:T(8,128)(2,1)S(1)}, u32[]{:S(2)}, u32[]{:S(2)}) collective-permute-start(bf16[2,16,2048]{2,1,0:T(8,128)(2,1)S(1)} %get-tuple-element.7), channel_id=1, source_target_pairs={{0,24},{8,0},{16,8},{24,16},{1,25},{9,1},{17,9},{25,17},{2,26},{10... | collective-permute-start | bytes 393224 | tf_op jit(solution)/shard_map/ppermute | solution.py:32
  21.1 28.2 %copy-start = (bf16[4,2,16,2048]{3,2,1,0:T(8,128)(2,1)}, bf16[4,2,16,2048]{3,2,1,0:T(8,128)(2,1)S(1)}, u32[]{:S(2)}) copy-start(bf16[4,2,16,2048]{3,2,1,0:T(8,128)(2,1)S(1)} %pad_maximum_fusion.2.rest_0_) | copy-start | bytes 1572868
  21.1 14.4 %collective-permute-start.17 = (bf16[4,2,16,2048]{3,2,1,0:T(8,128)(2,1)S(1)}, bf16[4,2,16,2048]{3,2,1,0:T(8,128)(2,1)S(1)}, u32[]{:S(2)}, u32[]{:S(2)}) collective-permute-start(bf16[4,2,16,2048]{3,2,1,0:T(8,128)(2,1)S(1)} %pad_maximum_fusion.2.rest_0_), channel_id=1, source_target_pairs={{0,8},{8,16},{16,24},{24,0},{1,9},{9,17},{17,25},{25,1},{2,10},{10... | collective-permute-start | bytes 1572872 | tf_op jit(solution)/shard_map/ppermute | solution.py:32
  22.2 14.1 %collective-permute-start.19 = (bf16[4,2,16,2048]{3,2,1,0:T(8,128)(2,1)S(1)}, bf16[4,2,16,2048]{3,2,1,0:T(8,128)(2,1)S(1)}, u32[]{:S(2)}, u32[]{:S(2)}) collective-permute-start(bf16[4,2,16,2048]{3,2,1,0:T(8,128)(2,1)S(1)} %pad_maximum_fusion.2.rest_0_), channel_id=1, source_target_pairs={{0,24},{8,0},{16,8},{24,16},{1,25},{9,1},{17,9},{25,17},{2,26},{10... | collective-permute-start | bytes 1572872 | tf_op jit(solution)/shard_map/ppermute | solution.py:32
  26.6 13.7 %collective-permute-start.24 = (bf16[4,2,16,2048]{3,2,1,0:T(8,128)(2,1)S(1)}, bf16[4,2,16,2048]{3,2,1,0:T(8,128)(2,1)S(1)}, u32[]{:S(2)}, u32[]{:S(2)}) collective-permute-start(bf16[4,2,16,2048]{3,2,1,0:T(8,128)(2,1)S(1)} %pad_maximum_fusion.3.rest_5_), channel_id=1, source_target_pairs={{0,32},{32,64},{64,96},{96,0},{1,33},{33,65},{65,97},{97,1},{2,34}... | collective-permute-start | bytes 1572872 | tf_op jit(solution)/shard_map/ppermute | solution.py:32
  27.3 14.4 %collective-permute-start.26 = (bf16[4,2,16,2048]{3,2,1,0:T(8,128)(2,1)S(1)}, bf16[4,2,16,2048]{3,2,1,0:T(8,128)(2,1)S(1)}, u32[]{:S(2)}, u32[]{:S(2)}) collective-permute-start(bf16[4,2,16,2048]{3,2,1,0:T(8,128)(2,1)S(1)} %pad_maximum_fusion.3.rest_5_), channel_id=1, source_target_pairs={{0,96},{32,0},{64,32},{96,64},{1,97},{33,1},{65,33},{97,65},{2,98}... | collective-permute-start | bytes 1572872 | tf_op jit(solution)/shard_map/ppermute | solution.py:32
  36.3 9.5 %collective-permute-start.18 = (bf16[2,2,16,2048]{3,2,1,0:T(8,128)(2,1)}, bf16[2,2,16,2048]{3,2,1,0:T(8,128)(2,1)S(1)}, u32[]{:S(2)}, u32[]{:S(2)}) collective-permute-start(bf16[2,2,16,2048]{3,2,1,0:T(8,128)(2,1)} %slice.52), channel_id=1, source_target_pairs={{0,8},{8,16},{16,24},{24,0},{1,9},{9,17},{17,25},{25,1},{2,10},{10... | collective-permute-start | bytes 786440 | tf_op jit(solution)/shard_map/ppermute | solution.py:32
  37.1 8.7 %collective-permute-start.20 = (bf16[2,2,16,2048]{3,2,1,0:T(8,128)(2,1)}, bf16[2,2,16,2048]{3,2,1,0:T(8,128)(2,1)}, u32[]{:S(2)}, u32[]{:S(2)}) collective-permute-start(bf16[2,2,16,2048]{3,2,1,0:T(8,128)(2,1)} %slice.53), channel_id=1, source_target_pairs={{0,24},{8,0},{16,8},{24,16},{1,25},{9,1},{17,9},{25,17},{2,26},{10... | collective-permute-start | bytes 786440 | tf_op jit(solution)/shard_map/ppermute | solution.py:32
  41.1 7.9 %collective-permute-start.25 = (bf16[2,2,16,2048]{3,2,1,0:T(8,128)(2,1)}, bf16[2,2,16,2048]{3,2,1,0:T(8,128)(2,1)}, u32[]{:S(2)}, u32[]{:S(2)}) collective-permute-start(bf16[2,2,16,2048]{3,2,1,0:T(8,128)(2,1)} %slice.54), channel_id=1, source_target_pairs={{0,32},{32,64},{64,96},{96,0},{1,33},{33,65},{65,97},{97,1},{2,34}... | collective-permute-start | bytes 786440 | tf_op jit(solution)/shard_map/ppermute | solution.py:32
  42.5 6.9 %collective-permute-start.27 = (bf16[2,2,16,2048]{3,2,1,0:T(8,128)(2,1)}, bf16[2,2,16,2048]{3,2,1,0:T(8,128)(2,1)}, u32[]{:S(2)}, u32[]{:S(2)}) collective-permute-start(bf16[2,2,16,2048]{3,2,1,0:T(8,128)(2,1)} %slice.55), channel_id=1, source_target_pairs={{0,96},{32,0},{64,32},{96,64},{1,97},{33,1},{65,33},{97,65},{2,98}... | collective-permute-start | bytes 786440 | tf_op jit(solution)/shard_map/ppermute | solution.py:32
  66.5 135.7 %all-to-all-start = ((bf16[32,528,128]{2,1,0:T(8,128)(2,1)}), bf16[32,528,128]{2,1,0:T(8,128)(2,1)}, u32[]{:S(2)}, u32[]{:S(2)}) async-start(bf16[32,528,128]{2,1,0:T(8,128)(2,1)} %shard_map.38), calls=%async_computation | async-start | bytes 8650752 | tf_op jit(solution)/shard_map/all_to_all | solution.py:362
  76.8 46.6 %collective-permute-start = (bf16[16,4096]{1,0:T(8,128)(2,1)S(1)}, bf16[16,4096]{1,0:T(8,128)(2,1)S(1)}, u32[]{:S(2)}, u32[]{:S(2)}) collective-permute-start(bf16[16,4096]{1,0:T(8,128)(2,1)S(1)} %multiply_convert_fusion.1), channel_id=1, source_target_pairs={{0,4},{4,0},{1,5},{5,1},{2,6},{6,2},{3,7},{7,3},{8,12},{12,8},{9,1... | collective-permute-start | bytes 393224 | tf_op jit(solution)/shard_map/ppermute | solution.py:32
  123.4 8.9 %collective-permute-start.7 = (bf16[2,16,2048]{2,1,0:T(8,128)(2,1)S(1)}, bf16[2,16,2048]{2,1,0:T(8,128)(2,1)S(1)}, u32[]{:S(2)}, u32[]{:S(2)}) collective-permute-start(bf16[2,16,2048]{2,1,0:T(8,128)(2,1)S(1)} %get-tuple-element.9), channel_id=1, source_target_pairs={{0,8},{8,16},{16,24},{24,0},{1,9},{9,17},{17,25},{25,1},{2,10},{10... | collective-permute-start | bytes 393224 | tf_op jit(solution)/shard_map/ppermute | solution.py:32
  129.2 6.5 %collective-permute-start.8 = (bf16[2,16,2048]{2,1,0:T(8,128)(2,1)S(1)}, bf16[2,16,2048]{2,1,0:T(8,128)(2,1)S(1)}, u32[]{:S(2)}, u32[]{:S(2)}) collective-permute-start(bf16[2,16,2048]{2,1,0:T(8,128)(2,1)S(1)} %get-tuple-element.9), channel_id=1, source_target_pairs={{0,16},{8,24},{16,0},{24,8},{1,17},{9,25},{17,1},{25,9},{2,18},{10... | collective-permute-start | bytes 393224 | tf_op jit(solution)/shard_map/ppermute | solution.py:32
  129.7 6.0 %collective-permute-start.9 = (bf16[2,16,2048]{2,1,0:T(8,128)(2,1)S(1)}, bf16[2,16,2048]{2,1,0:T(8,128)(2,1)S(1)}, u32[]{:S(2)}, u32[]{:S(2)}) collective-permute-start(bf16[2,16,2048]{2,1,0:T(8,128)(2,1)S(1)} %get-tuple-element.9), channel_id=1, source_target_pairs={{0,24},{8,0},{16,8},{24,16},{1,25},{9,1},{17,9},{25,17},{2,26},{10... | collective-permute-start | bytes 393224 | tf_op jit(solution)/shard_map/ppermute | solution.py:32
  135.8 52.9 %copy-start.1 = (bf16[4,2,16,2048]{3,2,1,0:T(8,128)(2,1)}, bf16[4,2,16,2048]{3,2,1,0:T(8,128)(2,1)S(1)}, u32[]{:S(2)}) copy-start(bf16[4,2,16,2048]{3,2,1,0:T(8,128)(2,1)S(1)} %pad_maximum_fusion.1.rest_4_.rest_14_) | copy-start | bytes 1572868
  135.8 31.0 %collective-permute-start.10 = (bf16[4,2,16,2048]{3,2,1,0:T(8,128)(2,1)S(1)}, bf16[4,2,16,2048]{3,2,1,0:T(8,128)(2,1)S(1)}, u32[]{:S(2)}, u32[]{:S(2)}) collective-permute-start(bf16[4,2,16,2048]{3,2,1,0:T(8,128)(2,1)S(1)} %pad_maximum_fusion.1.rest_4_.rest_14_), channel_id=1, source_target_pairs={{0,32},{32,64},{64,96},{96,0},{1,33},{33,65},{65,97},{97,1},{2,34}... | collective-permute-start | bytes 1572872 | tf_op jit(solution)/shard_map/ppermute | solution.py:32
  141.1 16.3 %collective-permute-start.1 = (bf16[2,16,2048]{2,1,0:T(8,128)(2,1)S(1)}, bf16[2,16,2048]{2,1,0:T(8,128)(2,1)S(1)}, u32[]{:S(2)}, u32[]{:S(2)}) collective-permute-start(bf16[2,16,2048]{2,1,0:T(8,128)(2,1)S(1)} %get-tuple-element.10), channel_id=1, source_target_pairs={{0,32},{32,64},{64,96},{96,0},{1,33},{33,65},{65,97},{97,1},{2,34}... | collective-permute-start | bytes 393224 | tf_op jit(solution)/shard_map/ppermute | solution.py:32
  141.2 21.3 %collective-permute-start.2 = (bf16[2,16,2048]{2,1,0:T(8,128)(2,1)S(1)}, bf16[2,16,2048]{2,1,0:T(8,128)(2,1)S(1)}, u32[]{:S(2)}, u32[]{:S(2)}) collective-permute-start(bf16[2,16,2048]{2,1,0:T(8,128)(2,1)S(1)} %get-tuple-element.10), channel_id=1, source_target_pairs={{0,64},{32,96},{64,0},{96,32},{1,65},{33,97},{65,1},{97,33},{2,66}... | collective-permute-start | bytes 393224 | tf_op jit(solution)/shard_map/ppermute | solution.py:32
  144.2 18.3 %collective-permute-start.3 = (bf16[2,16,2048]{2,1,0:T(8,128)(2,1)S(1)}, bf16[2,16,2048]{2,1,0:T(8,128)(2,1)S(1)}, u32[]{:S(2)}, u32[]{:S(2)}) collective-permute-start(bf16[2,16,2048]{2,1,0:T(8,128)(2,1)S(1)} %get-tuple-element.10), channel_id=1, source_target_pairs={{0,96},{32,0},{64,32},{96,64},{1,97},{33,1},{65,33},{97,65},{2,98}... | collective-permute-start | bytes 393224 | tf_op jit(solution)/shard_map/ppermute | solution.py:32
  146.8 24.9 %collective-permute-start.11 = (bf16[4,2,16,2048]{3,2,1,0:T(8,128)(2,1)S(1)}, bf16[4,2,16,2048]{3,2,1,0:T(8,128)(2,1)S(1)}, u32[]{:S(2)}, u32[]{:S(2)}) collective-permute-start(bf16[4,2,16,2048]{3,2,1,0:T(8,128)(2,1)S(1)} %pad_maximum_fusion.1.rest_4_.rest_14_), channel_id=1, source_target_pairs={{0,64},{32,96},{64,0},{96,32},{1,65},{33,97},{65,1},{97,33},{2,66}... | collective-permute-start | bytes 1572872 | tf_op jit(solution)/shard_map/ppermute | solution.py:32
  157.4 14.6 %collective-permute-start.12 = (bf16[4,2,16,2048]{3,2,1,0:T(8,128)(2,1)S(1)}, bf16[4,2,16,2048]{3,2,1,0:T(8,128)(2,1)S(1)}, u32[]{:S(2)}, u32[]{:S(2)}) collective-permute-start(bf16[4,2,16,2048]{3,2,1,0:T(8,128)(2,1)S(1)} %pad_maximum_fusion.1.rest_4_.rest_14_), channel_id=1, source_target_pairs={{0,96},{32,0},{64,32},{96,64},{1,97},{33,1},{65,33},{97,65},{2,98}... | collective-permute-start | bytes 1572872 | tf_op jit(solution)/shard_map/ppermute | solution.py:32
  162.6 14.6 %collective-permute-start.4 = (bf16[4,2,16,2048]{3,2,1,0:T(8,128)(2,1)S(1)}, bf16[4,2,16,2048]{3,2,1,0:T(8,128)(2,1)S(1)}, u32[]{:S(2)}, u32[]{:S(2)}) collective-permute-start(bf16[4,2,16,2048]{3,2,1,0:T(8,128)(2,1)S(1)} %pad_maximum_fusion.rest_0_.rest_10_), channel_id=1, source_target_pairs={{0,8},{8,16},{16,24},{24,0},{1,9},{9,17},{17,25},{25,1},{2,10},{10... | collective-permute-start | bytes 1572872 | tf_op jit(solution)/shard_map/ppermute | solution.py:32
  164.0 23.9 %collective-permute-start.5 = (bf16[4,2,16,2048]{3,2,1,0:T(8,128)(2,1)S(1)}, bf16[4,2,16,2048]{3,2,1,0:T(8,128)(2,1)S(1)}, u32[]{:S(2)}, u32[]{:S(2)}) collective-permute-start(bf16[4,2,16,2048]{3,2,1,0:T(8,128)(2,1)S(1)} %pad_maximum_fusion.rest_0_.rest_10_), channel_id=1, source_target_pairs={{0,16},{8,24},{16,0},{24,8},{1,17},{9,25},{17,1},{25,9},{2,18},{10... | collective-permute-start | bytes 1572872 | tf_op jit(solution)/shard_map/ppermute | solution.py:32
  166.8 21.9 %collective-permute-start.6 = (bf16[4,2,16,2048]{3,2,1,0:T(8,128)(2,1)S(1)}, bf16[4,2,16,2048]{3,2,1,0:T(8,128)(2,1)}, u32[]{:S(2)}, u32[]{:S(2)}) collective-permute-start(bf16[4,2,16,2048]{3,2,1,0:T(8,128)(2,1)S(1)} %pad_maximum_fusion.rest_0_.rest_10_), channel_id=1, source_target_pairs={{0,24},{8,0},{16,8},{24,16},{1,25},{9,1},{17,9},{25,17},{2,26},{10... | collective-permute-start | bytes 1572872 | tf_op jit(solution)/shard_map/ppermute | solution.py:32
  207.0 5.7 %collective-permute-start.28 = (bf16[512,128]{1,0:T(8,128)(2,1)}, bf16[512,128]{1,0:T(8,128)(2,1)S(1)}, u32[]{:S(2)}, u32[]{:S(2)}) collective-permute-start(bf16[512,128]{1,0:T(8,128)(2,1)} %shard_map.40), channel_id=1, source_target_pairs={{0,4},{4,0},{1,5},{5,1},{2,6},{6,2},{3,7},{7,3},{8,12},{12,8},{9,1... | collective-permute-start | bytes 393224 | tf_op jit(solution)/shard_map/ppermute | solution.py:32
  213.6 7.5 %collective-permute-start.36 = (bf16[512,128]{1,0:T(8,128)(2,1)S(1)}, bf16[512,128]{1,0:T(8,128)(2,1)S(1)}, u32[]{:S(2)}, u32[]{:S(2)}) collective-permute-start(bf16[512,128]{1,0:T(8,128)(2,1)S(1)} %get-tuple-element.5), channel_id=1, source_target_pairs={{0,8},{8,16},{16,24},{24,0},{1,9},{9,17},{17,25},{25,1},{2,10},{10... | collective-permute-start | bytes 393224 | tf_op jit(solution)/shard_map/ppermute | solution.py:32
  214.7 8.2 %collective-permute-start.37 = (bf16[512,128]{1,0:T(8,128)(2,1)S(1)}, bf16[512,128]{1,0:T(8,128)(2,1)S(1)}, u32[]{:S(2)}, u32[]{:S(2)}) collective-permute-start(bf16[512,128]{1,0:T(8,128)(2,1)S(1)} %get-tuple-element.5), channel_id=1, source_target_pairs={{0,16},{8,24},{16,0},{24,8},{1,17},{9,25},{17,1},{25,9},{2,18},{10... | collective-permute-start | bytes 393224 | tf_op jit(solution)/shard_map/ppermute | solution.py:32
  217.3 5.7 %collective-permute-start.38 = (bf16[512,128]{1,0:T(8,128)(2,1)S(1)}, bf16[512,128]{1,0:T(8,128)(2,1)S(1)}, u32[]{:S(2)}, u32[]{:S(2)}) collective-permute-start(bf16[512,128]{1,0:T(8,128)(2,1)S(1)} %get-tuple-element.5), channel_id=1, source_target_pairs={{0,24},{8,0},{16,8},{24,16},{1,25},{9,1},{17,9},{25,17},{2,26},{10... | collective-permute-start | bytes 393224 | tf_op jit(solution)/shard_map/ppermute | solution.py:32
  217.5 8.9 %collective-permute-start.29 = (bf16[512,128]{1,0:T(8,128)(2,1)S(1)}, bf16[512,128]{1,0:T(8,128)(2,1)S(1)}, u32[]{:S(2)}, u32[]{:S(2)}) collective-permute-start(bf16[512,128]{1,0:T(8,128)(2,1)S(1)} %get-tuple-element.6), channel_id=1, source_target_pairs={{0,32},{32,64},{64,96},{96,0},{1,33},{33,65},{65,97},{97,1},{2,34}... | collective-permute-start | bytes 393224 | tf_op jit(solution)/shard_map/ppermute | solution.py:32
  217.5 8.9 %collective-permute-start.30 = (bf16[512,128]{1,0:T(8,128)(2,1)S(1)}, bf16[512,128]{1,0:T(8,128)(2,1)S(1)}, u32[]{:S(2)}, u32[]{:S(2)}) collective-permute-start(bf16[512,128]{1,0:T(8,128)(2,1)S(1)} %get-tuple-element.6), channel_id=1, source_target_pairs={{0,64},{32,96},{64,0},{96,32},{1,65},{33,97},{65,1},{97,33},{2,66}... | collective-permute-start | bytes 393224 | tf_op jit(solution)/shard_map/ppermute | solution.py:32
  221.1 7.6 %collective-permute-start.31 = (bf16[512,128]{1,0:T(8,128)(2,1)S(1)}, bf16[512,128]{1,0:T(8,128)(2,1)S(1)}, u32[]{:S(2)}, u32[]{:S(2)}) collective-permute-start(bf16[512,128]{1,0:T(8,128)(2,1)S(1)} %get-tuple-element.6), channel_id=1, source_target_pairs={{0,96},{32,0},{64,32},{96,64},{1,97},{33,1},{65,33},{97,65},{2,98}... | collective-permute-start | bytes 393224 | tf_op jit(solution)/shard_map/ppermute | solution.py:32
  223.0 39.8 %copy-start.13 = (bf16[4,512,128]{2,1,0:T(8,128)(2,1)}, bf16[4,512,128]{2,1,0:T(8,128)(2,1)S(1)}, u32[]{:S(2)}) copy-start(bf16[4,512,128]{2,1,0:T(8,128)(2,1)S(1)} %pad_maximum_fusion.5.rest_1_) | copy-start | bytes 1572868
  223.1 13.9 %collective-permute-start.39 = (bf16[4,512,128]{2,1,0:T(8,128)(2,1)S(1)}, bf16[4,512,128]{2,1,0:T(8,128)(2,1)S(1)}, u32[]{:S(2)}, u32[]{:S(2)}) collective-permute-start(bf16[4,512,128]{2,1,0:T(8,128)(2,1)S(1)} %pad_maximum_fusion.5.rest_1_), channel_id=1, source_target_pairs={{0,32},{32,64},{64,96},{96,0},{1,33},{33,65},{65,97},{97,1},{2,34}... | collective-permute-start | bytes 1572872 | tf_op jit(solution)/shard_map/ppermute | solution.py:32
  223.3 14.5 %collective-permute-start.41 = (bf16[4,512,128]{2,1,0:T(8,128)(2,1)S(1)}, bf16[4,512,128]{2,1,0:T(8,128)(2,1)S(1)}, u32[]{:S(2)}, u32[]{:S(2)}) collective-permute-start(bf16[4,512,128]{2,1,0:T(8,128)(2,1)S(1)} %pad_maximum_fusion.5.rest_1_), channel_id=1, source_target_pairs={{0,96},{32,0},{64,32},{96,64},{1,97},{33,1},{65,33},{97,65},{2,98}... | collective-permute-start | bytes 1572872 | tf_op jit(solution)/shard_map/ppermute | solution.py:32
  228.8 34.1 %copy-start.14 = (bf16[4,512,128]{2,1,0:T(8,128)(2,1)}, bf16[4,512,128]{2,1,0:T(8,128)(2,1)S(1)}, u32[]{:S(2)}) copy-start(bf16[4,512,128]{2,1,0:T(8,128)(2,1)S(1)} %pad_maximum_fusion.4.rest_0_) | copy-start | bytes 1572868
  228.8 13.0 %collective-permute-start.32 = (bf16[4,512,128]{2,1,0:T(8,128)(2,1)S(1)}, bf16[4,512,128]{2,1,0:T(8,128)(2,1)S(1)}, u32[]{:S(2)}, u32[]{:S(2)}) collective-permute-start(bf16[4,512,128]{2,1,0:T(8,128)(2,1)S(1)} %pad_maximum_fusion.4.rest_0_), channel_id=1, source_target_pairs={{0,8},{8,16},{16,24},{24,0},{1,9},{9,17},{17,25},{25,1},{2,10},{10... | collective-permute-start | bytes 1572872 | tf_op jit(solution)/shard_map/ppermute | solution.py:32
  230.0 14.1 %collective-permute-start.34 = (bf16[4,512,128]{2,1,0:T(8,128)(2,1)S(1)}, bf16[4,512,128]{2,1,0:T(8,128)(2,1)S(1)}, u32[]{:S(2)}, u32[]{:S(2)}) collective-permute-start(bf16[4,512,128]{2,1,0:T(8,128)(2,1)S(1)} %pad_maximum_fusion.4.rest_0_), channel_id=1, source_target_pairs={{0,24},{8,0},{16,8},{24,16},{1,25},{9,1},{17,9},{25,17},{2,26},{10... | collective-permute-start | bytes 1572872 | tf_op jit(solution)/shard_map/ppermute | solution.py:32
  237.8 39.0 %collective-permute-start.40 = (bf16[2,512,128]{2,1,0:T(8,128)(2,1)}, bf16[2,512,128]{2,1,0:T(8,128)(2,1)S(1)}, u32[]{:S(2)}, u32[]{:S(2)}) collective-permute-start(bf16[2,512,128]{2,1,0:T(8,128)(2,1)} %slice.58), channel_id=1, source_target_pairs={{0,32},{32,64},{64,96},{96,0},{1,33},{33,65},{65,97},{97,1},{2,34}... | collective-permute-start | bytes 786440 | tf_op jit(solution)/shard_map/ppermute | solution.py:32
  238.5 38.3 %collective-permute-start.42 = (bf16[2,512,128]{2,1,0:T(8,128)(2,1)}, bf16[2,512,128]{2,1,0:T(8,128)(2,1)}, u32[]{:S(2)}, u32[]{:S(2)}) collective-permute-start(bf16[2,512,128]{2,1,0:T(8,128)(2,1)} %slice.59), channel_id=1, source_target_pairs={{0,96},{32,0},{64,32},{96,64},{1,97},{33,1},{65,33},{97,65},{2,98}... | collective-permute-start | bytes 786440 | tf_op jit(solution)/shard_map/ppermute | solution.py:32
  242.6 34.2 %collective-permute-start.33 = (bf16[2,512,128]{2,1,0:T(8,128)(2,1)}, bf16[2,512,128]{2,1,0:T(8,128)(2,1)}, u32[]{:S(2)}, u32[]{:S(2)}) collective-permute-start(bf16[2,512,128]{2,1,0:T(8,128)(2,1)} %slice.56), channel_id=1, source_target_pairs={{0,8},{8,16},{16,24},{24,0},{1,9},{9,17},{17,25},{25,1},{2,10},{10... | collective-permute-start | bytes 786440 | tf_op jit(solution)/shard_map/ppermute | solution.py:32
  244.9 31.9 %collective-permute-start.35 = (bf16[2,512,128]{2,1,0:T(8,128)(2,1)}, bf16[2,512,128]{2,1,0:T(8,128)(2,1)}, u32[]{:S(2)}, u32[]{:S(2)}) collective-permute-start(bf16[2,512,128]{2,1,0:T(8,128)(2,1)} %slice.57), channel_id=1, source_target_pairs={{0,24},{8,0},{16,8},{24,16},{1,25},{9,1},{17,9},{25,17},{2,26},{10... | collective-permute-start | bytes 786440 | tf_op jit(solution)/shard_map/ppermute | solution.py:32
  (17 other events, 255.5 us)

commit v4 on v3

--- a/solution.py
+++ b/solution.py
@@ -51,12 +51,16 @@
     return [v, one, *forward(one, three, axis), three]
 
 
+def gather_first(v):
+    other = shifted(v, "y", 1)
+    a = jnp.stack(ring(v, "x"))
+    b = jnp.stack(ring(other, "z"))
+    return a, b
+
+
 def gather_rows(v, second):
-    both = jnp.stack([v, shifted(v, "y", 1)])
-    half = both.shape[-1] // 2
-    a = jnp.stack(ring(both[..., :half], "x"))
-    b = jnp.stack(ring(both[..., half:], "z"))
-    return second(a, "z"), second(b, "x")
+    a, b = gather_first(v)
+    return second(a, "z") + second(b, "x")
 
 
 def blocks(pieces):
@@ -76,44 +80,24 @@
 def fill_table(pos, table):
     for later in range(4):
         for early in range(4):
-            for slot_y in range(2):
-                at = (later * 4 + early) * 2 + slot_y
-                table[at] = place(pos, early, later, slot_y) * ROWS
-                table[32 + at] = place(pos, later, early, slot_y) * ROWS
-
-
-def spread(table, base, pieces, out):
-    for later, first, piece in blocks(pieces):
-        for early in range(piece.shape[0]):
-            for slot_y in range(2):
-                slot = (later * 4 + first + early) * 2 + slot_y
-                at = pl.multiple_of(table[base + slot], ROWS)
-                out[pl.ds(at, ROWS), :] = piece[early, slot_y]
-
-
-def spread_head(table, head, pieces, out):
+            table[later * 4 + early] = place(pos, early, later, 0) * ROWS
+            table[16 + later * 4 + early] = place(pos, later, early, 1) * ROWS
+
+
+def spread(table, pieces, out):
     half = len(pieces) // 2
-
-    @pl.when(head < H // 2)
-    def _():
-        spread(table, 0, pieces[:half], out)
-
-    @pl.when(head >= H // 2)
-    def _():
-        spread(table, 32, pieces[half:], out)
+    for base, some in ((0, pieces[:half]), (16, pieces[half:])):
+        for later, first, piece in blocks(some):
+            for early in range(piece.shape[0]):
+                at = pl.multiple_of(table[base + later * 4 + first + early], ROWS)
+                out[pl.ds(at, ROWS), :] = piece[early]
 
 
 def piece_specs(pieces, block_of, heads):
-    last = H // 2 // heads
-    specs = []
-    for i, piece in enumerate(pieces):
-        shape = (piece.shape[0], 2, ROWS, heads * DH)
-        if i < len(pieces) // 2:
-            column = lambda *g: jnp.minimum(block_of(*g), last - 1)
-        else:
-            column = lambda *g: jnp.maximum(block_of(*g) - last, 0)
-        specs.append(pl.BlockSpec(shape, lambda *g, column=column: (0, 0, 0, column(*g))))
-    return specs
+    return [
+        pl.BlockSpec((piece.shape[0], ROWS, heads * DH), lambda *g: (0, 0, block_of(*g)))
+        for piece in pieces
+    ]
 
 
 def nt(a, b):
@@ -128,7 +112,7 @@
     def _():
         fill_table(pos, table)
 
-    spread_head(table, g * GROUP, pieces, land)
+    spread(table, pieces, land)
 
     def scores_of(j):
         return nt(keys[:, j * DH : (j + 1) * DH], land[:, j * DH : (j + 1) * DH])
@@ -177,7 +161,7 @@
     def _():
         fill_table(pos, table)
 
-    spread_head(table, g * GROUP, pieces, land)
+    spread(table, pieces, land)
     for j in range(GROUP):
         cols = slice(j * DH, (j + 1) * DH)
         for t in range(0, queries.shape[0], TALL):
@@ -191,9 +175,8 @@
 def inverse_kernel(n_q, pos, *rest):
     pieces, (out, land_q, land_k, table) = rest[:-4], rest[-4:]
     fill_table(pos, table)
-    head = place(pos, 0, 0, 0)
-    spread_head(table, head, pieces[:n_q], land_q)
-    spread_head(table, head, pieces[n_q:], land_k)
+    spread(table, pieces[:n_q], land_q)
+    spread(table, pieces[n_q:], land_k)
     scores = nt(land_q[...], land_k[...])
     top = jnp.max(scores, 1, keepdims=True)
     expo = jnp.exp2((scores - top) * C2)
@@ -254,8 +237,9 @@
     heads = []
     for shift in shifts:
         x, z = (pos[0] + 4 - shift) % 4, (pos[1] + 4 - shift) % 4
-        heads += [(((pos[0] + 4 - early) % 4) * 4 + z) * 2 for early in range(4)]
-        heads += [(x * 4 + (pos[1] + 4 - early) % 4) * 2 + 1 for early in range(4)]
+        y = pos[2]
+        heads += [(((pos[0] + 4 - early) % 4) * 4 + z) * 2 + y for early in range(4)]
+        heads += [(x * 4 + (pos[1] + 4 - early) % 4) * 2 + 1 - y for early in range(4)]
     pieces = [
         pltpu.make_async_copy(
             piece, prods.at[later, pl.ds(early, piece.shape[0])], sems_prod.at[i]
@@ -294,7 +278,7 @@
 
 
 def final(shifts, pos, weights, pieces, *out):
-    anywhere = pl.BlockSpec(memory_space=pl.ANY)
+    anywhere = pl.BlockSpec(memory_space=pltpu.HBM)
     here = weights.shape[1]
     n = LAST * len(shifts)
     return pl.pallas_call(
@@ -340,9 +324,8 @@
     pos = jnp.stack([lax.axis_index(a) for a in SEQ]).astype(jnp.int32)
     here = queries.shape[0]
     per_device = M // 32
-    q_a, q_b = gather_rows(landmarks(queries, per_device), relayed_ring)
-    k_a, k_b = gather_rows(landmarks(keys, per_device), ring)
-    land_q, land_k = q_a + q_b, k_a + k_b
+    land_q = gather_rows(landmarks(queries, per_device), relayed_ring)
+    land_k = gather_rows(landmarks(keys, per_device), ring)
 
     column = pl.BlockSpec((here, GROUP * DH), lambda h, pos: (0, h))
 
@@ -350,7 +333,7 @@
         return piece_specs(pieces, lambda h, pos: h, GROUP)
 
     land = pltpu.VMEM((M, GROUP * DH), BF16)
-    table = pltpu.SMEM((64,), jnp.int32)
+    table = pltpu.SMEM((32,), jnp.int32)
     parts = call(
         parts_kernel,
         (H // GROUP,),
@@ -397,12 +380,7 @@
         prefetch=0,
     )(parts, parts, inverse)
 
-    other = shifted(product, "y", 1)
-    lower = pos[2] == 0
-    a = jnp.where(lower, product, other)
-    b = jnp.where(lower, other, product)
-    a = jnp.stack(ring(a, "x"))
-    b = jnp.stack(ring(b, "z"))
+    a, b = gather_first(product)
     out = final((0,), pos, weights, [a, b])
     a_one, a_three = near_ring(a, "z")
     b_one, b_three = near_ring(b, "x")

time: 284 us -> 258 us (0.908)
  waiting for transfers between devices: 112 us -> 83.1 us
  starting transfers between devices: 83.1 us -> 87.6 us
    ppermute x43, waiting for transfers between devices: 112 us -> 83.1 us  [shifted(): return lax.ppermute(v, axis, [(i, (i + by) % n) for i in range(n)])]
    ppermute x43, starting transfers between devices: 76.2 us -> 82.3 us  [shifted(): return lax.ppermute(v, axis, [(i, (i + by) % n) for i in range(n)])]
  transfers between devices with their start and end apart: 44 -> 44, of which waited for: 21 -> 15; matrix products, arithmetic and copies ran while one was open for 4% -> 4% of each run, Pallas kernels for 15% -> 17%
where the time goes in v4:
time: 258 us
  starting transfers between devices  87.6 us (34%)
  waiting for transfers between devices  83.1 us (32%)
  Pallas kernels  70.1 us (27%)
  other arithmetic  8.63 us (3%)
  local copies, waits for them, and re-layouts  7.75 us (3%)
    ppermute x43, waiting for transfers between devices, shifted(): return lax.ppermute(v, axis, [(i, (i + by) % n) for i in range(n)])  83.1 us
    ppermute x43, starting transfers between devices, shifted(): return lax.ppermute(v, axis, [(i, (i + by) % n) for i in range(n)])  82.3 us
    pallas_call x3, Pallas kernels, final(): pl.pallas_call(functools.partial(final_kernel, shifts, len(pieces)), in_s...  19.2 us
    pallas_call x1, Pallas kernels, steps(): call(parts_kernel, (H // GROUP,), [column, column] + per_head(land_q), pl...  16.7 us
    pallas_call x1, Pallas kernels, steps(): call(near_kernel, (H // GROUP,), [column] + per_head(land_k), pl.BlockSpe...  15.9 us
    pallas_call x1, Pallas kernels, steps(): call(functools.partial(inverse_kernel, len(land_q)), (1,), owned(land_q)...  13.5 us
    reduce_sum x2, other arithmetic, landmarks(): sums = jnp.sum(tokens.reshape(per_device, segment, D), axis=1, dtype=F32)  6.61 us
    slice x8, local copies, waits for them, and re-layouts, forward(): return (shifted(one[:half], axis, 1), shifted(three[half:], axis, 3))  6.18 us
  transfers between devices with their start and end apart: 44, of which 15 were waited for; matrix products, arithmetic and copies ran while one was open for 4% of the time, Pallas kernels for 17%

profile of v4, /device:TPU:0, one launch (start us, length us, event | category | flops | bytes accessed | tf_op | source)
XLA Modules:
  0.0 257.7 jit_solution(15473493823809987768)
XLA Ops:
  0.0 3.3 %convert_reduce_fusion = f32[16,4096]{1,0:T(8,128)S(1)} fusion(bf16[512,4096]{1,0:T(8,128)(2,1)} %queries.1), kind=kLoop, calls=%fused_computation | loop fusion | flops 4128768 | bytes 4456448 | tf_op jit(solution)/shard_map/reduce_sum | solution.py:319
  3.3 1.8 collective-permute-start.20
  5.1 1.5 collective-permute-start.13
  6.6 2.7 %collective-permute-start.14 = (bf16[16,4096]{1,0:T(8,128)(2,1)S(1)}, bf16[16,4096]{1,0:T(8,128)(2,1)S(1)}, u32[]{:S(2)}, u32[]{:S(2)}) collective-permute-start(bf16[16,4096]{1,0:T(8,128)(2,1)S(1)} %multiply_convert_fusion), channel_id=1, source_target_pairs={{0,64},{32,96},{64,0},{96,32},{1,65},{33,97},{65,1},{97,33},{2,66}... | collective-permute-start | bytes 393224 | tf_op jit(solution)/shard_map/ppermute | solution.py:32
  9.3 1.4 collective-permute-start.15
  10.8 2.0 collective-permute-start.21
  12.8 3.6 %collective-permute-start.22 = (bf16[16,4096]{1,0:T(8,128)(2,1)S(1)}, bf16[16,4096]{1,0:T(8,128)(2,1)S(1)}, u32[]{:S(2)}, u32[]{:S(2)}) collective-permute-start(bf16[16,4096]{1,0:T(8,128)(2,1)S(1)} %collective-permute-done.20), channel_id=1, source_target_pairs={{0,16},{8,24},{16,0},{24,8},{1,17},{9,25},{17,1},{25,9},{2,18},{10... | collective-permute-start | bytes 393224 | tf_op jit(solution)/shard_map/ppermute | solution.py:32
  18.6 2.2 collective-permute-start.18
  20.8 1.7 collective-permute-done.22
  23.7 2.6 %collective-permute-start.26 = (bf16[4,16,4096]{2,1,0:T(8,128)(2,1)S(1)}, bf16[4,16,4096]{2,1,0:T(8,128)(2,1)S(1)}, u32[]{:S(2)}, u32[]{:S(2)}) collective-permute-start(bf16[4,16,4096]{2,1,0:T(8,128)(2,1)S(1)} %pad_maximum_fusion.3.rest_5_), channel_id=1, source_target_pairs={{0,96},{32,0},{64,32},{96,64},{1,97},{33,1},{65,33},{97,65},{2,98}... | collective-permute-start | bytes 1572872 | tf_op jit(solution)/shard_map/ppermute | solution.py:32
  26.4 5.5 %collective-permute-done.16.rest_1_ = bf16[4,16,4096]{2,1,0:T(8,128)(2,1)S(1)} collective-permute-done((bf16[4,16,4096]{2,1,0:T(8,128)(2,1)S(1)}, bf16[4,16,4096]{2,1,0:T(8,128)(2,1)S(1)}, u32[]{:S(2)}, u32[]{:S(2)}) %collective-permute-start.16) | collective-permute-done | bytes 524320 | tf_op jit(solution)/shard_map/ppermute | solution.py:32
  33.4 3.2 %collective-permute-start.19 = (bf16[2,16,4096]{2,1,0:T(8,128)(2,1)}, bf16[2,16,4096]{2,1,0:T(8,128)(2,1)}, u32[]{:S(2)}, u32[]{:S(2)}) collective-permute-start(bf16[2,16,4096]{2,1,0:T(8,128)(2,1)} %slice.33), channel_id=1, source_target_pairs={{0,24},{8,0},{16,8},{24,16},{1,25},{9,1},{17,9},{25,17},{2,26},{10... | collective-permute-start | bytes 786440 | tf_op jit(solution)/shard_map/ppermute | solution.py:32
  39.4 2.0 collective-permute-start.27
  42.1 3.2 %collective-permute-done.25.rest_7_ = bf16[2,16,4096]{2,1,0:T(8,128)(2,1)} collective-permute-done((bf16[2,16,4096]{2,1,0:T(8,128)(2,1)}, bf16[2,16,4096]{2,1,0:T(8,128)(2,1)}, u32[]{:S(2)}, u32[]{:S(2)}) %collective-permute-start.25) | collective-permute-done | bytes 262176 | tf_op jit(solution)/shard_map/ppermute | solution.py:32
  46.2 16.7 %shard_map.38 = bf16[32,528,128]{2,1,0:T(8,128)(2,1)} custom-call(s32[3]{0:T(128)} %pad_add_fusion.pos, bf16[512,4096]{1,0:T(8,128)(2,1)} %keys.1, bf16[512,4096]{1,0:T(8,128)(2,1)} %values.1, bf16[4,16,4096]{2,1,0:T(8,128)(2,1)} %copy-done, bf16[4,16,4096]{2,1,0:T(8,128)(2,1)} %copy-done.4, bf16[2,16,4096]{2,1,0:T(8,128)(2,1)} %copy-done.19, ...), custom_call_target="tpu_custom_call" | custom-call | tf_op jit(solution)/shard_map/pallas_call | solution.py:337
  63.0 5.2 %all-to-all-start = ((bf16[32,528,128]{2,1,0:T(8,128)(2,1)}), bf16[32,528,128]{2,1,0:T(8,128)(2,1)}, u32[]{:S(2)}, u32[]{:S(2)}) async-start(bf16[32,528,128]{2,1,0:T(8,128)(2,1)} %shard_map.38), calls=%async_computation | async-start | bytes 8650752 | tf_op jit(solution)/shard_map/all_to_all | solution.py:345
  68.2 3.3 %convert_reduce_fusion.1 = f32[16,4096]{1,0:T(8,128)S(1)} fusion(bf16[512,4096]{1,0:T(8,128)(2,1)} %keys.1), kind=kLoop, calls=%fused_computation.1 | loop fusion | flops 4128768 | bytes 4456448 | tf_op jit(solution)/shard_map/reduce_sum | solution.py:319
  71.5 1.8 collective-permute-start.6
  73.3 1.5 collective-permute-start
  74.8 2.7 %collective-permute-start.1 = (bf16[16,4096]{1,0:T(8,128)(2,1)S(1)}, bf16[16,4096]{1,0:T(8,128)(2,1)S(1)}, u32[]{:S(2)}, u32[]{:S(2)}) collective-permute-start(bf16[16,4096]{1,0:T(8,128)(2,1)S(1)} %multiply_convert_fusion.1), channel_id=1, source_target_pairs={{0,64},{32,96},{64,0},{96,32},{1,65},{33,97},{65,1},{97,33},{2,66}... | collective-permute-start | bytes 393224 | tf_op jit(solution)/shard_map/ppermute | solution.py:32
  77.5 1.4 collective-permute-start.2
  79.0 39.7 %collective-permute-done.6 = bf16[16,4096]{1,0:T(8,128)(2,1)S(1)} collective-permute-done((bf16[16,4096]{1,0:T(8,128)(2,1)S(1)}, bf16[16,4096]{1,0:T(8,128)(2,1)S(1)}, u32[]{:S(2)}, u32[]{:S(2)}) %collective-permute-start.6) | collective-permute-done | bytes 131104 | tf_op jit(solution)/shard_map/ppermute | solution.py:32
  118.7 3.0 %collective-permute-start.8 = (bf16[16,4096]{1,0:T(8,128)(2,1)S(1)}, bf16[16,4096]{1,0:T(8,128)(2,1)S(1)}, u32[]{:S(2)}, u32[]{:S(2)}) collective-permute-start(bf16[16,4096]{1,0:T(8,128)(2,1)S(1)} %collective-permute-done.6), channel_id=1, source_target_pairs={{0,16},{8,24},{16,0},{24,8},{1,17},{9,25},{17,1},{25,9},{2,18},{10... | collective-permute-start | bytes 393224 | tf_op jit(solution)/shard_map/ppermute | solution.py:32
  121.7 5.0 %collective-permute-start.9 = (bf16[16,4096]{1,0:T(8,128)(2,1)S(1)}, bf16[16,4096]{1,0:T(8,128)(2,1)S(1)}, u32[]{:S(2)}, u32[]{:S(2)}) collective-permute-start(bf16[16,4096]{1,0:T(8,128)(2,1)S(1)} %collective-permute-done.6), channel_id=1, source_target_pairs={{0,24},{8,0},{16,8},{24,16},{1,25},{9,1},{17,9},{25,17},{2,26},{10... | collective-permute-start | bytes 393224 | tf_op jit(solution)/shard_map/ppermute | solution.py:32
  126.7 1.6 collective-permute-done.1
  129.4 2.1 collective-permute-start.4
  132.2 4.4 %collective-permute-done.9 = bf16[16,4096]{1,0:T(8,128)(2,1)S(1)} collective-permute-done((bf16[16,4096]{1,0:T(8,128)(2,1)S(1)}, bf16[16,4096]{1,0:T(8,128)(2,1)S(1)}, u32[]{:S(2)}, u32[]{:S(2)}) %collective-permute-start.9) | collective-permute-done | bytes 131104 | tf_op jit(solution)/shard_map/ppermute | solution.py:32
  136.6 4.9 %collective-permute-start.10 = (bf16[4,16,4096]{2,1,0:T(8,128)(2,1)S(1)}, bf16[4,16,4096]{2,1,0:T(8,128)(2,1)S(1)}, u32[]{:S(2)}, u32[]{:S(2)}) collective-permute-start(bf16[4,16,4096]{2,1,0:T(8,128)(2,1)S(1)} %pad_maximum_fusion.1.rest_4_.rest_14_), channel_id=1, source_target_pairs={{0,32},{32,64},{64,96},{96,0},{1,33},{33,65},{65,97},{97,1},{2,34}... | collective-permute-start | bytes 1572872 | tf_op jit(solution)/shard_map/ppermute | solution.py:32
  141.6 1.5 collective-permute-start.11
  143.1 10.1 %collective-permute-done.3.rest_1_.rest_11_ = bf16[4,16,4096]{2,1,0:T(8,128)(2,1)S(1)} collective-permute-done((bf16[4,16,4096]{2,1,0:T(8,128)(2,1)S(1)}, bf16[4,16,4096]{2,1,0:T(8,128)(2,1)S(1)}, u32[]{:S(2)}, u32[]{:S(2)}) %collective-permute-start.3) | collective-permute-done | bytes 524320 | tf_op jit(solution)/shard_map/ppermute | solution.py:32
  153.1 6.1 %collective-permute-start.12 = (bf16[4,16,4096]{2,1,0:T(8,128)(2,1)S(1)}, bf16[4,16,4096]{2,1,0:T(8,128)(2,1)}, u32[]{:S(2)}, u32[]{:S(2)}) collective-permute-start(bf16[4,16,4096]{2,1,0:T(8,128)(2,1)S(1)} %pad_maximum_fusion.1.rest_4_.rest_14_), channel_id=1, source_target_pairs={{0,96},{32,0},{64,32},{96,64},{1,97},{33,1},{65,33},{97,65},{2,98}... | collective-permute-start | bytes 1572872 | tf_op jit(solution)/shard_map/ppermute | solution.py:32
  161.1 4.8 %collective-permute-done.12.rest_7_.rest_17_ = bf16[4,16,4096]{2,1,0:T(8,128)(2,1)} collective-permute-done((bf16[4,16,4096]{2,1,0:T(8,128)(2,1)S(1)}, bf16[4,16,4096]{2,1,0:T(8,128)(2,1)}, u32[]{:S(2)}, u32[]{:S(2)}) %collective-permute-start.12) | collective-permute-done | bytes 524320 | tf_op jit(solution)/shard_map/ppermute | solution.py:32
  166.0 13.5 %shard_map.39.inverse = bf16[512,512]{1,0:T(8,128)(2,1)} custom-call(s32[3]{0:T(128)} %pad_add_fusion.pos, bf16[4,16,4096]{2,1,0:T(8,128)(2,1)} %copy-done, bf16[4,16,4096]{2,1,0:T(8,128)(2,1)} %copy-done.4, bf16[2,16,4096]{2,1,0:T(8,128)(2,1)} %copy-done.19, bf16[2,16,4096]{2,1,0:T(8,128)(2,1)} %collective-permute-done.19.rest_3_, ...), custom_call_target="tpu_custom_call" | custom-call | tf_op jit(solution)/shard_map/pallas_call | solution.py:360
  179.5 4.8 %shard_map.40 = bf16[512,128]{1,0:T(8,128)(2,1)} custom-call(bf16[32,528,128]{2,1,0:T(8,128)(2,1)} %all-to-all-done.parts.levels, bf16[32,528,128]{2,1,0:T(8,128)(2,1)} %all-to-all-done.parts.levels, bf16[512,512]{1,0:T(8,128)(2,1)} %shard_map.39.inverse), custom_call_target="tpu_custom_call" | custom-call | tf_op jit(solution)/shard_map/pallas_call | solution.py:369
  184.2 2.5 collective-permute-start.35
  186.8 5.3 %collective-permute-start.29 = (bf16[512,128]{1,0:T(8,128)(2,1)}, bf16[512,128]{1,0:T(8,128)(2,1)S(1)}, u32[]{:S(2)}, u32[]{:S(2)}) collective-permute-start(bf16[512,128]{1,0:T(8,128)(2,1)} %shard_map.40), channel_id=1, source_target_pairs={{0,64},{32,96},{64,0},{96,32},{1,65},{33,97},{65,1},{97,33},{2,66}... | collective-permute-start | bytes 393224 | tf_op jit(solution)/shard_map/ppermute | solution.py:32
  193.8 1.5 collective-permute-start.38
  195.3 1.9 collective-permute-done.29
  198.8 3.2 %collective-permute-start.33 = (bf16[4,512,128]{2,1,0:T(8,128)(2,1)S(1)}, bf16[4,512,128]{2,1,0:T(8,128)(2,1)S(1)}, u32[]{:S(2)}, u32[]{:S(2)}) collective-permute-start(bf16[4,512,128]{2,1,0:T(8,128)(2,1)S(1)} %pad_maximum_fusion.4.rest_0_), channel_id=1, source_target_pairs={{0,24},{8,0},{16,8},{24,16},{1,25},{9,1},{17,9},{25,17},{2,26},{10... | collective-permute-start | bytes 1572872 | tf_op jit(solution)/shard_map/ppermute | solution.py:32
  202.1 1.6 collective-permute-start.39
  203.8 1.7 collective-permute-start.41
  205.4 6.6 %collective-permute-done.31.rest_0_ = bf16[4,512,128]{2,1,0:T(8,128)(2,1)S(1)} collective-permute-done((bf16[4,512,128]{2,1,0:T(8,128)(2,1)S(1)}, bf16[4,512,128]{2,1,0:T(8,128)(2,1)S(1)}, u32[]{:S(2)}, u32[]{:S(2)}) %collective-permute-start.31) | collective-permute-done | bytes 524320 | tf_op jit(solution)/shard_map/ppermute | solution.py:32
  213.6 3.2 %collective-permute-start.34 = (bf16[2,512,128]{2,1,0:T(8,128)(2,1)}, bf16[2,512,128]{2,1,0:T(8,128)(2,1)}, u32[]{:S(2)}, u32[]{:S(2)}) collective-permute-start(bf16[2,512,128]{2,1,0:T(8,128)(2,1)} %slice.37), channel_id=1, source_target_pairs={{0,24},{8,0},{16,8},{24,16},{1,25},{9,1},{17,9},{25,17},{2,26},{10... | collective-permute-start | bytes 786440 | tf_op jit(solution)/shard_map/ppermute | solution.py:32
  218.4 3.2 %collective-permute-start.42 = (bf16[2,512,128]{2,1,0:T(8,128)(2,1)}, bf16[2,512,128]{2,1,0:T(8,128)(2,1)}, u32[]{:S(2)}, u32[]{:S(2)}) collective-permute-start(bf16[2,512,128]{2,1,0:T(8,128)(2,1)} %slice.39), channel_id=1, source_target_pairs={{0,96},{32,0},{64,32},{96,64},{1,97},{33,1},{65,33},{97,65},{2,98}... | collective-permute-start | bytes 786440 | tf_op jit(solution)/shard_map/ppermute | solution.py:32
  221.6 15.9 %shard_map.37.weights = bf16[32,512,512]{2,1,0:T(8,128)(2,1)} custom-call(s32[3]{0:T(128)} %pad_add_fusion.pos, bf16[512,4096]{1,0:T(8,128)(2,1)} %queries.1, bf16[4,16,4096]{2,1,0:T(8,128)(2,1)} %copy-done.2, bf16[4,16,4096]{2,1,0:T(8,128)(2,1)} %copy-done.8, bf16[4,16,4096]{2,1,0:T(8,128)(2,1)} %copy-done.9, bf16[4,16,4096]{2,1,0:T(8,128)(2,1)} %copy-done.10, ...), custom_call_target="tpu_custom_call" | custom-call | tf_op jit(solution)/shard_map/pallas_call | solution.py:347
  237.6 5.4 %shard_map.41.rest_4_ = bf16[512,4096]{1,0:T(8,128)(2,1)} custom-call(s32[3]{0:T(128)} %pad_add_fusion.pos, bf16[32,512,512]{2,1,0:T(8,128)(2,1)} %shard_map.37.weights, bf16[4,512,128]{2,1,0:T(8,128)(2,1)} %copy-done.13, bf16[4,512,128]{2,1,0:T(8,128)(2,1)} %copy-done.14), custom_call_target="tpu_custom_call" | custom-call | tf_op jit(solution)/shard_map/pallas_call | solution.py:284
  242.9 8.5 %shard_map.42.rest_4_ = bf16[512,4096]{1,0:T(8,128)(2,1)} custom-call(s32[3]{0:T(128)} %pad_add_fusion.pos, bf16[32,512,512]{2,1,0:T(8,128)(2,1)} %shard_map.37.weights, bf16[4,512,128]{2,1,0:T(8,128)(2,1)} %copy-done.15, bf16[4,512,128]{2,1,0:T(8,128)(2,1)} %copy-done.17, bf16[4,512,128]{2,1,0:T(8,128)(2,1)} %copy-done.16, ...), custom_call_target="tpu_custom_call", output_to_operand_aliasing={{}: (6, {})} | custom-call | tf_op jit(solution)/shard_map/pallas_call | solution.py:284
  252.2 5.4 %shard_map.43 = bf16[512,4096]{1,0:T(8,128)(2,1)} custom-call(s32[3]{0:T(128)} %pad_add_fusion.pos, bf16[32,512,512]{2,1,0:T(8,128)(2,1)} %shard_map.37.weights, bf16[2,512,128]{2,1,0:T(8,128)(2,1)} %copy-done.20, bf16[2,512,128]{2,1,0:T(8,128)(2,1)} %collective-permute-done.34.rest_1_, ...), custom_call_target="tpu_custom_call", output_to_operand_aliasing={{}: (6, {})} | custom-call | tf_op jit(solution)/shard_map/pallas_call | solution.py:284
  (110 shorter events, 20.3 us)
Async XLA Ops:
  3.3 7.4 %collective-permute-start.20 = (bf16[16,4096]{1,0:T(8,128)(2,1)S(1)}, bf16[16,4096]{1,0:T(8,128)(2,1)S(1)}, u32[]{:S(2)}, u32[]{:S(2)}) collective-permute-start(bf16[16,4096]{1,0:T(8,128)(2,1)S(1)} %multiply_convert_fusion), channel_id=1, source_target_pairs={{0,4},{4,0},{1,5},{5,1},{2,6},{6,2},{3,7},{7,3},{8,12},{12,8},{9,1... | collective-permute-start | bytes 393224 | tf_op jit(solution)/shard_map/ppermute | solution.py:32
  5.1 11.3 %collective-permute-start.13 = (bf16[16,4096]{1,0:T(8,128)(2,1)S(1)}, bf16[16,4096]{1,0:T(8,128)(2,1)S(1)}, u32[]{:S(2)}, u32[]{:S(2)}) collective-permute-start(bf16[16,4096]{1,0:T(8,128)(2,1)S(1)} %multiply_convert_fusion), channel_id=1, source_target_pairs={{0,32},{32,64},{64,96},{96,0},{1,33},{33,65},{65,97},{97,1},{2,34}... | collective-permute-start | bytes 393224 | tf_op jit(solution)/shard_map/ppermute | solution.py:32
  6.6 10.8 %collective-permute-start.14 = (bf16[16,4096]{1,0:T(8,128)(2,1)S(1)}, bf16[16,4096]{1,0:T(8,128)(2,1)S(1)}, u32[]{:S(2)}, u32[]{:S(2)}) collective-permute-start(bf16[16,4096]{1,0:T(8,128)(2,1)S(1)} %multiply_convert_fusion), channel_id=1, source_target_pairs={{0,64},{32,96},{64,0},{96,32},{1,65},{33,97},{65,1},{97,33},{2,66}... | collective-permute-start | bytes 393224 | tf_op jit(solution)/shard_map/ppermute | solution.py:32
  9.3 8.1 %collective-permute-start.15 = (bf16[16,4096]{1,0:T(8,128)(2,1)S(1)}, bf16[16,4096]{1,0:T(8,128)(2,1)S(1)}, u32[]{:S(2)}, u32[]{:S(2)}) collective-permute-start(bf16[16,4096]{1,0:T(8,128)(2,1)S(1)} %multiply_convert_fusion), channel_id=1, source_target_pairs={{0,96},{32,0},{64,32},{96,64},{1,97},{33,1},{65,33},{97,65},{2,98}... | collective-permute-start | bytes 393224 | tf_op jit(solution)/shard_map/ppermute | solution.py:32
  10.8 10.0 %collective-permute-start.21 = (bf16[16,4096]{1,0:T(8,128)(2,1)S(1)}, bf16[16,4096]{1,0:T(8,128)(2,1)S(1)}, u32[]{:S(2)}, u32[]{:S(2)}) collective-permute-start(bf16[16,4096]{1,0:T(8,128)(2,1)S(1)} %collective-permute-done.20), channel_id=1, source_target_pairs={{0,8},{8,16},{16,24},{24,0},{1,9},{9,17},{17,25},{25,1},{2,10},{10... | collective-permute-start | bytes 393224 | tf_op jit(solution)/shard_map/ppermute | solution.py:32
  12.8 9.7 %collective-permute-start.22 = (bf16[16,4096]{1,0:T(8,128)(2,1)S(1)}, bf16[16,4096]{1,0:T(8,128)(2,1)S(1)}, u32[]{:S(2)}, u32[]{:S(2)}) collective-permute-start(bf16[16,4096]{1,0:T(8,128)(2,1)S(1)} %collective-permute-done.20), channel_id=1, source_target_pairs={{0,16},{8,24},{16,0},{24,8},{1,17},{9,25},{17,1},{25,9},{2,18},{10... | collective-permute-start | bytes 393224 | tf_op jit(solution)/shard_map/ppermute | solution.py:32
  16.4 6.6 %collective-permute-start.23 = (bf16[16,4096]{1,0:T(8,128)(2,1)S(1)}, bf16[16,4096]{1,0:T(8,128)(2,1)S(1)}, u32[]{:S(2)}, u32[]{:S(2)}) collective-permute-start(bf16[16,4096]{1,0:T(8,128)(2,1)S(1)} %collective-permute-done.20), channel_id=1, source_target_pairs={{0,24},{8,0},{16,8},{24,16},{1,25},{9,1},{17,9},{25,17},{2,26},{10... | collective-permute-start | bytes 393224 | tf_op jit(solution)/shard_map/ppermute | solution.py:32
  17.5 14.4 %collective-permute-start.16 = (bf16[4,16,4096]{2,1,0:T(8,128)(2,1)S(1)}, bf16[4,16,4096]{2,1,0:T(8,128)(2,1)S(1)}, u32[]{:S(2)}, u32[]{:S(2)}) collective-permute-start(bf16[4,16,4096]{2,1,0:T(8,128)(2,1)S(1)} %pad_maximum_fusion.2.rest_0_), channel_id=1, source_target_pairs={{0,8},{8,16},{16,24},{24,0},{1,9},{9,17},{17,25},{25,1},{2,10},{10... | collective-permute-start | bytes 1572872 | tf_op jit(solution)/shard_map/ppermute | solution.py:32
  18.6 14.1 %collective-permute-start.18 = (bf16[4,16,4096]{2,1,0:T(8,128)(2,1)S(1)}, bf16[4,16,4096]{2,1,0:T(8,128)(2,1)S(1)}, u32[]{:S(2)}, u32[]{:S(2)}) collective-permute-start(bf16[4,16,4096]{2,1,0:T(8,128)(2,1)S(1)} %pad_maximum_fusion.2.rest_0_), channel_id=1, source_target_pairs={{0,24},{8,0},{16,8},{24,16},{1,25},{9,1},{17,9},{25,17},{2,26},{10... | collective-permute-start | bytes 1572872 | tf_op jit(solution)/shard_map/ppermute | solution.py:32
  23.1 13.6 %collective-permute-start.24 = (bf16[4,16,4096]{2,1,0:T(8,128)(2,1)S(1)}, bf16[4,16,4096]{2,1,0:T(8,128)(2,1)S(1)}, u32[]{:S(2)}, u32[]{:S(2)}) collective-permute-start(bf16[4,16,4096]{2,1,0:T(8,128)(2,1)S(1)} %pad_maximum_fusion.3.rest_5_), channel_id=1, source_target_pairs={{0,32},{32,64},{64,96},{96,0},{1,33},{33,65},{65,97},{97,1},{2,34}... | collective-permute-start | bytes 1572872 | tf_op jit(solution)/shard_map/ppermute | solution.py:32
  23.7 14.9 %collective-permute-start.26 = (bf16[4,16,4096]{2,1,0:T(8,128)(2,1)S(1)}, bf16[4,16,4096]{2,1,0:T(8,128)(2,1)S(1)}, u32[]{:S(2)}, u32[]{:S(2)}) collective-permute-start(bf16[4,16,4096]{2,1,0:T(8,128)(2,1)S(1)} %pad_maximum_fusion.3.rest_5_), channel_id=1, source_target_pairs={{0,96},{32,0},{64,32},{96,64},{1,97},{33,1},{65,33},{97,65},{2,98}... | collective-permute-start | bytes 1572872 | tf_op jit(solution)/shard_map/ppermute | solution.py:32
  32.6 9.4 %collective-permute-start.17 = (bf16[2,16,4096]{2,1,0:T(8,128)(2,1)}, bf16[2,16,4096]{2,1,0:T(8,128)(2,1)S(1)}, u32[]{:S(2)}, u32[]{:S(2)}) collective-permute-start(bf16[2,16,4096]{2,1,0:T(8,128)(2,1)} %slice.32), channel_id=1, source_target_pairs={{0,8},{8,16},{16,24},{24,0},{1,9},{9,17},{17,25},{25,1},{2,10},{10... | collective-permute-start | bytes 786440 | tf_op jit(solution)/shard_map/ppermute | solution.py:32
  33.4 8.7 %collective-permute-start.19 = (bf16[2,16,4096]{2,1,0:T(8,128)(2,1)}, bf16[2,16,4096]{2,1,0:T(8,128)(2,1)}, u32[]{:S(2)}, u32[]{:S(2)}) collective-permute-start(bf16[2,16,4096]{2,1,0:T(8,128)(2,1)} %slice.33), channel_id=1, source_target_pairs={{0,24},{8,0},{16,8},{24,16},{1,25},{9,1},{17,9},{25,17},{2,26},{10... | collective-permute-start | bytes 786440 | tf_op jit(solution)/shard_map/ppermute | solution.py:32
  37.4 7.9 %collective-permute-start.25 = (bf16[2,16,4096]{2,1,0:T(8,128)(2,1)}, bf16[2,16,4096]{2,1,0:T(8,128)(2,1)}, u32[]{:S(2)}, u32[]{:S(2)}) collective-permute-start(bf16[2,16,4096]{2,1,0:T(8,128)(2,1)} %slice.34), channel_id=1, source_target_pairs={{0,32},{32,64},{64,96},{96,0},{1,33},{33,65},{65,97},{97,1},{2,34}... | collective-permute-start | bytes 786440 | tf_op jit(solution)/shard_map/ppermute | solution.py:32
  39.4 6.8 %collective-permute-start.27 = (bf16[2,16,4096]{2,1,0:T(8,128)(2,1)}, bf16[2,16,4096]{2,1,0:T(8,128)(2,1)}, u32[]{:S(2)}, u32[]{:S(2)}) collective-permute-start(bf16[2,16,4096]{2,1,0:T(8,128)(2,1)} %slice.35), channel_id=1, source_target_pairs={{0,96},{32,0},{64,32},{96,64},{1,97},{33,1},{65,33},{97,65},{2,98}... | collective-permute-start | bytes 786440 | tf_op jit(solution)/shard_map/ppermute | solution.py:32
  63.0 116.5 %all-to-all-start = ((bf16[32,528,128]{2,1,0:T(8,128)(2,1)}), bf16[32,528,128]{2,1,0:T(8,128)(2,1)}, u32[]{:S(2)}, u32[]{:S(2)}) async-start(bf16[32,528,128]{2,1,0:T(8,128)(2,1)} %shard_map.38), calls=%async_computation | async-start | bytes 8650752 | tf_op jit(solution)/shard_map/all_to_all | solution.py:345
  71.5 47.1 %collective-permute-start.6 = (bf16[16,4096]{1,0:T(8,128)(2,1)S(1)}, bf16[16,4096]{1,0:T(8,128)(2,1)S(1)}, u32[]{:S(2)}, u32[]{:S(2)}) collective-permute-start(bf16[16,4096]{1,0:T(8,128)(2,1)S(1)} %multiply_convert_fusion.1), channel_id=1, source_target_pairs={{0,4},{4,0},{1,5},{5,1},{2,6},{6,2},{3,7},{7,3},{8,12},{12,8},{9,1... | collective-permute-start | bytes 393224 | tf_op jit(solution)/shard_map/ppermute | solution.py:32
  73.3 53.3 %collective-permute-start = (bf16[16,4096]{1,0:T(8,128)(2,1)S(1)}, bf16[16,4096]{1,0:T(8,128)(2,1)S(1)}, u32[]{:S(2)}, u32[]{:S(2)}) collective-permute-start(bf16[16,4096]{1,0:T(8,128)(2,1)S(1)} %multiply_convert_fusion.1), channel_id=1, source_target_pairs={{0,32},{32,64},{64,96},{96,0},{1,33},{33,65},{65,97},{97,1},{2,34}... | collective-permute-start | bytes 393224 | tf_op jit(solution)/shard_map/ppermute | solution.py:32
  74.8 53.4 %collective-permute-start.1 = (bf16[16,4096]{1,0:T(8,128)(2,1)S(1)}, bf16[16,4096]{1,0:T(8,128)(2,1)S(1)}, u32[]{:S(2)}, u32[]{:S(2)}) collective-permute-start(bf16[16,4096]{1,0:T(8,128)(2,1)S(1)} %multiply_convert_fusion.1), channel_id=1, source_target_pairs={{0,64},{32,96},{64,0},{96,32},{1,65},{33,97},{65,1},{97,33},{2,66}... | collective-permute-start | bytes 393224 | tf_op jit(solution)/shard_map/ppermute | solution.py:32
  77.5 50.7 %collective-permute-start.2 = (bf16[16,4096]{1,0:T(8,128)(2,1)S(1)}, bf16[16,4096]{1,0:T(8,128)(2,1)S(1)}, u32[]{:S(2)}, u32[]{:S(2)}) collective-permute-start(bf16[16,4096]{1,0:T(8,128)(2,1)S(1)} %multiply_convert_fusion.1), channel_id=1, source_target_pairs={{0,96},{32,0},{64,32},{96,64},{1,97},{33,1},{65,33},{97,65},{2,98}... | collective-permute-start | bytes 393224 | tf_op jit(solution)/shard_map/ppermute | solution.py:32
  118.7 12.9 %collective-permute-start.8 = (bf16[16,4096]{1,0:T(8,128)(2,1)S(1)}, bf16[16,4096]{1,0:T(8,128)(2,1)S(1)}, u32[]{:S(2)}, u32[]{:S(2)}) collective-permute-start(bf16[16,4096]{1,0:T(8,128)(2,1)S(1)} %collective-permute-done.6), channel_id=1, source_target_pairs={{0,16},{8,24},{16,0},{24,8},{1,17},{9,25},{17,1},{25,9},{2,18},{10... | collective-permute-start | bytes 393224 | tf_op jit(solution)/shard_map/ppermute | solution.py:32
  121.7 14.8 %collective-permute-start.9 = (bf16[16,4096]{1,0:T(8,128)(2,1)S(1)}, bf16[16,4096]{1,0:T(8,128)(2,1)S(1)}, u32[]{:S(2)}, u32[]{:S(2)}) collective-permute-start(bf16[16,4096]{1,0:T(8,128)(2,1)S(1)} %collective-permute-done.6), channel_id=1, source_target_pairs={{0,24},{8,0},{16,8},{24,16},{1,25},{9,1},{17,9},{25,17},{2,26},{10... | collective-permute-start | bytes 393224 | tf_op jit(solution)/shard_map/ppermute | solution.py:32
  126.7 9.9 %collective-permute-start.7 = (bf16[16,4096]{1,0:T(8,128)(2,1)S(1)}, bf16[16,4096]{1,0:T(8,128)(2,1)S(1)}, u32[]{:S(2)}, u32[]{:S(2)}) collective-permute-start(bf16[16,4096]{1,0:T(8,128)(2,1)S(1)} %collective-permute-done.6), channel_id=1, source_target_pairs={{0,8},{8,16},{16,24},{24,0},{1,9},{9,17},{17,25},{25,1},{2,10},{10... | collective-permute-start | bytes 393224 | tf_op jit(solution)/shard_map/ppermute | solution.py:32
  128.3 37.6 %copy-start.2 = (bf16[4,16,4096]{2,1,0:T(8,128)(2,1)}, bf16[4,16,4096]{2,1,0:T(8,128)(2,1)S(1)}, u32[]{:S(2)}) copy-start(bf16[4,16,4096]{2,1,0:T(8,128)(2,1)S(1)} %pad_maximum_fusion.rest_0_.rest_10_) | copy-start | bytes 1572868
  128.3 24.8 %collective-permute-start.3 = (bf16[4,16,4096]{2,1,0:T(8,128)(2,1)S(1)}, bf16[4,16,4096]{2,1,0:T(8,128)(2,1)S(1)}, u32[]{:S(2)}, u32[]{:S(2)}) collective-permute-start(bf16[4,16,4096]{2,1,0:T(8,128)(2,1)S(1)} %pad_maximum_fusion.rest_0_.rest_10_), channel_id=1, source_target_pairs={{0,8},{8,16},{16,24},{24,0},{1,9},{9,17},{17,25},{25,1},{2,10},{10... | collective-permute-start | bytes 1572872 | tf_op jit(solution)/shard_map/ppermute | solution.py:32
  129.4 29.8 %collective-permute-start.4 = (bf16[4,16,4096]{2,1,0:T(8,128)(2,1)S(1)}, bf16[4,16,4096]{2,1,0:T(8,128)(2,1)S(1)}, u32[]{:S(2)}, u32[]{:S(2)}) collective-permute-start(bf16[4,16,4096]{2,1,0:T(8,128)(2,1)S(1)} %pad_maximum_fusion.rest_0_.rest_10_), channel_id=1, source_target_pairs={{0,16},{8,24},{16,0},{24,8},{1,17},{9,25},{17,1},{25,9},{2,18},{10... | collective-permute-start | bytes 1572872 | tf_op jit(solution)/shard_map/ppermute | solution.py:32
  131.5 27.7 %collective-permute-start.5 = (bf16[4,16,4096]{2,1,0:T(8,128)(2,1)S(1)}, bf16[4,16,4096]{2,1,0:T(8,128)(2,1)S(1)}, u32[]{:S(2)}, u32[]{:S(2)}) collective-permute-start(bf16[4,16,4096]{2,1,0:T(8,128)(2,1)S(1)} %pad_maximum_fusion.rest_0_.rest_10_), channel_id=1, source_target_pairs={{0,24},{8,0},{16,8},{24,16},{1,25},{9,1},{17,9},{25,17},{2,26},{10... | collective-permute-start | bytes 1572872 | tf_op jit(solution)/shard_map/ppermute | solution.py:32
  136.6 29.3 %copy-start.3 = (bf16[4,16,4096]{2,1,0:T(8,128)(2,1)}, bf16[4,16,4096]{2,1,0:T(8,128)(2,1)S(1)}, u32[]{:S(2)}) copy-start(bf16[4,16,4096]{2,1,0:T(8,128)(2,1)S(1)} %pad_maximum_fusion.1.rest_4_.rest_14_) | copy-start | bytes 1572868
  136.6 22.6 %collective-permute-start.10 = (bf16[4,16,4096]{2,1,0:T(8,128)(2,1)S(1)}, bf16[4,16,4096]{2,1,0:T(8,128)(2,1)S(1)}, u32[]{:S(2)}, u32[]{:S(2)}) collective-permute-start(bf16[4,16,4096]{2,1,0:T(8,128)(2,1)S(1)} %pad_maximum_fusion.1.rest_4_.rest_14_), channel_id=1, source_target_pairs={{0,32},{32,64},{64,96},{96,0},{1,33},{33,65},{65,97},{97,1},{2,34}... | collective-permute-start | bytes 1572872 | tf_op jit(solution)/shard_map/ppermute | solution.py:32
  141.6 18.8 %collective-permute-start.11 = (bf16[4,16,4096]{2,1,0:T(8,128)(2,1)S(1)}, bf16[4,16,4096]{2,1,0:T(8,128)(2,1)S(1)}, u32[]{:S(2)}, u32[]{:S(2)}) collective-permute-start(bf16[4,16,4096]{2,1,0:T(8,128)(2,1)S(1)} %pad_maximum_fusion.1.rest_4_.rest_14_), channel_id=1, source_target_pairs={{0,64},{32,96},{64,0},{96,32},{1,65},{33,97},{65,1},{97,33},{2,66}... | collective-permute-start | bytes 1572872 | tf_op jit(solution)/shard_map/ppermute | solution.py:32
  153.1 12.8 %collective-permute-start.12 = (bf16[4,16,4096]{2,1,0:T(8,128)(2,1)S(1)}, bf16[4,16,4096]{2,1,0:T(8,128)(2,1)}, u32[]{:S(2)}, u32[]{:S(2)}) collective-permute-start(bf16[4,16,4096]{2,1,0:T(8,128)(2,1)S(1)} %pad_maximum_fusion.1.rest_4_.rest_14_), channel_id=1, source_target_pairs={{0,96},{32,0},{64,32},{96,64},{1,97},{33,1},{65,33},{97,65},{2,98}... | collective-permute-start | bytes 1572872 | tf_op jit(solution)/shard_map/ppermute | solution.py:32
  184.2 7.8 %collective-permute-start.35 = (bf16[512,128]{1,0:T(8,128)(2,1)}, bf16[512,128]{1,0:T(8,128)(2,1)S(1)}, u32[]{:S(2)}, u32[]{:S(2)}) collective-permute-start(bf16[512,128]{1,0:T(8,128)(2,1)} %shard_map.40), channel_id=1, source_target_pairs={{0,4},{4,0},{1,5},{5,1},{2,6},{6,2},{3,7},{7,3},{8,12},{12,8},{9,1... | collective-permute-start | bytes 393224 | tf_op jit(solution)/shard_map/ppermute | solution.py:32
  186.8 7.0 %collective-permute-start.28 = (bf16[512,128]{1,0:T(8,128)(2,1)}, bf16[512,128]{1,0:T(8,128)(2,1)S(1)}, u32[]{:S(2)}, u32[]{:S(2)}) collective-permute-start(bf16[512,128]{1,0:T(8,128)(2,1)} %shard_map.40), channel_id=1, source_target_pairs={{0,32},{32,64},{64,96},{96,0},{1,33},{33,65},{65,97},{97,1},{2,34}... | collective-permute-start | bytes 393224 | tf_op jit(solution)/shard_map/ppermute | solution.py:32
  186.8 10.4 %collective-permute-start.29 = (bf16[512,128]{1,0:T(8,128)(2,1)}, bf16[512,128]{1,0:T(8,128)(2,1)S(1)}, u32[]{:S(2)}, u32[]{:S(2)}) collective-permute-start(bf16[512,128]{1,0:T(8,128)(2,1)} %shard_map.40), channel_id=1, source_target_pairs={{0,64},{32,96},{64,0},{96,32},{1,65},{33,97},{65,1},{97,33},{2,66}... | collective-permute-start | bytes 393224 | tf_op jit(solution)/shard_map/ppermute | solution.py:32
  192.0 5.7 %collective-permute-start.30 = (bf16[512,128]{1,0:T(8,128)(2,1)}, bf16[512,128]{1,0:T(8,128)(2,1)S(1)}, u32[]{:S(2)}, u32[]{:S(2)}) collective-permute-start(bf16[512,128]{1,0:T(8,128)(2,1)} %shard_map.40), channel_id=1, source_target_pairs={{0,96},{32,0},{64,32},{96,64},{1,97},{33,1},{65,33},{97,65},{2,98}... | collective-permute-start | bytes 393224 | tf_op jit(solution)/shard_map/ppermute | solution.py:32
  192.0 10.0 %collective-permute-start.36 = (bf16[512,128]{1,0:T(8,128)(2,1)S(1)}, bf16[512,128]{1,0:T(8,128)(2,1)S(1)}, u32[]{:S(2)}, u32[]{:S(2)}) collective-permute-start(bf16[512,128]{1,0:T(8,128)(2,1)S(1)} %collective-permute-done.35), channel_id=1, source_target_pairs={{0,8},{8,16},{16,24},{24,0},{1,9},{9,17},{17,25},{25,1},{2,10},{10... | collective-permute-start | bytes 393224 | tf_op jit(solution)/shard_map/ppermute | solution.py:32
  192.0 10.0 %collective-permute-start.37 = (bf16[512,128]{1,0:T(8,128)(2,1)S(1)}, bf16[512,128]{1,0:T(8,128)(2,1)S(1)}, u32[]{:S(2)}, u32[]{:S(2)}) collective-permute-start(bf16[512,128]{1,0:T(8,128)(2,1)S(1)} %collective-permute-done.35), channel_id=1, source_target_pairs={{0,16},{8,24},{16,0},{24,8},{1,17},{9,25},{17,1},{25,9},{2,18},{10... | collective-permute-start | bytes 393224 | tf_op jit(solution)/shard_map/ppermute | solution.py:32
  193.8 8.3 %collective-permute-start.38 = (bf16[512,128]{1,0:T(8,128)(2,1)S(1)}, bf16[512,128]{1,0:T(8,128)(2,1)S(1)}, u32[]{:S(2)}, u32[]{:S(2)}) collective-permute-start(bf16[512,128]{1,0:T(8,128)(2,1)S(1)} %collective-permute-done.35), channel_id=1, source_target_pairs={{0,24},{8,0},{16,8},{24,16},{1,25},{9,1},{17,9},{25,17},{2,26},{10... | collective-permute-start | bytes 393224 | tf_op jit(solution)/shard_map/ppermute | solution.py:32
  198.7 38.8 %copy-start.13 = (bf16[4,512,128]{2,1,0:T(8,128)(2,1)}, bf16[4,512,128]{2,1,0:T(8,128)(2,1)S(1)}, u32[]{:S(2)}) copy-start(bf16[4,512,128]{2,1,0:T(8,128)(2,1)S(1)} %pad_maximum_fusion.4.rest_0_) | copy-start | bytes 1572868
  198.7 13.3 %collective-permute-start.31 = (bf16[4,512,128]{2,1,0:T(8,128)(2,1)S(1)}, bf16[4,512,128]{2,1,0:T(8,128)(2,1)S(1)}, u32[]{:S(2)}, u32[]{:S(2)}) collective-permute-start(bf16[4,512,128]{2,1,0:T(8,128)(2,1)S(1)} %pad_maximum_fusion.4.rest_0_), channel_id=1, source_target_pairs={{0,8},{8,16},{16,24},{24,0},{1,9},{9,17},{17,25},{25,1},{2,10},{10... | collective-permute-start | bytes 1572872 | tf_op jit(solution)/shard_map/ppermute | solution.py:32
  198.8 14.0 %collective-permute-start.33 = (bf16[4,512,128]{2,1,0:T(8,128)(2,1)S(1)}, bf16[4,512,128]{2,1,0:T(8,128)(2,1)S(1)}, u32[]{:S(2)}, u32[]{:S(2)}) collective-permute-start(bf16[4,512,128]{2,1,0:T(8,128)(2,1)S(1)} %pad_maximum_fusion.4.rest_0_), channel_id=1, source_target_pairs={{0,24},{8,0},{16,8},{24,16},{1,25},{9,1},{17,9},{25,17},{2,26},{10... | collective-permute-start | bytes 1572872 | tf_op jit(solution)/shard_map/ppermute | solution.py:32
  202.1 35.4 %copy-start.14 = (bf16[4,512,128]{2,1,0:T(8,128)(2,1)}, bf16[4,512,128]{2,1,0:T(8,128)(2,1)S(1)}, u32[]{:S(2)}) copy-start(bf16[4,512,128]{2,1,0:T(8,128)(2,1)S(1)} %pad_maximum_fusion.5.rest_1_) | copy-start | bytes 1572868
  202.1 14.7 %collective-permute-start.39 = (bf16[4,512,128]{2,1,0:T(8,128)(2,1)S(1)}, bf16[4,512,128]{2,1,0:T(8,128)(2,1)S(1)}, u32[]{:S(2)}, u32[]{:S(2)}) collective-permute-start(bf16[4,512,128]{2,1,0:T(8,128)(2,1)S(1)} %pad_maximum_fusion.5.rest_1_), channel_id=1, source_target_pairs={{0,32},{32,64},{64,96},{96,0},{1,33},{33,65},{65,97},{97,1},{2,34}... | collective-permute-start | bytes 1572872 | tf_op jit(solution)/shard_map/ppermute | solution.py:32
  203.8 13.8 %collective-permute-start.41 = (bf16[4,512,128]{2,1,0:T(8,128)(2,1)S(1)}, bf16[4,512,128]{2,1,0:T(8,128)(2,1)S(1)}, u32[]{:S(2)}, u32[]{:S(2)}) collective-permute-start(bf16[4,512,128]{2,1,0:T(8,128)(2,1)S(1)} %pad_maximum_fusion.5.rest_1_), channel_id=1, source_target_pairs={{0,96},{32,0},{64,32},{96,64},{1,97},{33,1},{65,33},{97,65},{2,98}... | collective-permute-start | bytes 1572872 | tf_op jit(solution)/shard_map/ppermute | solution.py:32
  212.8 38.7 %collective-permute-start.32 = (bf16[2,512,128]{2,1,0:T(8,128)(2,1)}, bf16[2,512,128]{2,1,0:T(8,128)(2,1)S(1)}, u32[]{:S(2)}, u32[]{:S(2)}) collective-permute-start(bf16[2,512,128]{2,1,0:T(8,128)(2,1)} %slice.36), channel_id=1, source_target_pairs={{0,8},{8,16},{16,24},{24,0},{1,9},{9,17},{17,25},{25,1},{2,10},{10... | collective-permute-start | bytes 786440 | tf_op jit(solution)/shard_map/ppermute | solution.py:32
  213.6 37.9 %collective-permute-start.34 = (bf16[2,512,128]{2,1,0:T(8,128)(2,1)}, bf16[2,512,128]{2,1,0:T(8,128)(2,1)}, u32[]{:S(2)}, u32[]{:S(2)}) collective-permute-start(bf16[2,512,128]{2,1,0:T(8,128)(2,1)} %slice.37), channel_id=1, source_target_pairs={{0,24},{8,0},{16,8},{24,16},{1,25},{9,1},{17,9},{25,17},{2,26},{10... | collective-permute-start | bytes 786440 | tf_op jit(solution)/shard_map/ppermute | solution.py:32
  217.6 33.9 %collective-permute-start.40 = (bf16[2,512,128]{2,1,0:T(8,128)(2,1)}, bf16[2,512,128]{2,1,0:T(8,128)(2,1)}, u32[]{:S(2)}, u32[]{:S(2)}) collective-permute-start(bf16[2,512,128]{2,1,0:T(8,128)(2,1)} %slice.38), channel_id=1, source_target_pairs={{0,32},{32,64},{64,96},{96,0},{1,33},{33,65},{65,97},{97,1},{2,34}... | collective-permute-start | bytes 786440 | tf_op jit(solution)/shard_map/ppermute | solution.py:32
  218.4 33.1 %collective-permute-start.42 = (bf16[2,512,128]{2,1,0:T(8,128)(2,1)}, bf16[2,512,128]{2,1,0:T(8,128)(2,1)}, u32[]{:S(2)}, u32[]{:S(2)}) collective-permute-start(bf16[2,512,128]{2,1,0:T(8,128)(2,1)} %slice.39), channel_id=1, source_target_pairs={{0,96},{32,0},{64,32},{96,64},{1,97},{33,1},{65,33},{97,65},{2,98}... | collective-permute-start | bytes 786440 | tf_op jit(solution)/shard_map/ppermute | solution.py:32
  (17 other events, 226.2 us)

commit v5 on v4

--- a/solution.py
+++ b/solution.py
@@ -233,19 +233,14 @@
 def final_kernel(shifts, n_given, pos, weights, *rest):
     n = LAST * len(shifts)
     given = rest[:n_given]
-    out, tiles, results, prods, sems_in, sems_out, sems_prod = rest[-7:]
+    out, tiles, results, sems_in, sems_out = rest[-5:]
     heads = []
     for shift in shifts:
         x, z = (pos[0] + 4 - shift) % 4, (pos[1] + 4 - shift) % 4
         y = pos[2]
         heads += [(((pos[0] + 4 - early) % 4) * 4 + z) * 2 + y for early in range(4)]
         heads += [(x * 4 + (pos[1] + 4 - early) % 4) * 2 + 1 - y for early in range(4)]
-    pieces = [
-        pltpu.make_async_copy(
-            piece, prods.at[later, pl.ds(early, piece.shape[0])], sems_prod.at[i]
-        )
-        for i, (later, early, piece) in enumerate(blocks(given))
-    ]
+    prods = [piece.at[e] for piece in given for e in range(piece.shape[0])]
     into = [
         pltpu.make_async_copy(weights.at[h], tiles.at[i], sems_in.at[i]) for i, h in enumerate(heads)
     ]
@@ -257,16 +252,14 @@
         )
         for i, h in enumerate(heads)
     ]
-    for copy in pieces + into:
+    for copy in into:
         copy.start()
-    for copy in pieces:
-        copy.wait()
     for first in range(0, n, 4):
         for i in range(first, first + 4):
             into[i].wait()
         held = None
         for i in range(first, first + 4):
-            both = jnp.dot(tiles[i], prods[i // 4, i % 4], preferred_element_type=F32)
+            both = jnp.dot(tiles[i], prods[i][...], preferred_element_type=F32)
             if held is not None:
                 results[i - 1] = held.astype(BF16)
             held = both
@@ -283,19 +276,19 @@
     n = LAST * len(shifts)
     return pl.pallas_call(
         functools.partial(final_kernel, shifts, len(pieces)),
-        in_specs=[pl.BlockSpec(memory_space=pltpu.SMEM)]
-        + [anywhere] * (1 + len(pieces) + len(out)),
+        in_specs=[pl.BlockSpec(memory_space=pltpu.SMEM), anywhere]
+        + [pl.BlockSpec(memory_space=pltpu.VMEM)] * len(pieces)
+        + [anywhere] * len(out),
         out_specs=anywhere,
         out_shape=jax.ShapeDtypeStruct((here, D), BF16),
         scratch_shapes=[
             pltpu.VMEM((n, here, M), BF16),
             pltpu.VMEM((n, here, DH), BF16),
-            pltpu.VMEM((2 * len(shifts), 4, M, DH), BF16),
             pltpu.SemaphoreType.DMA((n,)),
             pltpu.SemaphoreType.DMA((n,)),
-            pltpu.SemaphoreType.DMA((len(pieces),)),
         ],
         input_output_aliases={2 + len(pieces): 0} if out else {},
+        compiler_params=pltpu.CompilerParams(vmem_limit_bytes=24 << 20),
     )(pos, weights, *pieces, *out)
 
 

time: 258 us -> 257 us (level)
  Pallas kernels: 70.1 us -> 63.1 us
  local copies, waits for them, and re-layouts: 7.75 us -> 12.5 us
    pallas_call x3, Pallas kernels: 19.2 us -> 12.2 us  [final(): pl.pallas_call(functools.partial(final_kernel, shifts, len(pieces)), in_s...]
    unnamed x42 -> x32, local copies, waits for them, and re-layouts: 1.57 us -> 6.6 us
  transfers between devices with their start and end apart: 44 -> 44, of which waited for: 15 -> 15; matrix products, arithmetic and copies ran while one was open for 4% -> 4% of each run, Pallas kernels for 17% -> 15%
where the time goes in v5:
time: 257 us; the launch traced here: 256 us
  starting transfers between devices  87.6 us (34%)
  waiting for transfers between devices  83.5 us (32%)
  Pallas kernels  63.1 us (25%)
  local copies, waits for them, and re-layouts  12.5 us (5%)
  other arithmetic  8.6 us (3%)
    ppermute x43, waiting for transfers between devices, shifted(): return lax.ppermute(v, axis, [(i, (i + by) % n) for i in range(n)])  83.5 us
    ppermute x43, starting transfers between devices, shifted(): return lax.ppermute(v, axis, [(i, (i + by) % n) for i in range(n)])  82.4 us
    pallas_call x1, Pallas kernels, steps(): call(parts_kernel, (H // GROUP,), [column, column] + per_head(land_q), pl...  16.7 us
    pallas_call x1, Pallas kernels, steps(): call(near_kernel, (H // GROUP,), [column] + per_head(land_k), pl.BlockSpe...  15.9 us
    pallas_call x1, Pallas kernels, steps(): call(functools.partial(inverse_kernel, len(land_q)), (1,), owned(land_q)...  13.5 us
    pallas_call x3, Pallas kernels, final(): pl.pallas_call(functools.partial(final_kernel, shifts, len(pieces)), in_s...  12.2 us
    reduce_sum x2, other arithmetic, landmarks(): sums = jnp.sum(tokens.reshape(per_device, segment, D), axis=1, dtype=F32)  6.61 us
    unnamed x32, local copies, waits for them, and re-layouts  6.6 us
  transfers between devices with their start and end apart: 44, of which 15 were waited for; matrix products, arithmetic and copies ran while one was open for 4% of the time, Pallas kernels for 15%

profile of v5, /device:TPU:0, one launch (start us, length us, event | category | flops | bytes accessed | tf_op | source)
XLA Modules:
  0.0 255.9 jit_solution(7458713298769089801)
XLA Ops:
  0.0 3.3 %convert_reduce_fusion = f32[16,4096]{1,0:T(8,128)S(1)} fusion(bf16[512,4096]{1,0:T(8,128)(2,1)} %queries.1), kind=kLoop, calls=%fused_computation | loop fusion | flops 4128768 | bytes 4456448 | tf_op jit(solution)/shard_map/reduce_sum | solution.py:312
  3.3 1.8 collective-permute-start.20
  5.1 1.5 collective-permute-start.13
  6.6 2.7 %collective-permute-start.14 = (bf16[16,4096]{1,0:T(8,128)(2,1)S(1)}, bf16[16,4096]{1,0:T(8,128)(2,1)S(1)}, u32[]{:S(2)}, u32[]{:S(2)}) collective-permute-start(bf16[16,4096]{1,0:T(8,128)(2,1)S(1)} %multiply_convert_fusion), channel_id=1, source_target_pairs={{0,64},{32,96},{64,0},{96,32},{1,65},{33,97},{65,1},{97,33},{2,66}... | collective-permute-start | bytes 393224 | tf_op jit(solution)/shard_map/ppermute | solution.py:32
  9.3 1.4 collective-permute-start.15
  10.8 2.0 collective-permute-start.21
  12.8 3.6 %collective-permute-start.22 = (bf16[16,4096]{1,0:T(8,128)(2,1)S(1)}, bf16[16,4096]{1,0:T(8,128)(2,1)S(1)}, u32[]{:S(2)}, u32[]{:S(2)}) collective-permute-start(bf16[16,4096]{1,0:T(8,128)(2,1)S(1)} %collective-permute-done.20), channel_id=1, source_target_pairs={{0,16},{8,24},{16,0},{24,8},{1,17},{9,25},{17,1},{25,9},{2,18},{10... | collective-permute-start | bytes 393224 | tf_op jit(solution)/shard_map/ppermute | solution.py:32
  18.6 2.2 collective-permute-start.18
  20.8 1.7 collective-permute-done.22
  23.7 2.6 %collective-permute-start.26 = (bf16[4,16,4096]{2,1,0:T(8,128)(2,1)S(1)}, bf16[4,16,4096]{2,1,0:T(8,128)(2,1)S(1)}, u32[]{:S(2)}, u32[]{:S(2)}) collective-permute-start(bf16[4,16,4096]{2,1,0:T(8,128)(2,1)S(1)} %pad_maximum_fusion.3.rest_5_), channel_id=1, source_target_pairs={{0,96},{32,0},{64,32},{96,64},{1,97},{33,1},{65,33},{97,65},{2,98}... | collective-permute-start | bytes 1572872 | tf_op jit(solution)/shard_map/ppermute | solution.py:32
  26.4 5.5 %collective-permute-done.16.rest_1_ = bf16[4,16,4096]{2,1,0:T(8,128)(2,1)S(1)} collective-permute-done((bf16[4,16,4096]{2,1,0:T(8,128)(2,1)S(1)}, bf16[4,16,4096]{2,1,0:T(8,128)(2,1)S(1)}, u32[]{:S(2)}, u32[]{:S(2)}) %collective-permute-start.16) | collective-permute-done | bytes 524320 | tf_op jit(solution)/shard_map/ppermute | solution.py:32
  33.5 3.2 %collective-permute-start.19 = (bf16[2,16,4096]{2,1,0:T(8,128)(2,1)}, bf16[2,16,4096]{2,1,0:T(8,128)(2,1)}, u32[]{:S(2)}, u32[]{:S(2)}) collective-permute-start(bf16[2,16,4096]{2,1,0:T(8,128)(2,1)} %slice.33), channel_id=1, source_target_pairs={{0,24},{8,0},{16,8},{24,16},{1,25},{9,1},{17,9},{25,17},{2,26},{10... | collective-permute-start | bytes 786440 | tf_op jit(solution)/shard_map/ppermute | solution.py:32
  39.4 2.0 collective-permute-start.27
  42.1 3.3 %collective-permute-done.25.rest_7_ = bf16[2,16,4096]{2,1,0:T(8,128)(2,1)} collective-permute-done((bf16[2,16,4096]{2,1,0:T(8,128)(2,1)}, bf16[2,16,4096]{2,1,0:T(8,128)(2,1)}, u32[]{:S(2)}, u32[]{:S(2)}) %collective-permute-start.25) | collective-permute-done | bytes 262176 | tf_op jit(solution)/shard_map/ppermute | solution.py:32
  46.2 16.7 %shard_map.38 = bf16[32,528,128]{2,1,0:T(8,128)(2,1)} custom-call(s32[3]{0:T(128)} %pad_add_fusion.pos, bf16[512,4096]{1,0:T(8,128)(2,1)} %keys.1, bf16[512,4096]{1,0:T(8,128)(2,1)} %values.1, bf16[4,16,4096]{2,1,0:T(8,128)(2,1)} %copy-done.2, bf16[4,16,4096]{2,1,0:T(8,128)(2,1)} %copy-done.6, bf16[2,16,4096]{2,1,0:T(8,128)(2,1)} %copy-done.15, ...), custom_call_target="tpu_custom_call" | custom-call | tf_op jit(solution)/shard_map/pallas_call | solution.py:330
  63.0 5.2 %all-to-all-start = ((bf16[32,528,128]{2,1,0:T(8,128)(2,1)}), bf16[32,528,128]{2,1,0:T(8,128)(2,1)}, u32[]{:S(2)}, u32[]{:S(2)}) async-start(bf16[32,528,128]{2,1,0:T(8,128)(2,1)} %shard_map.38), calls=%async_computation | async-start | bytes 8650752 | tf_op jit(solution)/shard_map/all_to_all | solution.py:338
  68.2 3.3 %convert_reduce_fusion.1 = f32[16,4096]{1,0:T(8,128)S(1)} fusion(bf16[512,4096]{1,0:T(8,128)(2,1)} %keys.1), kind=kLoop, calls=%fused_computation.1 | loop fusion | flops 4128768 | bytes 4456448 | tf_op jit(solution)/shard_map/reduce_sum | solution.py:312
  71.5 1.8 collective-permute-start.6
  73.4 1.5 collective-permute-start
  74.8 2.7 %collective-permute-start.1 = (bf16[16,4096]{1,0:T(8,128)(2,1)S(1)}, bf16[16,4096]{1,0:T(8,128)(2,1)S(1)}, u32[]{:S(2)}, u32[]{:S(2)}) collective-permute-start(bf16[16,4096]{1,0:T(8,128)(2,1)S(1)} %multiply_convert_fusion.1), channel_id=1, source_target_pairs={{0,64},{32,96},{64,0},{96,32},{1,65},{33,97},{65,1},{97,33},{2,66}... | collective-permute-start | bytes 393224 | tf_op jit(solution)/shard_map/ppermute | solution.py:32
  77.5 1.4 collective-permute-start.2
  79.0 39.7 %collective-permute-done.6 = bf16[16,4096]{1,0:T(8,128)(2,1)S(1)} collective-permute-done((bf16[16,4096]{1,0:T(8,128)(2,1)S(1)}, bf16[16,4096]{1,0:T(8,128)(2,1)S(1)}, u32[]{:S(2)}, u32[]{:S(2)}) %collective-permute-start.6) | collective-permute-done | bytes 131104 | tf_op jit(solution)/shard_map/ppermute | solution.py:32
  118.7 3.0 %collective-permute-start.8 = (bf16[16,4096]{1,0:T(8,128)(2,1)S(1)}, bf16[16,4096]{1,0:T(8,128)(2,1)S(1)}, u32[]{:S(2)}, u32[]{:S(2)}) collective-permute-start(bf16[16,4096]{1,0:T(8,128)(2,1)S(1)} %collective-permute-done.6), channel_id=1, source_target_pairs={{0,16},{8,24},{16,0},{24,8},{1,17},{9,25},{17,1},{25,9},{2,18},{10... | collective-permute-start | bytes 393224 | tf_op jit(solution)/shard_map/ppermute | solution.py:32
  121.7 5.0 %collective-permute-start.9 = (bf16[16,4096]{1,0:T(8,128)(2,1)S(1)}, bf16[16,4096]{1,0:T(8,128)(2,1)S(1)}, u32[]{:S(2)}, u32[]{:S(2)}) collective-permute-start(bf16[16,4096]{1,0:T(8,128)(2,1)S(1)} %collective-permute-done.6), channel_id=1, source_target_pairs={{0,24},{8,0},{16,8},{24,16},{1,25},{9,1},{17,9},{25,17},{2,26},{10... | collective-permute-start | bytes 393224 | tf_op jit(solution)/shard_map/ppermute | solution.py:32
  126.7 1.6 collective-permute-done.1
  129.4 2.1 collective-permute-start.4
  132.2 4.2 %collective-permute-done.9 = bf16[16,4096]{1,0:T(8,128)(2,1)S(1)} collective-permute-done((bf16[16,4096]{1,0:T(8,128)(2,1)S(1)}, bf16[16,4096]{1,0:T(8,128)(2,1)S(1)}, u32[]{:S(2)}, u32[]{:S(2)}) %collective-permute-start.9) | collective-permute-done | bytes 131104 | tf_op jit(solution)/shard_map/ppermute | solution.py:32
  136.5 5.1 %collective-permute-start.10 = (bf16[4,16,4096]{2,1,0:T(8,128)(2,1)S(1)}, bf16[4,16,4096]{2,1,0:T(8,128)(2,1)S(1)}, u32[]{:S(2)}, u32[]{:S(2)}) collective-permute-start(bf16[4,16,4096]{2,1,0:T(8,128)(2,1)S(1)} %pad_maximum_fusion.1.rest_4_.rest_14_), channel_id=1, source_target_pairs={{0,32},{32,64},{64,96},{96,0},{1,33},{33,65},{65,97},{97,1},{2,34}... | collective-permute-start | bytes 1572872 | tf_op jit(solution)/shard_map/ppermute | solution.py:32
  141.6 1.5 collective-permute-start.11
  143.1 10.0 %collective-permute-done.3.rest_1_.rest_11_ = bf16[4,16,4096]{2,1,0:T(8,128)(2,1)S(1)} collective-permute-done((bf16[4,16,4096]{2,1,0:T(8,128)(2,1)S(1)}, bf16[4,16,4096]{2,1,0:T(8,128)(2,1)S(1)}, u32[]{:S(2)}, u32[]{:S(2)}) %collective-permute-start.3) | collective-permute-done | bytes 524320 | tf_op jit(solution)/shard_map/ppermute | solution.py:32
  153.1 6.1 %collective-permute-start.12 = (bf16[4,16,4096]{2,1,0:T(8,128)(2,1)S(1)}, bf16[4,16,4096]{2,1,0:T(8,128)(2,1)}, u32[]{:S(2)}, u32[]{:S(2)}) collective-permute-start(bf16[4,16,4096]{2,1,0:T(8,128)(2,1)S(1)} %pad_maximum_fusion.1.rest_4_.rest_14_), channel_id=1, source_target_pairs={{0,96},{32,0},{64,32},{96,64},{1,97},{33,1},{65,33},{97,65},{2,98}... | collective-permute-start | bytes 1572872 | tf_op jit(solution)/shard_map/ppermute | solution.py:32
  161.1 4.8 %collective-permute-done.12.rest_7_.rest_17_ = bf16[4,16,4096]{2,1,0:T(8,128)(2,1)} collective-permute-done((bf16[4,16,4096]{2,1,0:T(8,128)(2,1)S(1)}, bf16[4,16,4096]{2,1,0:T(8,128)(2,1)}, u32[]{:S(2)}, u32[]{:S(2)}) %collective-permute-start.12) | collective-permute-done | bytes 524320 | tf_op jit(solution)/shard_map/ppermute | solution.py:32
  165.9 13.5 %shard_map.39.inverse = bf16[512,512]{1,0:T(8,128)(2,1)} custom-call(s32[3]{0:T(128)} %pad_add_fusion.pos, bf16[4,16,4096]{2,1,0:T(8,128)(2,1)} %copy-done.2, bf16[4,16,4096]{2,1,0:T(8,128)(2,1)} %copy-done.6, bf16[2,16,4096]{2,1,0:T(8,128)(2,1)} %copy-done.15, bf16[2,16,4096]{2,1,0:T(8,128)(2,1)} %collective-permute-done.19.rest_3_, ...), custom_call_target="tpu_custom_call" | custom-call | tf_op jit(solution)/shard_map/pallas_call | solution.py:353
  179.4 4.8 %shard_map.40 = bf16[512,128]{1,0:T(8,128)(2,1)} custom-call(bf16[32,528,128]{2,1,0:T(8,128)(2,1)} %all-to-all-done.parts.levels, bf16[32,528,128]{2,1,0:T(8,128)(2,1)} %all-to-all-done.parts.levels, bf16[512,512]{1,0:T(8,128)(2,1)} %shard_map.39.inverse), custom_call_target="tpu_custom_call" | custom-call | tf_op jit(solution)/shard_map/pallas_call | solution.py:362
  184.2 2.5 collective-permute-start.35
  186.7 5.3 %collective-permute-start.29 = (bf16[512,128]{1,0:T(8,128)(2,1)}, bf16[512,128]{1,0:T(8,128)(2,1)S(1)}, u32[]{:S(2)}, u32[]{:S(2)}) collective-permute-start(bf16[512,128]{1,0:T(8,128)(2,1)} %shard_map.40), channel_id=1, source_target_pairs={{0,64},{32,96},{64,0},{96,32},{1,65},{33,97},{65,1},{97,33},{2,66}... | collective-permute-start | bytes 393224 | tf_op jit(solution)/shard_map/ppermute | solution.py:32
  193.7 1.5 collective-permute-start.38
  195.3 1.9 collective-permute-done.29
  199.2 3.2 %collective-permute-start.33 = (bf16[4,512,128]{2,1,0:T(8,128)(2,1)S(1)}, bf16[4,512,128]{2,1,0:T(8,128)(2,1)S(1)}, u32[]{:S(2)}, u32[]{:S(2)}) collective-permute-start(bf16[4,512,128]{2,1,0:T(8,128)(2,1)S(1)} %pad_maximum_fusion.4.rest_0_), channel_id=1, source_target_pairs={{0,24},{8,0},{16,8},{24,16},{1,25},{9,1},{17,9},{25,17},{2,26},{10... | collective-permute-start | bytes 1572872 | tf_op jit(solution)/shard_map/ppermute | solution.py:32
  203.6 2.2 collective-permute-start.41
  205.8 6.6 %collective-permute-done.31.rest_0_ = bf16[4,512,128]{2,1,0:T(8,128)(2,1)S(1)} collective-permute-done((bf16[4,512,128]{2,1,0:T(8,128)(2,1)S(1)}, bf16[4,512,128]{2,1,0:T(8,128)(2,1)S(1)}, u32[]{:S(2)}, u32[]{:S(2)}) %collective-permute-start.31) | collective-permute-done | bytes 524320 | tf_op jit(solution)/shard_map/ppermute | solution.py:32
  213.8 3.2 %collective-permute-start.34 = (bf16[2,512,128]{2,1,0:T(8,128)(2,1)}, bf16[2,512,128]{2,1,0:T(8,128)(2,1)}, u32[]{:S(2)}, u32[]{:S(2)}) collective-permute-start(bf16[2,512,128]{2,1,0:T(8,128)(2,1)} %slice.37), channel_id=1, source_target_pairs={{0,24},{8,0},{16,8},{24,16},{1,25},{9,1},{17,9},{25,17},{2,26},{10... | collective-permute-start | bytes 786440 | tf_op jit(solution)/shard_map/ppermute | solution.py:32
  218.5 3.2 %collective-permute-start.42 = (bf16[2,512,128]{2,1,0:T(8,128)(2,1)}, bf16[2,512,128]{2,1,0:T(8,128)(2,1)}, u32[]{:S(2)}, u32[]{:S(2)}) collective-permute-start(bf16[2,512,128]{2,1,0:T(8,128)(2,1)} %slice.39), channel_id=1, source_target_pairs={{0,96},{32,0},{64,32},{96,64},{1,97},{33,1},{65,33},{97,65},{2,98}... | collective-permute-start | bytes 786440 | tf_op jit(solution)/shard_map/ppermute | solution.py:32
  221.7 15.9 %shard_map.37.weights = bf16[32,512,512]{2,1,0:T(8,128)(2,1)} custom-call(s32[3]{0:T(128)} %pad_add_fusion.pos, bf16[512,4096]{1,0:T(8,128)(2,1)} %queries.1, bf16[4,16,4096]{2,1,0:T(8,128)(2,1)} %copy-done.4, bf16[4,16,4096]{2,1,0:T(8,128)(2,1)} %copy-done.10, bf16[4,16,4096]{2,1,0:T(8,128)(2,1)} %copy-done.11, bf16[4,16,4096]{2,1,0:T(8,128)(2,1)} %copy-done.12, ...), custom_call_target="tpu_custom_call" | custom-call | tf_op jit(solution)/shard_map/pallas_call | solution.py:340
  237.7 5.8 %copy-done = bf16[32,512,512]{2,1,0:T(8,128)(2,1)S(1)} copy-done((bf16[32,512,512]{2,1,0:T(8,128)(2,1)S(1)}, bf16[32,512,512]{2,1,0:T(8,128)(2,1)}, u32[]{:S(2)}) %copy-start) | copy-done | bytes 16777240
  243.4 3.2 %shard_map.41.rest_4_ = bf16[512,4096]{1,0:T(8,128)(2,1)} custom-call(s32[3]{0:T(128)S(1)} %copy-done.1, bf16[32,512,512]{2,1,0:T(8,128)(2,1)S(1)} %copy-done, bf16[4,512,128]{2,1,0:T(8,128)(2,1)S(1)} %pad_maximum_fusion.4.rest_0_, bf16[4,512,128]{2,1,0:T(8,128)(2,1)S(1)} %pad_maximum_fusion.5.rest_1_), custom_call_target="tpu_custom_call" | custom-call | tf_op jit(solution)/shard_map/pallas_call | solution.py:277
  246.7 5.2 %shard_map.42.rest_4_ = bf16[512,4096]{1,0:T(8,128)(2,1)} custom-call(s32[3]{0:T(128)S(1)} %copy-done.1, bf16[32,512,512]{2,1,0:T(8,128)(2,1)S(1)} %copy-done, bf16[4,512,128]{2,1,0:T(8,128)(2,1)S(1)} %collective-permute-done.31.rest_0_, bf16[4,512,128]{2,1,0:T(8,128)(2,1)S(1)} %collective-permute-done.39.rest_1_, ...), custom_call_target="tpu_custom_call", output_to_operand_aliasing={{}: (6, {})} | custom-call | tf_op jit(solution)/shard_map/pallas_call | solution.py:277
  251.9 3.8 %shard_map.43 = bf16[512,4096]{1,0:T(8,128)(2,1)} custom-call(s32[3]{0:T(128)S(1)} %copy-done.1, bf16[32,512,512]{2,1,0:T(8,128)(2,1)S(1)} %copy-done, bf16[2,512,128]{2,1,0:T(8,128)(2,1)S(1)} %collective-permute-done.32.rest_0_, bf16[2,512,128]{2,1,0:T(8,128)(2,1)} %collective-permute-done.34.rest_1_, ...), custom_call_target="tpu_custom_call", output_to_operand_aliasing={{}: (6, {})} | custom-call | tf_op jit(solution)/shard_map/pallas_call | solution.py:277
  (100 shorter events, 20.8 us)
Async XLA Ops:
  3.3 7.4 %collective-permute-start.20 = (bf16[16,4096]{1,0:T(8,128)(2,1)S(1)}, bf16[16,4096]{1,0:T(8,128)(2,1)S(1)}, u32[]{:S(2)}, u32[]{:S(2)}) collective-permute-start(bf16[16,4096]{1,0:T(8,128)(2,1)S(1)} %multiply_convert_fusion), channel_id=1, source_target_pairs={{0,4},{4,0},{1,5},{5,1},{2,6},{6,2},{3,7},{7,3},{8,12},{12,8},{9,1... | collective-permute-start | bytes 393224 | tf_op jit(solution)/shard_map/ppermute | solution.py:32
  5.1 11.3 %collective-permute-start.13 = (bf16[16,4096]{1,0:T(8,128)(2,1)S(1)}, bf16[16,4096]{1,0:T(8,128)(2,1)S(1)}, u32[]{:S(2)}, u32[]{:S(2)}) collective-permute-start(bf16[16,4096]{1,0:T(8,128)(2,1)S(1)} %multiply_convert_fusion), channel_id=1, source_target_pairs={{0,32},{32,64},{64,96},{96,0},{1,33},{33,65},{65,97},{97,1},{2,34}... | collective-permute-start | bytes 393224 | tf_op jit(solution)/shard_map/ppermute | solution.py:32
  6.6 10.8 %collective-permute-start.14 = (bf16[16,4096]{1,0:T(8,128)(2,1)S(1)}, bf16[16,4096]{1,0:T(8,128)(2,1)S(1)}, u32[]{:S(2)}, u32[]{:S(2)}) collective-permute-start(bf16[16,4096]{1,0:T(8,128)(2,1)S(1)} %multiply_convert_fusion), channel_id=1, source_target_pairs={{0,64},{32,96},{64,0},{96,32},{1,65},{33,97},{65,1},{97,33},{2,66}... | collective-permute-start | bytes 393224 | tf_op jit(solution)/shard_map/ppermute | solution.py:32
  9.3 8.1 %collective-permute-start.15 = (bf16[16,4096]{1,0:T(8,128)(2,1)S(1)}, bf16[16,4096]{1,0:T(8,128)(2,1)S(1)}, u32[]{:S(2)}, u32[]{:S(2)}) collective-permute-start(bf16[16,4096]{1,0:T(8,128)(2,1)S(1)} %multiply_convert_fusion), channel_id=1, source_target_pairs={{0,96},{32,0},{64,32},{96,64},{1,97},{33,1},{65,33},{97,65},{2,98}... | collective-permute-start | bytes 393224 | tf_op jit(solution)/shard_map/ppermute | solution.py:32
  10.8 10.0 %collective-permute-start.21 = (bf16[16,4096]{1,0:T(8,128)(2,1)S(1)}, bf16[16,4096]{1,0:T(8,128)(2,1)S(1)}, u32[]{:S(2)}, u32[]{:S(2)}) collective-permute-start(bf16[16,4096]{1,0:T(8,128)(2,1)S(1)} %collective-permute-done.20), channel_id=1, source_target_pairs={{0,8},{8,16},{16,24},{24,0},{1,9},{9,17},{17,25},{25,1},{2,10},{10... | collective-permute-start | bytes 393224 | tf_op jit(solution)/shard_map/ppermute | solution.py:32
  12.8 9.7 %collective-permute-start.22 = (bf16[16,4096]{1,0:T(8,128)(2,1)S(1)}, bf16[16,4096]{1,0:T(8,128)(2,1)S(1)}, u32[]{:S(2)}, u32[]{:S(2)}) collective-permute-start(bf16[16,4096]{1,0:T(8,128)(2,1)S(1)} %collective-permute-done.20), channel_id=1, source_target_pairs={{0,16},{8,24},{16,0},{24,8},{1,17},{9,25},{17,1},{25,9},{2,18},{10... | collective-permute-start | bytes 393224 | tf_op jit(solution)/shard_map/ppermute | solution.py:32
  16.4 6.6 %collective-permute-start.23 = (bf16[16,4096]{1,0:T(8,128)(2,1)S(1)}, bf16[16,4096]{1,0:T(8,128)(2,1)S(1)}, u32[]{:S(2)}, u32[]{:S(2)}) collective-permute-start(bf16[16,4096]{1,0:T(8,128)(2,1)S(1)} %collective-permute-done.20), channel_id=1, source_target_pairs={{0,24},{8,0},{16,8},{24,16},{1,25},{9,1},{17,9},{25,17},{2,26},{10... | collective-permute-start | bytes 393224 | tf_op jit(solution)/shard_map/ppermute | solution.py:32
  17.5 28.7 %copy-start.2 = (bf16[4,16,4096]{2,1,0:T(8,128)(2,1)}, bf16[4,16,4096]{2,1,0:T(8,128)(2,1)S(1)}, u32[]{:S(2)}) copy-start(bf16[4,16,4096]{2,1,0:T(8,128)(2,1)S(1)} %pad_maximum_fusion.2.rest_0_) | copy-start | bytes 1572868
  17.5 14.4 %collective-permute-start.16 = (bf16[4,16,4096]{2,1,0:T(8,128)(2,1)S(1)}, bf16[4,16,4096]{2,1,0:T(8,128)(2,1)S(1)}, u32[]{:S(2)}, u32[]{:S(2)}) collective-permute-start(bf16[4,16,4096]{2,1,0:T(8,128)(2,1)S(1)} %pad_maximum_fusion.2.rest_0_), channel_id=1, source_target_pairs={{0,8},{8,16},{16,24},{24,0},{1,9},{9,17},{17,25},{25,1},{2,10},{10... | collective-permute-start | bytes 1572872 | tf_op jit(solution)/shard_map/ppermute | solution.py:32
  18.6 14.1 %collective-permute-start.18 = (bf16[4,16,4096]{2,1,0:T(8,128)(2,1)S(1)}, bf16[4,16,4096]{2,1,0:T(8,128)(2,1)S(1)}, u32[]{:S(2)}, u32[]{:S(2)}) collective-permute-start(bf16[4,16,4096]{2,1,0:T(8,128)(2,1)S(1)} %pad_maximum_fusion.2.rest_0_), channel_id=1, source_target_pairs={{0,24},{8,0},{16,8},{24,16},{1,25},{9,1},{17,9},{25,17},{2,26},{10... | collective-permute-start | bytes 1572872 | tf_op jit(solution)/shard_map/ppermute | solution.py:32
  23.1 23.1 %copy-start.3 = (bf16[4,16,4096]{2,1,0:T(8,128)(2,1)}, bf16[4,16,4096]{2,1,0:T(8,128)(2,1)S(1)}, u32[]{:S(2)}) copy-start(bf16[4,16,4096]{2,1,0:T(8,128)(2,1)S(1)} %pad_maximum_fusion.3.rest_5_) | copy-start | bytes 1572868
  23.1 13.6 %collective-permute-start.24 = (bf16[4,16,4096]{2,1,0:T(8,128)(2,1)S(1)}, bf16[4,16,4096]{2,1,0:T(8,128)(2,1)S(1)}, u32[]{:S(2)}, u32[]{:S(2)}) collective-permute-start(bf16[4,16,4096]{2,1,0:T(8,128)(2,1)S(1)} %pad_maximum_fusion.3.rest_5_), channel_id=1, source_target_pairs={{0,32},{32,64},{64,96},{96,0},{1,33},{33,65},{65,97},{97,1},{2,34}... | collective-permute-start | bytes 1572872 | tf_op jit(solution)/shard_map/ppermute | solution.py:32
  23.7 14.9 %collective-permute-start.26 = (bf16[4,16,4096]{2,1,0:T(8,128)(2,1)S(1)}, bf16[4,16,4096]{2,1,0:T(8,128)(2,1)S(1)}, u32[]{:S(2)}, u32[]{:S(2)}) collective-permute-start(bf16[4,16,4096]{2,1,0:T(8,128)(2,1)S(1)} %pad_maximum_fusion.3.rest_5_), channel_id=1, source_target_pairs={{0,96},{32,0},{64,32},{96,64},{1,97},{33,1},{65,33},{97,65},{2,98}... | collective-permute-start | bytes 1572872 | tf_op jit(solution)/shard_map/ppermute | solution.py:32
  32.7 9.4 %collective-permute-start.17 = (bf16[2,16,4096]{2,1,0:T(8,128)(2,1)}, bf16[2,16,4096]{2,1,0:T(8,128)(2,1)S(1)}, u32[]{:S(2)}, u32[]{:S(2)}) collective-permute-start(bf16[2,16,4096]{2,1,0:T(8,128)(2,1)} %slice.32), channel_id=1, source_target_pairs={{0,8},{8,16},{16,24},{24,0},{1,9},{9,17},{17,25},{25,1},{2,10},{10... | collective-permute-start | bytes 786440 | tf_op jit(solution)/shard_map/ppermute | solution.py:32
  33.5 8.6 %collective-permute-start.19 = (bf16[2,16,4096]{2,1,0:T(8,128)(2,1)}, bf16[2,16,4096]{2,1,0:T(8,128)(2,1)}, u32[]{:S(2)}, u32[]{:S(2)}) collective-permute-start(bf16[2,16,4096]{2,1,0:T(8,128)(2,1)} %slice.33), channel_id=1, source_target_pairs={{0,24},{8,0},{16,8},{24,16},{1,25},{9,1},{17,9},{25,17},{2,26},{10... | collective-permute-start | bytes 786440 | tf_op jit(solution)/shard_map/ppermute | solution.py:32
  37.5 7.9 %collective-permute-start.25 = (bf16[2,16,4096]{2,1,0:T(8,128)(2,1)}, bf16[2,16,4096]{2,1,0:T(8,128)(2,1)}, u32[]{:S(2)}, u32[]{:S(2)}) collective-permute-start(bf16[2,16,4096]{2,1,0:T(8,128)(2,1)} %slice.34), channel_id=1, source_target_pairs={{0,32},{32,64},{64,96},{96,0},{1,33},{33,65},{65,97},{97,1},{2,34}... | collective-permute-start | bytes 786440 | tf_op jit(solution)/shard_map/ppermute | solution.py:32
  39.4 6.8 %collective-permute-start.27 = (bf16[2,16,4096]{2,1,0:T(8,128)(2,1)}, bf16[2,16,4096]{2,1,0:T(8,128)(2,1)}, u32[]{:S(2)}, u32[]{:S(2)}) collective-permute-start(bf16[2,16,4096]{2,1,0:T(8,128)(2,1)} %slice.35), channel_id=1, source_target_pairs={{0,96},{32,0},{64,32},{96,64},{1,97},{33,1},{65,33},{97,65},{2,98}... | collective-permute-start | bytes 786440 | tf_op jit(solution)/shard_map/ppermute | solution.py:32
  63.0 116.5 %all-to-all-start = ((bf16[32,528,128]{2,1,0:T(8,128)(2,1)}), bf16[32,528,128]{2,1,0:T(8,128)(2,1)}, u32[]{:S(2)}, u32[]{:S(2)}) async-start(bf16[32,528,128]{2,1,0:T(8,128)(2,1)} %shard_map.38), calls=%async_computation | async-start | bytes 8650752 | tf_op jit(solution)/shard_map/all_to_all | solution.py:338
  71.5 47.1 %collective-permute-start.6 = (bf16[16,4096]{1,0:T(8,128)(2,1)S(1)}, bf16[16,4096]{1,0:T(8,128)(2,1)S(1)}, u32[]{:S(2)}, u32[]{:S(2)}) collective-permute-start(bf16[16,4096]{1,0:T(8,128)(2,1)S(1)} %multiply_convert_fusion.1), channel_id=1, source_target_pairs={{0,4},{4,0},{1,5},{5,1},{2,6},{6,2},{3,7},{7,3},{8,12},{12,8},{9,1... | collective-permute-start | bytes 393224 | tf_op jit(solution)/shard_map/ppermute | solution.py:32
  73.4 53.3 %collective-permute-start = (bf16[16,4096]{1,0:T(8,128)(2,1)S(1)}, bf16[16,4096]{1,0:T(8,128)(2,1)S(1)}, u32[]{:S(2)}, u32[]{:S(2)}) collective-permute-start(bf16[16,4096]{1,0:T(8,128)(2,1)S(1)} %multiply_convert_fusion.1), channel_id=1, source_target_pairs={{0,32},{32,64},{64,96},{96,0},{1,33},{33,65},{65,97},{97,1},{2,34}... | collective-permute-start | bytes 393224 | tf_op jit(solution)/shard_map/ppermute | solution.py:32
  74.8 53.5 %collective-permute-start.1 = (bf16[16,4096]{1,0:T(8,128)(2,1)S(1)}, bf16[16,4096]{1,0:T(8,128)(2,1)S(1)}, u32[]{:S(2)}, u32[]{:S(2)}) collective-permute-start(bf16[16,4096]{1,0:T(8,128)(2,1)S(1)} %multiply_convert_fusion.1), channel_id=1, source_target_pairs={{0,64},{32,96},{64,0},{96,32},{1,65},{33,97},{65,1},{97,33},{2,66}... | collective-permute-start | bytes 393224 | tf_op jit(solution)/shard_map/ppermute | solution.py:32
  77.5 50.7 %collective-permute-start.2 = (bf16[16,4096]{1,0:T(8,128)(2,1)S(1)}, bf16[16,4096]{1,0:T(8,128)(2,1)S(1)}, u32[]{:S(2)}, u32[]{:S(2)}) collective-permute-start(bf16[16,4096]{1,0:T(8,128)(2,1)S(1)} %multiply_convert_fusion.1), channel_id=1, source_target_pairs={{0,96},{32,0},{64,32},{96,64},{1,97},{33,1},{65,33},{97,65},{2,98}... | collective-permute-start | bytes 393224 | tf_op jit(solution)/shard_map/ppermute | solution.py:32
  118.7 12.8 %collective-permute-start.8 = (bf16[16,4096]{1,0:T(8,128)(2,1)S(1)}, bf16[16,4096]{1,0:T(8,128)(2,1)S(1)}, u32[]{:S(2)}, u32[]{:S(2)}) collective-permute-start(bf16[16,4096]{1,0:T(8,128)(2,1)S(1)} %collective-permute-done.6), channel_id=1, source_target_pairs={{0,16},{8,24},{16,0},{24,8},{1,17},{9,25},{17,1},{25,9},{2,18},{10... | collective-permute-start | bytes 393224 | tf_op jit(solution)/shard_map/ppermute | solution.py:32
  121.7 14.7 %collective-permute-start.9 = (bf16[16,4096]{1,0:T(8,128)(2,1)S(1)}, bf16[16,4096]{1,0:T(8,128)(2,1)S(1)}, u32[]{:S(2)}, u32[]{:S(2)}) collective-permute-start(bf16[16,4096]{1,0:T(8,128)(2,1)S(1)} %collective-permute-done.6), channel_id=1, source_target_pairs={{0,24},{8,0},{16,8},{24,16},{1,25},{9,1},{17,9},{25,17},{2,26},{10... | collective-permute-start | bytes 393224 | tf_op jit(solution)/shard_map/ppermute | solution.py:32
  126.6 9.7 %collective-permute-start.7 = (bf16[16,4096]{1,0:T(8,128)(2,1)S(1)}, bf16[16,4096]{1,0:T(8,128)(2,1)S(1)}, u32[]{:S(2)}, u32[]{:S(2)}) collective-permute-start(bf16[16,4096]{1,0:T(8,128)(2,1)S(1)} %collective-permute-done.6), channel_id=1, source_target_pairs={{0,8},{8,16},{16,24},{24,0},{1,9},{9,17},{17,25},{25,1},{2,10},{10... | collective-permute-start | bytes 393224 | tf_op jit(solution)/shard_map/ppermute | solution.py:32
  128.3 37.5 %copy-start.4 = (bf16[4,16,4096]{2,1,0:T(8,128)(2,1)}, bf16[4,16,4096]{2,1,0:T(8,128)(2,1)S(1)}, u32[]{:S(2)}) copy-start(bf16[4,16,4096]{2,1,0:T(8,128)(2,1)S(1)} %pad_maximum_fusion.rest_0_.rest_10_) | copy-start | bytes 1572868
  128.4 24.8 %collective-permute-start.3 = (bf16[4,16,4096]{2,1,0:T(8,128)(2,1)S(1)}, bf16[4,16,4096]{2,1,0:T(8,128)(2,1)S(1)}, u32[]{:S(2)}, u32[]{:S(2)}) collective-permute-start(bf16[4,16,4096]{2,1,0:T(8,128)(2,1)S(1)} %pad_maximum_fusion.rest_0_.rest_10_), channel_id=1, source_target_pairs={{0,8},{8,16},{16,24},{24,0},{1,9},{9,17},{17,25},{25,1},{2,10},{10... | collective-permute-start | bytes 1572872 | tf_op jit(solution)/shard_map/ppermute | solution.py:32
  129.4 29.8 %collective-permute-start.4 = (bf16[4,16,4096]{2,1,0:T(8,128)(2,1)S(1)}, bf16[4,16,4096]{2,1,0:T(8,128)(2,1)S(1)}, u32[]{:S(2)}, u32[]{:S(2)}) collective-permute-start(bf16[4,16,4096]{2,1,0:T(8,128)(2,1)S(1)} %pad_maximum_fusion.rest_0_.rest_10_), channel_id=1, source_target_pairs={{0,16},{8,24},{16,0},{24,8},{1,17},{9,25},{17,1},{25,9},{2,18},{10... | collective-permute-start | bytes 1572872 | tf_op jit(solution)/shard_map/ppermute | solution.py:32
  131.5 27.7 %collective-permute-start.5 = (bf16[4,16,4096]{2,1,0:T(8,128)(2,1)S(1)}, bf16[4,16,4096]{2,1,0:T(8,128)(2,1)S(1)}, u32[]{:S(2)}, u32[]{:S(2)}) collective-permute-start(bf16[4,16,4096]{2,1,0:T(8,128)(2,1)S(1)} %pad_maximum_fusion.rest_0_.rest_10_), channel_id=1, source_target_pairs={{0,24},{8,0},{16,8},{24,16},{1,25},{9,1},{17,9},{25,17},{2,26},{10... | collective-permute-start | bytes 1572872 | tf_op jit(solution)/shard_map/ppermute | solution.py:32
  136.5 29.4 %copy-start.5 = (bf16[4,16,4096]{2,1,0:T(8,128)(2,1)}, bf16[4,16,4096]{2,1,0:T(8,128)(2,1)S(1)}, u32[]{:S(2)}) copy-start(bf16[4,16,4096]{2,1,0:T(8,128)(2,1)S(1)} %pad_maximum_fusion.1.rest_4_.rest_14_) | copy-start | bytes 1572868
  136.5 22.7 %collective-permute-start.10 = (bf16[4,16,4096]{2,1,0:T(8,128)(2,1)S(1)}, bf16[4,16,4096]{2,1,0:T(8,128)(2,1)S(1)}, u32[]{:S(2)}, u32[]{:S(2)}) collective-permute-start(bf16[4,16,4096]{2,1,0:T(8,128)(2,1)S(1)} %pad_maximum_fusion.1.rest_4_.rest_14_), channel_id=1, source_target_pairs={{0,32},{32,64},{64,96},{96,0},{1,33},{33,65},{65,97},{97,1},{2,34}... | collective-permute-start | bytes 1572872 | tf_op jit(solution)/shard_map/ppermute | solution.py:32
  141.6 18.8 %collective-permute-start.11 = (bf16[4,16,4096]{2,1,0:T(8,128)(2,1)S(1)}, bf16[4,16,4096]{2,1,0:T(8,128)(2,1)S(1)}, u32[]{:S(2)}, u32[]{:S(2)}) collective-permute-start(bf16[4,16,4096]{2,1,0:T(8,128)(2,1)S(1)} %pad_maximum_fusion.1.rest_4_.rest_14_), channel_id=1, source_target_pairs={{0,64},{32,96},{64,0},{96,32},{1,65},{33,97},{65,1},{97,33},{2,66}... | collective-permute-start | bytes 1572872 | tf_op jit(solution)/shard_map/ppermute | solution.py:32
  153.1 12.8 %collective-permute-start.12 = (bf16[4,16,4096]{2,1,0:T(8,128)(2,1)S(1)}, bf16[4,16,4096]{2,1,0:T(8,128)(2,1)}, u32[]{:S(2)}, u32[]{:S(2)}) collective-permute-start(bf16[4,16,4096]{2,1,0:T(8,128)(2,1)S(1)} %pad_maximum_fusion.1.rest_4_.rest_14_), channel_id=1, source_target_pairs={{0,96},{32,0},{64,32},{96,64},{1,97},{33,1},{65,33},{97,65},{2,98}... | collective-permute-start | bytes 1572872 | tf_op jit(solution)/shard_map/ppermute | solution.py:32
  184.2 7.8 %collective-permute-start.35 = (bf16[512,128]{1,0:T(8,128)(2,1)}, bf16[512,128]{1,0:T(8,128)(2,1)S(1)}, u32[]{:S(2)}, u32[]{:S(2)}) collective-permute-start(bf16[512,128]{1,0:T(8,128)(2,1)} %shard_map.40), channel_id=1, source_target_pairs={{0,4},{4,0},{1,5},{5,1},{2,6},{6,2},{3,7},{7,3},{8,12},{12,8},{9,1... | collective-permute-start | bytes 393224 | tf_op jit(solution)/shard_map/ppermute | solution.py:32
  186.7 7.0 %collective-permute-start.28 = (bf16[512,128]{1,0:T(8,128)(2,1)}, bf16[512,128]{1,0:T(8,128)(2,1)S(1)}, u32[]{:S(2)}, u32[]{:S(2)}) collective-permute-start(bf16[512,128]{1,0:T(8,128)(2,1)} %shard_map.40), channel_id=1, source_target_pairs={{0,32},{32,64},{64,96},{96,0},{1,33},{33,65},{65,97},{97,1},{2,34}... | collective-permute-start | bytes 393224 | tf_op jit(solution)/shard_map/ppermute | solution.py:32
  186.7 10.4 %collective-permute-start.29 = (bf16[512,128]{1,0:T(8,128)(2,1)}, bf16[512,128]{1,0:T(8,128)(2,1)S(1)}, u32[]{:S(2)}, u32[]{:S(2)}) collective-permute-start(bf16[512,128]{1,0:T(8,128)(2,1)} %shard_map.40), channel_id=1, source_target_pairs={{0,64},{32,96},{64,0},{96,32},{1,65},{33,97},{65,1},{97,33},{2,66}... | collective-permute-start | bytes 393224 | tf_op jit(solution)/shard_map/ppermute | solution.py:32
  192.0 6.1 %collective-permute-start.30 = (bf16[512,128]{1,0:T(8,128)(2,1)}, bf16[512,128]{1,0:T(8,128)(2,1)S(1)}, u32[]{:S(2)}, u32[]{:S(2)}) collective-permute-start(bf16[512,128]{1,0:T(8,128)(2,1)} %shard_map.40), channel_id=1, source_target_pairs={{0,96},{32,0},{64,32},{96,64},{1,97},{33,1},{65,33},{97,65},{2,98}... | collective-permute-start | bytes 393224 | tf_op jit(solution)/shard_map/ppermute | solution.py:32
  192.0 10.4 %collective-permute-start.36 = (bf16[512,128]{1,0:T(8,128)(2,1)S(1)}, bf16[512,128]{1,0:T(8,128)(2,1)S(1)}, u32[]{:S(2)}, u32[]{:S(2)}) collective-permute-start(bf16[512,128]{1,0:T(8,128)(2,1)S(1)} %collective-permute-done.35), channel_id=1, source_target_pairs={{0,8},{8,16},{16,24},{24,0},{1,9},{9,17},{17,25},{25,1},{2,10},{10... | collective-permute-start | bytes 393224 | tf_op jit(solution)/shard_map/ppermute | solution.py:32
  192.0 10.4 %collective-permute-start.37 = (bf16[512,128]{1,0:T(8,128)(2,1)S(1)}, bf16[512,128]{1,0:T(8,128)(2,1)S(1)}, u32[]{:S(2)}, u32[]{:S(2)}) collective-permute-start(bf16[512,128]{1,0:T(8,128)(2,1)S(1)} %collective-permute-done.35), channel_id=1, source_target_pairs={{0,16},{8,24},{16,0},{24,8},{1,17},{9,25},{17,1},{25,9},{2,18},{10... | collective-permute-start | bytes 393224 | tf_op jit(solution)/shard_map/ppermute | solution.py:32
  193.7 8.7 %collective-permute-start.38 = (bf16[512,128]{1,0:T(8,128)(2,1)S(1)}, bf16[512,128]{1,0:T(8,128)(2,1)S(1)}, u32[]{:S(2)}, u32[]{:S(2)}) collective-permute-start(bf16[512,128]{1,0:T(8,128)(2,1)S(1)} %collective-permute-done.35), channel_id=1, source_target_pairs={{0,24},{8,0},{16,8},{24,16},{1,25},{9,1},{17,9},{25,17},{2,26},{10... | collective-permute-start | bytes 393224 | tf_op jit(solution)/shard_map/ppermute | solution.py:32
  199.1 13.3 %collective-permute-start.31 = (bf16[4,512,128]{2,1,0:T(8,128)(2,1)S(1)}, bf16[4,512,128]{2,1,0:T(8,128)(2,1)S(1)}, u32[]{:S(2)}, u32[]{:S(2)}) collective-permute-start(bf16[4,512,128]{2,1,0:T(8,128)(2,1)S(1)} %pad_maximum_fusion.4.rest_0_), channel_id=1, source_target_pairs={{0,8},{8,16},{16,24},{24,0},{1,9},{9,17},{17,25},{25,1},{2,10},{10... | collective-permute-start | bytes 1572872 | tf_op jit(solution)/shard_map/ppermute | solution.py:32
  199.2 13.9 %collective-permute-start.33 = (bf16[4,512,128]{2,1,0:T(8,128)(2,1)S(1)}, bf16[4,512,128]{2,1,0:T(8,128)(2,1)S(1)}, u32[]{:S(2)}, u32[]{:S(2)}) collective-permute-start(bf16[4,512,128]{2,1,0:T(8,128)(2,1)S(1)} %pad_maximum_fusion.4.rest_0_), channel_id=1, source_target_pairs={{0,24},{8,0},{16,8},{24,16},{1,25},{9,1},{17,9},{25,17},{2,26},{10... | collective-permute-start | bytes 1572872 | tf_op jit(solution)/shard_map/ppermute | solution.py:32
  202.5 14.6 %collective-permute-start.39 = (bf16[4,512,128]{2,1,0:T(8,128)(2,1)S(1)}, bf16[4,512,128]{2,1,0:T(8,128)(2,1)S(1)}, u32[]{:S(2)}, u32[]{:S(2)}) collective-permute-start(bf16[4,512,128]{2,1,0:T(8,128)(2,1)S(1)} %pad_maximum_fusion.5.rest_1_), channel_id=1, source_target_pairs={{0,32},{32,64},{64,96},{96,0},{1,33},{33,65},{65,97},{97,1},{2,34}... | collective-permute-start | bytes 1572872 | tf_op jit(solution)/shard_map/ppermute | solution.py:32
  203.6 14.2 %collective-permute-start.41 = (bf16[4,512,128]{2,1,0:T(8,128)(2,1)S(1)}, bf16[4,512,128]{2,1,0:T(8,128)(2,1)S(1)}, u32[]{:S(2)}, u32[]{:S(2)}) collective-permute-start(bf16[4,512,128]{2,1,0:T(8,128)(2,1)S(1)} %pad_maximum_fusion.5.rest_1_), channel_id=1, source_target_pairs={{0,96},{32,0},{64,32},{96,64},{1,97},{33,1},{65,33},{97,65},{2,98}... | collective-permute-start | bytes 1572872 | tf_op jit(solution)/shard_map/ppermute | solution.py:32
  213.1 38.7 %collective-permute-start.32 = (bf16[2,512,128]{2,1,0:T(8,128)(2,1)}, bf16[2,512,128]{2,1,0:T(8,128)(2,1)S(1)}, u32[]{:S(2)}, u32[]{:S(2)}) collective-permute-start(bf16[2,512,128]{2,1,0:T(8,128)(2,1)} %slice.36), channel_id=1, source_target_pairs={{0,8},{8,16},{16,24},{24,0},{1,9},{9,17},{17,25},{25,1},{2,10},{10... | collective-permute-start | bytes 786440 | tf_op jit(solution)/shard_map/ppermute | solution.py:32
  213.8 38.0 %collective-permute-start.34 = (bf16[2,512,128]{2,1,0:T(8,128)(2,1)}, bf16[2,512,128]{2,1,0:T(8,128)(2,1)}, u32[]{:S(2)}, u32[]{:S(2)}) collective-permute-start(bf16[2,512,128]{2,1,0:T(8,128)(2,1)} %slice.37), channel_id=1, source_target_pairs={{0,24},{8,0},{16,8},{24,16},{1,25},{9,1},{17,9},{25,17},{2,26},{10... | collective-permute-start | bytes 786440 | tf_op jit(solution)/shard_map/ppermute | solution.py:32
  217.8 34.1 %collective-permute-start.40 = (bf16[2,512,128]{2,1,0:T(8,128)(2,1)}, bf16[2,512,128]{2,1,0:T(8,128)(2,1)}, u32[]{:S(2)}, u32[]{:S(2)}) collective-permute-start(bf16[2,512,128]{2,1,0:T(8,128)(2,1)} %slice.38), channel_id=1, source_target_pairs={{0,32},{32,64},{64,96},{96,0},{1,33},{33,65},{65,97},{97,1},{2,34}... | collective-permute-start | bytes 786440 | tf_op jit(solution)/shard_map/ppermute | solution.py:32
  218.5 33.4 %collective-permute-start.42 = (bf16[2,512,128]{2,1,0:T(8,128)(2,1)}, bf16[2,512,128]{2,1,0:T(8,128)(2,1)}, u32[]{:S(2)}, u32[]{:S(2)}) collective-permute-start(bf16[2,512,128]{2,1,0:T(8,128)(2,1)} %slice.39), channel_id=1, source_target_pairs={{0,96},{32,0},{64,32},{96,64},{1,97},{33,1},{65,33},{97,65},{2,98}... | collective-permute-start | bytes 786440 | tf_op jit(solution)/shard_map/ppermute | solution.py:32
  (12 other events, 107.6 us)
